TPU v7x, 8 devices: a whole 2x2x1 slice. The times are simulated.
8 devices in a mesh: dp: 1 (over z), tp: 2 (over y), cp: 4 (over x, core).
Axes of the slice: x: 2, y: 2, z: 1, core: 2. Of those that a mesh axis runs over, the one named last changes fastest.
Arguments:
- x: bfloat16 [4096, 4096], P(('dp', 'cp'))
- k_cache: bfloat16 [4096, 2, 128], P(('dp', 'cp'), 'tp')
- v_cache: bfloat16 [4096, 2, 128], P(('dp', 'cp'), 'tp')
- rope_table: float32 [4096, 64], P(('dp', 'cp'))
- norm_gain: bfloat16 [4096], replicated
- w_qkv: bfloat16 [4096, 4608], P(None, 'tp')
- b_qkv: bfloat16 [4608], P('tp')
- w_out: bfloat16 [4096, 4096], P('tp')
Outputs:
- output 1: bfloat16 [4096, 4096], P(('dp', 'cp'))
- output 2: bfloat16 [4096, 2, 128], P(('dp', 'cp'), 'tp')
- output 3: bfloat16 [4096, 2, 128], P(('dp', 'cp'), 'tp')
All inputs are finite; a program needn't handle non-finite values.
Results may differ from a plain program's by a relative error of at most 0.004026.
Values are sent between devices in bfloat16 or wider.
A program may use at most 1 GiB of HBM per device.

v0:
```python
import functools
import math

import jax
import jax.numpy as jnp
from jax import lax
from jax.experimental import pallas as pl
from jax.experimental.pallas import tpu as pltpu
from jax.sharding import PartitionSpec as P


EPS = 1.5625e-07
NEG = -1e30
HEAD = 128
SCALE2 = HEAD ** -0.5 * math.log2(math.e)
F32 = jnp.float32
BF = jnp.bfloat16
VMEM_LIMIT = 60 * 2 ** 20
ATTN_VMEM = 24 * 2 ** 20


def rotate(a, cos, sin):
    lane = lax.broadcasted_iota(jnp.int32, a.shape, 1)
    other = jnp.where(lane % 2 == 0, pltpu.roll(a, HEAD - 1, 1), pltpu.roll(a, 1, 1))
    return a * cos + other * sin


def norm_kv_kernel(x_ref, g_ref, w_ref, b_ref, cos_ref, sin_ref, h_ref, k_ref, v_ref):
    for r in range(x_ref.shape[0] // 128):
        rs = pl.ds(r * 128, 128)
        x = x_ref[rs, :].astype(F32)
        inv = lax.rsqrt(jnp.mean(x * x, axis=-1, keepdims=True) + EPS)
        h = (x * inv * g_ref[...].astype(F32)).astype(BF)
        h_ref[rs, :] = h
        a = jnp.dot(h, w_ref[...], preferred_element_type=F32) + b_ref[...].astype(F32)
        k_ref[rs, :] = rotate(a[:, :HEAD], cos_ref[rs, :], sin_ref[rs, :]).astype(BF)
        v_ref[rs, :] = a[:, HEAD:].astype(BF)


def norm_kv(x, g, w_qkv, b, cos, sin, block=256):
    rows, d = x.shape
    last = w_qkv.shape[1] // (2 * HEAD) - 1
    row = lambda i: (i, 0)
    return pl.pallas_call(
        norm_kv_kernel,
        grid=(rows // block,),
        in_specs=[
            pl.BlockSpec((block, d), row),
            pl.BlockSpec((1, d), lambda i: (0, 0)),
            pl.BlockSpec((d, 2 * HEAD), lambda i: (0, last)),
            pl.BlockSpec((1, 2 * HEAD), lambda i: (0, last)),
            pl.BlockSpec((block, HEAD), row),
            pl.BlockSpec((block, HEAD), row),
        ],
        out_specs=[pl.BlockSpec((block, d), row), pl.BlockSpec((block, HEAD), row), pl.BlockSpec((block, HEAD), row)],
        out_shape=[jax.ShapeDtypeStruct((rows, d), BF), jax.ShapeDtypeStruct((rows, HEAD), BF), jax.ShapeDtypeStruct((rows, HEAD), BF)],
        compiler_params=pltpu.CompilerParams(dimension_semantics=("arbitrary",), vmem_limit_bytes=VMEM_LIMIT),
        cost_estimate=pl.CostEstimate(flops=2 * rows * d * 2 * HEAD, bytes_accessed=4 * rows * d, transcendentals=0),
        name="norm_kv",
    )(x, g, w_qkv, b, cos, sin)


def q_kernel(h_ref, w_ref, b_ref, cos_ref, sin_ref, q_ref):
    for r in range(h_ref.shape[0] // 128):
        rs = pl.ds(r * 128, 128)
        a = jnp.dot(h_ref[rs, :], w_ref[...], preferred_element_type=F32) + b_ref[...].astype(F32)
        for i in range(a.shape[1] // HEAD):
            at = slice(i * HEAD, (i + 1) * HEAD)
            q_ref[rs, at] = rotate(a[:, at], cos_ref[rs, :], sin_ref[rs, :]).astype(BF)


def q_proj(h, w_qkv, b, cos, sin, width, block=512):
    rows, d = h.shape
    return pl.pallas_call(
        q_kernel,
        grid=(width // block,),
        in_specs=[
            pl.BlockSpec((rows, d), lambda i: (0, 0)),
            pl.BlockSpec((d, block), lambda i: (0, i)),
            pl.BlockSpec((1, block), lambda i: (0, i)),
            pl.BlockSpec((rows, HEAD), lambda i: (0, 0)),
            pl.BlockSpec((rows, HEAD), lambda i: (0, 0)),
        ],
        out_specs=pl.BlockSpec((rows, block), lambda i: (0, i)),
        out_shape=jax.ShapeDtypeStruct((rows, width), BF),
        compiler_params=pltpu.CompilerParams(dimension_semantics=("arbitrary",), vmem_limit_bytes=VMEM_LIMIT),
        cost_estimate=pl.CostEstimate(flops=2 * rows * d * width, bytes_accessed=2 * d * width, transcendentals=0),
        name="q_proj",
    )(h, w_qkv, b, cos, sin)


HEADS = 16
MOVED = 3


def given(cp):
    return jnp.where(cp == 3, MOVED, jnp.where(cp == 2, 1, 0))


def taken(cp):
    return given(3 - cp)


STRIP = 256
CHUNK = 256


def attn_kernel(cp_ref, q_ref, qn_ref, k_ref, vt_ref, *rest, old, first, foreign):
    back_ref = rest[0] if len(rest) == 9 else None
    o_ref, s_ref, p_ref, acc_ref, mx_ref, m_ref, l_ref, al_ref = rest[-8:]
    slot = pl.program_id(0)
    rows = q_ref.shape[0]
    strips = rows // STRIP
    chunks = rows // CHUNK
    cp = cp_ref[0]
    if foreign:
        owner = jnp.where(slot < taken(cp), 3 - cp, -1)
    else:
        owner = jnp.where(first + slot < HEADS - given(cp), cp, -1)

    def scores(qr, base, u, w):
        k = k_ref[pl.ds(base + u * CHUNK, CHUNK), :]
        return lax.dot_general(k, qr[pl.ds(w * STRIP, STRIP), :], (((1,), (1,)), ((), ())), preferred_element_type=F32)

    def col_max(s):
        return s.reshape(CHUNK // 8, 8, STRIP).max(axis=0)

    def triangle(s):
        key = lax.broadcasted_iota(jnp.int32, s.shape, 0)
        query = lax.broadcasted_iota(jnp.int32, s.shape, 1)
        return jnp.where(key <= query, s, NEG)

    def product(base, u, w):
        at = base // HEAD + u * (CHUNK // HEAD)
        vt = jnp.concatenate([vt_ref[at + i] for i in range(CHUNK // HEAD)], axis=1)
        p = jnp.concatenate([p_ref[w * (STRIP // HEAD) + i, pl.ds(u * CHUNK, CHUNK), :] for i in range(STRIP // HEAD)], axis=1)
        return jnp.dot(vt, p, preferred_element_type=F32)

    def stage(ex=None, pv=None, qk=None, diagonal=False):
        for w in range(strips):
            ne = ex[w] if ex else 0
            np_ = pv[1][w] if pv else 0
            nq = qk[2][w] if qk else 0
            cs = pl.ds(w * STRIP, STRIP)
            total = None
            top = None
            if ne:
                m_old = m_ref[0:1, cs]
                m_new = jnp.maximum(m_old, mx_ref[:, cs].max(axis=0, keepdims=True))
                alpha = jnp.exp2((m_old - m_new) * SCALE2)
                l8 = l_ref[:, cs] * alpha
            for u in range(chunks):
                ks = pl.ds(u * CHUNK, CHUNK)
                if u < np_:
                    x = product(pv[0], u, w)
                    total = x if total is None else total + x
                if u < ne:
                    e = jnp.exp2((s_ref[ks, cs] - m_new) * SCALE2)
                    l8 = l8 + e.reshape(CHUNK // 8, 8, STRIP).sum(axis=0)
                    e = e.astype(BF)
                    for i in range(STRIP // HEAD):
                        p_ref[w * (STRIP // HEAD) + i, ks, :] = e[:, i * HEAD:(i + 1) * HEAD]
                if u < nq:
                    s = scores(qk[0], qk[1], u, w)
                    if diagonal and u == nq - 1:
                        s = triangle(s)
                    s_ref[ks, cs] = s
                    x = col_max(s)
                    top = x if top is None else jnp.maximum(top, x)
            if np_:
                acc_ref[:, cs] = acc_ref[:, cs] * al_ref[0:1, cs] + total
            if ne:
                m_ref[:, cs] = jnp.broadcast_to(m_new, (8, STRIP))
                al_ref[:, cs] = jnp.broadcast_to(alpha, (8, STRIP))
                l_ref[:, cs] = l8
            if nq:
                mx_ref[:, cs] = top

    full = [chunks] * strips
    upper = [w + 1 for w in range(strips)]

    @pl.when((slot == 0) & (owner >= 0))
    def _():
        stage(qk=(q_ref, 0, full))
        p_ref[...] = jnp.zeros_like(p_ref)
        acc_ref[...] = jnp.zeros_like(acc_ref)

    @pl.when(owner >= 0)
    def _():
        own = pl.multiple_of(old + rows * owner, rows)
        m_ref[...] = jnp.full_like(m_ref, NEG)
        l_ref[...] = jnp.zeros_like(l_ref)
        al_ref[...] = jnp.zeros_like(al_ref)

        def body(j, carry):
            before = pl.multiple_of(jnp.maximum(j - 1, 0) * rows, rows)
            after = pl.multiple_of((j + 1) * rows, rows)
            stage(full, (before, full), (q_ref, after, full))
            return carry

        lax.fori_loop(0, own // rows - 1, body, 0)
        stage(full, (pl.multiple_of(own - 2 * rows, rows), full), (q_ref, own, upper), diagonal=True)
        stage(upper, (pl.multiple_of(own - rows, rows), full), (qn_ref, 0, full))
        stage(pv=(own, upper))
        for w in range(strips):
            cs = pl.ds(w * STRIP, STRIP)
            o_ref[cs, :] = (acc_ref[:, cs] / l_ref[:, cs].sum(axis=0, keepdims=True)).astype(BF).T

    if back_ref is not None:
        @pl.when(owner < 0)
        def _():
            o_ref[...] = back_ref[...]


def attention(cp, q, k_all, vt_all, *, slots, first=0, foreign=False, back=None):
    rows = q.shape[0]
    keys = k_all.shape[0]
    old = keys - 4 * rows
    if foreign:
        col = lambda s: slots - 1 - s
    else:
        col = lambda s: s + first
    row_block = lambda index: pl.BlockSpec((rows, HEAD), index)
    operands = [q, q, k_all, vt_all]
    in_specs = [
        row_block(lambda s, c: (0, col(s))),
        row_block(lambda s, c: (0, col(jnp.minimum(s + 1, slots - 1)))),
        pl.BlockSpec((keys, HEAD), lambda s, c: (0, 0)),
        pl.BlockSpec((keys // HEAD, HEAD, HEAD), lambda s, c: (0, 0, 0)),
    ]
    if back is not None:
        skip = slots - MOVED
        operands.append(back)
        in_specs.append(row_block(lambda s, c: (0, jnp.maximum(s - skip, 0))))
    return pl.pallas_call(
        functools.partial(attn_kernel, old=old, first=first, foreign=foreign),
        grid_spec=pltpu.PrefetchScalarGridSpec(
            num_scalar_prefetch=1,
            grid=(slots,),
            in_specs=in_specs,
            out_specs=row_block(lambda s, c: (0, col(s) if foreign else s)),
            scratch_shapes=[
                pltpu.VMEM((rows, rows), F32),
                pltpu.VMEM((rows // HEAD, rows, HEAD), BF),
                pltpu.VMEM((HEAD, rows), F32),
            ]
            + [pltpu.VMEM((8, rows), F32)] * 4,
        ),
        out_shape=jax.ShapeDtypeStruct((rows, slots * HEAD), BF),
        compiler_params=pltpu.CompilerParams(dimension_semantics=("arbitrary",), vmem_limit_bytes=ATTN_VMEM),
        cost_estimate=pl.CostEstimate(flops=4 * rows * slots * HEAD * keys, bytes_accessed=4 * rows * slots * HEAD, transcendentals=0),
        name="attention",
    )(cp, *operands)


def gather_kernel(cp_ref, *refs):
    parts, (k_ref, vt_ref) = refs[:-2], refs[-2:]
    rows = k_ref.shape[0]
    for i, part in enumerate(parts):
        @pl.when(pl.program_id(0) == i)
        def _(part=part):
            k_ref[...] = part[pl.ds(0, rows), :]
            for b in range(rows // HEAD):
                vt_ref[b] = part[pl.ds(rows + b * HEAD, HEAD), :].T


def gather(cp, old, new):
    n = len(old)
    rows = old[0].shape[0] // 2
    place = lambda i, c: (i // n) * n + lax.rem(c[0] + n - lax.rem(i, n), n)
    return pl.pallas_call(
        gather_kernel,
        grid_spec=pltpu.PrefetchScalarGridSpec(
            num_scalar_prefetch=1,
            grid=(2 * n,),
            in_specs=[pl.BlockSpec((2 * rows, HEAD), lambda i, c: (0, 0))] * (2 * n),
            out_specs=[
                pl.BlockSpec((rows, HEAD), lambda i, c: (place(i, c), 0)),
                pl.BlockSpec((rows // HEAD, HEAD, HEAD), lambda i, c: (place(i, c), 0, 0)),
            ],
        ),
        out_shape=[
            jax.ShapeDtypeStruct((2 * n * rows, HEAD), BF),
            jax.ShapeDtypeStruct((2 * n * rows // HEAD, HEAD, HEAD), BF),
        ],
        compiler_params=pltpu.CompilerParams(dimension_semantics=("arbitrary",), vmem_limit_bytes=ATTN_VMEM),
        cost_estimate=pl.CostEstimate(flops=2 ** 20, bytes_accessed=2 ** 23, transcendentals=0),
        name="gather",
    )(cp, *old, *new)


def own_kernel(x_ref, *rest):
    o_refs, w_ref, y_ref = rest[:-2], rest[-2], rest[-1]
    for r in range(x_ref.shape[0] // 256):
        rs = pl.ds(r * 256, 256)
        o = jnp.concatenate([o_ref[rs, :] for o_ref in o_refs], axis=1)
        y_ref[rs, :] = x_ref[rs, :].astype(F32) + jnp.dot(o, w_ref[...], preferred_element_type=F32)


def own_part(x, o_parts, w, block=512):
    rows, d = x.shape
    depth = w.shape[0]
    col = lambda i: (0, i)
    return pl.pallas_call(
        own_kernel,
        grid=(d // block,),
        in_specs=[pl.BlockSpec((rows, block), col)]
        + [pl.BlockSpec(o.shape, lambda i: (0, 0)) for o in o_parts]
        + [pl.BlockSpec((depth, block), col)],
        out_specs=pl.BlockSpec((rows, block), col),
        out_shape=jax.ShapeDtypeStruct((rows, d), F32),
        compiler_params=pltpu.CompilerParams(dimension_semantics=("arbitrary",), vmem_limit_bytes=VMEM_LIMIT),
        cost_estimate=pl.CostEstimate(flops=2 * rows * d * depth, bytes_accessed=6 * rows * d, transcendentals=0),
        name="own_part",
    )(x, *o_parts, w)


def other_kernel(cp_ref, y_ref, *rest, parts):
    o_refs, w_refs, out_ref, o_buf = rest[:parts], rest[parts:-2], rest[-2], rest[-1]

    @pl.when(pl.program_id(0) == 0)
    def _():
        at = 0
        for o_ref in o_refs:
            o_buf[:, pl.ds(at, o_ref.shape[1])] = o_ref[...]
            at += o_ref.shape[1]

    depth = w_refs[0].shape[0]
    halves = len(w_refs) // 4
    for r in range(y_ref.shape[0] // 256):
        rs = pl.ds(r * 256, 256)
        total = None
        for i, w_ref in enumerate(w_refs):
            at = pl.multiple_of(((cp_ref[0] ^ (i // halves)) * halves + i % halves) * depth, depth)
            x = jnp.dot(o_buf[rs, pl.ds(at, depth)], w_ref[...], preferred_element_type=F32)
            total = x if total is None else total + x
        out_ref[rs, :] = (y_ref[rs, :] + total).astype(BF)


def other_part(cp, y, o_parts, w_parts, block=512):
    rows, d = y.shape
    col = lambda i, c: (0, i)
    depth = sum(w.shape[0] for w in w_parts)
    return pl.pallas_call(
        functools.partial(other_kernel, parts=len(o_parts)),
        grid_spec=pltpu.PrefetchScalarGridSpec(
            num_scalar_prefetch=1,
            grid=(d // block,),
            in_specs=[pl.BlockSpec((rows, block), col)]
            + [pl.BlockSpec(o.shape, lambda i, c: (0, 0)) for o in o_parts]
            + [pl.BlockSpec((w.shape[0], block), col) for w in w_parts],
            out_specs=pl.BlockSpec((rows, block), col),
            scratch_shapes=[pltpu.VMEM((rows, depth), BF)],
        ),
        out_shape=jax.ShapeDtypeStruct((rows, d), BF),
        compiler_params=pltpu.CompilerParams(dimension_semantics=("arbitrary",), vmem_limit_bytes=VMEM_LIMIT),
        cost_estimate=pl.CostEstimate(flops=2 * rows * d * depth, bytes_accessed=6 * rows * d, transcendentals=0),
        name="other_part",
    )(cp, y, *o_parts, *w_parts)


def rope_tables(table):
    pairs = table.shape[1] // 2
    pair = jnp.arange(HEAD) // 2
    hot = (jnp.arange(pairs)[:, None] == pair[None, :]).astype(F32)
    sign = jnp.where(jnp.arange(HEAD) % 2 == 0, -1.0, 1.0)
    spread = lambda a, b: jnp.dot(a, b, precision=lax.Precision.HIGHEST, preferred_element_type=F32)
    stay = (pair >= pairs).astype(F32)
    return spread(table[:, :pairs], hot) + stay, spread(table[:, pairs:], hot * sign)


SIZES = (4, 5, 3, 4)
PIECES = 2


def after(a, *others):
    return lax.optimization_barrier((a, *others))[0]


def local_step(x, k_cache, v_cache, rope_table, norm_gain, w_qkv, b_qkv, w_out):
    n = lax.axis_size("cp")
    cp = lax.axis_index("cp")
    swap = [(0, 1), (1, 0)]
    width = w_out.shape[0]
    piece = width // (n * PIECES)
    where = cp.astype(jnp.int32)[None]
    around = lambda s: [(i, (i + s) % n) for i in range(n)]
    flip = lambda bits: [(i, i ^ bits) for i in range(n)]

    kv_cache = jnp.concatenate([k_cache[:, 0], v_cache[:, 0]], axis=0)
    old = [kv_cache] + [lax.ppermute(kv_cache, "cp", around(s)) for s in range(1, n)]
    w_peer = []
    for i in range(PIECES):
        mine = lax.dynamic_slice_in_dim(w_out, (cp * PIECES + i) * piece, piece, 0)
        w_peer.append(lax.ppermute(mine, "tp", swap))

    cos, sin = rope_tables(rope_table)
    bias = b_qkv[None]
    h, new_k, new_v = norm_kv(x, norm_gain[None], w_qkv, bias, cos, sin)
    kv_new = jnp.concatenate([new_k, new_v], axis=0)
    new = [kv_new] + [lax.ppermute(kv_new, "cp", around(s)) for s in range(1, n)]
    queries = q_proj(h, w_qkv, bias, cos, sin, width)
    q_far = lax.ppermute(queries[:, width - MOVED * HEAD:], "cp", [(3, 0), (2, 1)])

    k_all, vt_all = gather(where, old, new)
    attend = functools.partial(attention, where, k_all=k_all, vt_all=vt_all)

    o_own, o_other = [], []

    def heads(i, *previous, back=None):
        q = after(queries, *previous) if previous else queries
        part = attend(q=q, slots=SIZES[i], first=sum(SIZES[:i]), back=back)
        o_own.append(part)
        o_other.append(lax.ppermute(part, "tp", swap))
        return part

    part = heads(0)
    w_peer = [after(w, part) for w in w_peer]
    w_x = [lax.ppermute(w, "cp", flip(2)) for w in w_peer]
    w_core = [lax.ppermute(w, "cp", flip(1)) for w in w_peer]
    far = attend(q=after(q_far, part), slots=MOVED, foreign=True)
    part = heads(1, far)
    back = lax.ppermute(far, "cp", [(0, 3), (1, 2)])
    part = heads(2, part)
    part = heads(3, part, back=back)
    w_x = [after(w, part) for w in w_x]
    w_far = [lax.ppermute(w, "cp", flip(1)) for w in w_x]

    y = own_part(x, o_own, w_out)
    y = other_part(where, y, o_other, [*w_peer, *w_core, *w_x, *w_far])
    return y, new_k[:, None], new_v[:, None]


def solution(mesh):
    row_spec = P(("dp", "cp"), None)
    cache_spec = P(("dp", "cp"), "tp", None)
    return jax.shard_map(
        local_step,
        mesh=mesh,
        in_specs=(row_spec, cache_spec, cache_spec, row_spec, P(None), P(None, "tp"), P("tp"), P("tp", None)),
        out_specs=(row_spec, cache_spec, cache_spec),
        check_vma=False,
    )
```

profile of v0, /device:TPU:0, one launch (start us, length us, event | category | flops | bytes accessed | tf_op | source)
XLA Modules:
  0.0 300.0 jit_solution(5108508203477978476)
XLA Ops:
  1.7 2.8 collective-permute-start.2
  7.9 2.7 convolution_bitcast_fusion.sin_ref
  10.6 2.3 fusion.cos_ref
  12.9 9.9 %norm_kv.1 = (bf16[1024,4096]{1,0:T(8,128)(2,1)}, bf16[1024,128]{1,0:T(8,128)(2,1)}, bf16[1024,128]{1,0:T(8,128)(2,1)}) custom-call(bf16[1024,4096]{1,0:T(8,128)(2,1)} %x_ref.3, bf16[1,4096]{1,0:T(2,128)(2,1)} %broadcast_in_dim.28.g_ref, bf16[4096,2304]{1,0:T(8,128)(2,1)} %w_ref.3, bf16[1,2304]{1,0:T(2,128)(2,1)} %broadcast_in_dim.29.b_ref, ...), custom_call_target="tpu_custom_call" | custom-call | flops 2147483648 | bytes 16777216 | tf_op jit(solution)/shard_map/norm_kv/pallas_call | solution.py:44
  24.8 1.6 collective-permute-start.5
  27.8 24.8 %q_proj.1.q_ref.qn_ref = bf16[1024,2048]{1,0:T(8,128)(2,1)} custom-call(bf16[1024,4096]{1,0:T(8,128)(2,1)} %get-tuple-element.16.h_ref, bf16[4096,2304]{1,0:T(8,128)(2,1)} %w_ref.3, bf16[1,2304]{1,0:T(2,128)(2,1)} %broadcast_in_dim.29.b_ref, f32[1024,128]{1,0:T(8,128)} %fusion.cos_ref, f32[1024,128]{1,0:T(8,128)} %convolution_bitcast_fusion.sin_ref), custom_call_target="tpu_custom_call" | custom-call | flops 17179869184 | bytes 16777216 | tf_op jit(solution)/shard_map/q_proj/pallas_call | solution.py:74
  52.6 2.1 slice.12
  54.7 2.8 constant_dynamic-slice_fusion
  57.5 1.5 collective-permute-start.13
  61.1 2.3 collective-permute-done.3.refs_5_
  63.3 2.6 gather.1
  65.9 24.9 %attention.5.rest_0_ = bf16[1024,512]{1,0:T(8,128)(2,1)S(1)} custom-call(s32[1]{0:T(128)} %bitcast.cp_ref, bf16[1024,2048]{1,0:T(8,128)(2,1)S(1)} %copy-done, bf16[1024,2048]{1,0:T(8,128)(2,1)S(1)} %copy-done, bf16[8192,128]{1,0:T(8,128)(2,1)S(1)} %get-tuple-element.19.k_ref, bf16[64,128,128]{2,1,0:T(8,128)(2,1)S(1)} %get-tuple-element.20.vt_ref), custom_call_target="tpu_custom_call" | custom-call | flops 17179869184 | bytes 2097152 | tf_op jit(solution)/shard_map/attention/pallas_call | solution.py:235
  90.9 1.5 collective-permute-start.8
  92.4 29.1 %attention.6 = bf16[1024,384]{1,0:T(8,128)(2,1)S(1)} custom-call(s32[1]{0:T(128)} %bitcast.cp_ref, bf16[1024,384]{1,0:T(8,128)(2,1)S(1)} %collective-permute-done.6.q_ref.qn_ref, bf16[1024,384]{1,0:T(8,128)(2,1)S(1)} %collective-permute-done.6.q_ref.qn_ref, bf16[8192,128]{1,0:T(8,128)(2,1)S(1)} %get-tuple-element.19.k_ref, ...), custom_call_target="tpu_custom_call" | custom-call | flops 12884901888 | bytes 1572864 | tf_op jit(solution)/shard_map/attention/pallas_call | solution.py:235
  121.5 1.6 collective-permute-start.7
  123.1 31.0 %attention.7.rest_1_ = bf16[1024,640]{1,0:T(8,128)(2,1)S(1)} custom-call(s32[1]{0:T(128)} %bitcast.cp_ref, bf16[1024,2048]{1,0:T(8,128)(2,1)S(1)} %copy-done, bf16[1024,2048]{1,0:T(8,128)(2,1)S(1)} %copy-done, bf16[8192,128]{1,0:T(8,128)(2,1)S(1)} %get-tuple-element.19.k_ref, bf16[64,128,128]{2,1,0:T(8,128)(2,1)S(1)} %get-tuple-element.20.vt_ref), custom_call_target="tpu_custom_call" | custom-call | flops 21474836480 | bytes 2621440 | tf_op jit(solution)/shard_map/attention/pallas_call | solution.py:235
  154.1 2.0 collective-permute-start.17
  156.1 18.9 %attention.8.rest_2_ = bf16[1024,384]{1,0:T(8,128)(2,1)S(1)} custom-call(s32[1]{0:T(128)} %bitcast.cp_ref, bf16[1024,2048]{1,0:T(8,128)(2,1)S(1)} %copy-done, bf16[1024,2048]{1,0:T(8,128)(2,1)S(1)} %copy-done, bf16[8192,128]{1,0:T(8,128)(2,1)S(1)} %get-tuple-element.19.k_ref, bf16[64,128,128]{2,1,0:T(8,128)(2,1)S(1)} %get-tuple-element.20.vt_ref), custom_call_target="tpu_custom_call" | custom-call | flops 12884901888 | bytes 1572864 | tf_op jit(solution)/shard_map/attention/pallas_call | solution.py:235
  175.6 1.5 collective-permute-start.9
  177.1 25.1 %attention.9.rest_3_ = bf16[1024,512]{1,0:T(8,128)(2,1)S(1)} custom-call(s32[1]{0:T(128)} %bitcast.cp_ref, bf16[1024,2048]{1,0:T(8,128)(2,1)S(1)} %copy-done, bf16[1024,2048]{1,0:T(8,128)(2,1)S(1)} %copy-done, bf16[8192,128]{1,0:T(8,128)(2,1)S(1)} %get-tuple-element.19.k_ref, bf16[64,128,128]{2,1,0:T(8,128)(2,1)S(1)} %get-tuple-element.20.vt_ref, ...), custom_call_target="tpu_custom_call" | custom-call | flops 17179869184 | bytes 2097152 | tf_op jit(solution)/shard_map/attention/pallas_call | solution.py:235
  202.8 7.1 %collective-permute-start.14 = (bf16[256,4096]{1,0:T(8,128)(2,1)}, bf16[256,4096]{1,0:T(8,128)(2,1)}, u32[]{:S(2)}, u32[]{:S(2)}) collective-permute-start(bf16[256,4096]{1,0:T(8,128)(2,1)} %collective-permute-done.12.rest_4_), channel_id=1, source_target_pairs={{0,1},{1,0},{2,3},{3,2},{4,5},{5,4},{6,7},{7,6}} | collective-permute-start | bytes 6291464 | tf_op jit(solution)/shard_map/ppermute | solution.py:420
  209.9 37.7 %collective-permute-done.17.rest_9_ = bf16[256,4096]{1,0:T(8,128)(2,1)} collective-permute-done((bf16[256,4096]{1,0:T(8,128)(2,1)}, bf16[256,4096]{1,0:T(8,128)(2,1)}, u32[]{:S(2)}, u32[]{:S(2)}) %collective-permute-start.17) | collective-permute-done | bytes 2097184 | tf_op jit(solution)/shard_map/ppermute | solution.py:419
  250.3 24.5 %own_part.1.y_ref = f32[1024,4096]{1,0:T(8,128)} custom-call(bf16[1024,4096]{1,0:T(8,128)(2,1)} %x_ref.3, bf16[1024,512]{1,0:T(8,128)(2,1)} %copy-done.2, bf16[1024,640]{1,0:T(8,128)(2,1)} %copy-done.1, bf16[1024,384]{1,0:T(8,128)(2,1)} %copy-done.4, bf16[1024,512]{1,0:T(8,128)(2,1)} %copy-done.3, bf16[2048,4096]{1,0:T(8,128)(2,1)} %rest_4_.1), custom_call_target="tpu_custom_call" | custom-call | flops 17179869184 | bytes 25165824 | tf_op jit(solution)/shard_map/own_part/pallas_call | solution.py:304
  275.3 24.7 %other_part.1 = bf16[1024,4096]{1,0:T(8,128)(2,1)} custom-call(s32[1]{0:T(128)} %bitcast.cp_ref, f32[1024,4096]{1,0:T(8,128)} %own_part.1.y_ref, bf16[1024,512]{1,0:T(8,128)(2,1)} %copy-done.8, bf16[1024,640]{1,0:T(8,128)(2,1)} %copy-done.7, bf16[1024,384]{1,0:T(8,128)(2,1)} %copy-done.9, bf16[1024,512]{1,0:T(8,128)(2,1)} %collective-permute-done.11.rest_3_, ...), custom_call_target="tpu_custom_call" | custom-call | flops 17179869184 | bytes 25165824 | tf_op jit(solution)/shard_map/other_part/pallas_call | solution.py:344
  (58 shorter events, 14.1 us)
Async XLA Ops:
  1.7 53.0 %collective-permute-start.2 = (bf16[2048,128]{1,0:T(8,128)(2,1)S(1)}, bf16[2048,128]{1,0:T(8,128)(2,1)S(1)}, u32[]{:S(2)}, u32[]{:S(2)}) collective-permute-start(bf16[2048,128]{1,0:T(8,128)(2,1)S(1)} %pad_maximum_fusion.refs_0_), channel_id=1, source_target_pairs={{0,3},{1,0},{2,1},{3,2},{4,7},{5,4},{6,5},{7,6}} | collective-permute-start | bytes 1572872 | tf_op jit(solution)/shard_map/ppermute | solution.py:391
  4.5 53.1 %collective-permute-start.1 = (bf16[2048,128]{1,0:T(8,128)(2,1)S(1)}, bf16[2048,128]{1,0:T(8,128)(2,1)S(1)}, u32[]{:S(2)}, u32[]{:S(2)}) collective-permute-start(bf16[2048,128]{1,0:T(8,128)(2,1)S(1)} %pad_maximum_fusion.refs_0_), channel_id=1, source_target_pairs={{0,2},{1,3},{2,0},{3,1},{4,6},{5,7},{6,4},{7,5}} | collective-permute-start | bytes 1572872 | tf_op jit(solution)/shard_map/ppermute | solution.py:391
  5.1 54.0 %collective-permute-start = (bf16[2048,128]{1,0:T(8,128)(2,1)S(1)}, bf16[2048,128]{1,0:T(8,128)(2,1)S(1)}, u32[]{:S(2)}, u32[]{:S(2)}) collective-permute-start(bf16[2048,128]{1,0:T(8,128)(2,1)S(1)} %pad_maximum_fusion.refs_0_), channel_id=1, source_target_pairs={{0,1},{1,2},{2,3},{3,0},{4,5},{5,6},{6,7},{7,4}} | collective-permute-start | bytes 1572872 | tf_op jit(solution)/shard_map/ppermute | solution.py:391
  24.8 34.8 %collective-permute-start.5 = (bf16[2048,128]{1,0:T(8,128)(2,1)S(1)}, bf16[2048,128]{1,0:T(8,128)(2,1)S(1)}, u32[]{:S(2)}, u32[]{:S(2)}) collective-permute-start(bf16[2048,128]{1,0:T(8,128)(2,1)S(1)} %constant_dynamic-update-slice_fusion.refs_4_), channel_id=1, source_target_pairs={{0,3},{1,0},{2,1},{3,2},{4,7},{5,4},{6,5},{7,6}} | collective-permute-start | bytes 1572872 | tf_op jit(solution)/shard_map/ppermute | solution.py:401
  26.3 34.7 %collective-permute-start.4 = (bf16[2048,128]{1,0:T(8,128)(2,1)S(1)}, bf16[2048,128]{1,0:T(8,128)(2,1)}, u32[]{:S(2)}, u32[]{:S(2)}) collective-permute-start(bf16[2048,128]{1,0:T(8,128)(2,1)S(1)} %constant_dynamic-update-slice_fusion.refs_4_), channel_id=1, source_target_pairs={{0,2},{1,3},{2,0},{3,1},{4,6},{5,7},{6,4},{7,5}} | collective-permute-start | bytes 1572872 | tf_op jit(solution)/shard_map/ppermute | solution.py:401
  54.7 8.6 %collective-permute-start.3 = (bf16[2048,128]{1,0:T(8,128)(2,1)S(1)}, bf16[2048,128]{1,0:T(8,128)(2,1)S(1)}, u32[]{:S(2)}, u32[]{:S(2)}) collective-permute-start(bf16[2048,128]{1,0:T(8,128)(2,1)S(1)} %constant_dynamic-update-slice_fusion.refs_4_), channel_id=1, source_target_pairs={{0,1},{1,2},{2,3},{3,0},{4,5},{5,6},{6,7},{7,4}} | collective-permute-start | bytes 1572872 | tf_op jit(solution)/shard_map/ppermute | solution.py:401
  57.5 96.5 %collective-permute-start.13 = (bf16[256,4096]{1,0:T(8,128)(2,1)S(1)}, bf16[256,4096]{1,0:T(8,128)(2,1)}, u32[]{:S(2)}, u32[]{:S(2)}) collective-permute-start(bf16[256,4096]{1,0:T(8,128)(2,1)S(1)} %get-tuple-element.29), channel_id=1, source_target_pairs={{0,4},{4,0},{1,5},{5,1},{2,6},{6,2},{3,7},{7,3}} | collective-permute-start | bytes 6291464 | tf_op jit(solution)/shard_map/ppermute | solution.py:395
  59.1 95.0 %collective-permute-start.12 = (bf16[256,4096]{1,0:T(8,128)(2,1)S(1)}, bf16[256,4096]{1,0:T(8,128)(2,1)}, u32[]{:S(2)}, u32[]{:S(2)}) collective-permute-start(bf16[256,4096]{1,0:T(8,128)(2,1)S(1)} %get-tuple-element.30), channel_id=1, source_target_pairs={{0,4},{4,0},{1,5},{5,1},{2,6},{6,2},{3,7},{7,3}} | collective-permute-start | bytes 6291464 | tf_op jit(solution)/shard_map/ppermute | solution.py:395
  59.6 32.8 %collective-permute-start.6 = (bf16[1024,384]{1,0:T(8,128)(2,1)S(1)}, bf16[1024,384]{1,0:T(8,128)(2,1)S(1)}, u32[]{:S(2)}, u32[]{:S(2)}) collective-permute-start(bf16[1024,384]{1,0:T(8,128)(2,1)S(1)} %copy-done.5), channel_id=1, source_target_pairs={{3,0},{2,1},{7,4},{6,5}} | collective-permute-start | bytes 2359304 | tf_op jit(solution)/shard_map/ppermute | solution.py:403
  90.9 30.6 %copy-start.2 = (bf16[1024,512]{1,0:T(8,128)(2,1)}, bf16[1024,512]{1,0:T(8,128)(2,1)S(1)}, u32[]{:S(2)}) copy-start(bf16[1024,512]{1,0:T(8,128)(2,1)S(1)} %attention.5.rest_0_) | copy-start | bytes 3145732
  90.9 156.7 %collective-permute-start.8 = (bf16[1024,512]{1,0:T(8,128)(2,1)S(1)}, bf16[1024,512]{1,0:T(8,128)(2,1)S(1)}, u32[]{:S(2)}, u32[]{:S(2)}) collective-permute-start(bf16[1024,512]{1,0:T(8,128)(2,1)S(1)} %attention.5.rest_0_), channel_id=1, source_target_pairs={{0,4},{4,0},{1,5},{5,1},{2,6},{6,2},{3,7},{7,3}} | collective-permute-start | bytes 3145736 | tf_op jit(solution)/shard_map/ppermute | solution.py:414
  121.5 54.1 %collective-permute-start.7 = (bf16[1024,384]{1,0:T(8,128)(2,1)S(1)}, bf16[1024,384]{1,0:T(8,128)(2,1)S(1)}, u32[]{:S(2)}, u32[]{:S(2)}) collective-permute-start(bf16[1024,384]{1,0:T(8,128)(2,1)S(1)} %attention.6), channel_id=1, source_target_pairs={{0,3},{1,2},{4,7},{5,6}} | collective-permute-start | bytes 2359304 | tf_op jit(solution)/shard_map/ppermute | solution.py:423
  154.1 48.7 %collective-permute-start.16 = (bf16[256,4096]{1,0:T(8,128)(2,1)}, bf16[256,4096]{1,0:T(8,128)(2,1)S(1)}, u32[]{:S(2)}, u32[]{:S(2)}) collective-permute-start(bf16[256,4096]{1,0:T(8,128)(2,1)} %collective-permute-done.12.rest_4_), channel_id=1, source_target_pairs={{0,2},{1,3},{2,0},{3,1},{4,6},{5,7},{6,4},{7,5}} | collective-permute-start | bytes 6291464 | tf_op jit(solution)/shard_map/ppermute | solution.py:419
  154.1 93.4 %collective-permute-start.17 = (bf16[256,4096]{1,0:T(8,128)(2,1)}, bf16[256,4096]{1,0:T(8,128)(2,1)}, u32[]{:S(2)}, u32[]{:S(2)}) collective-permute-start(bf16[256,4096]{1,0:T(8,128)(2,1)} %collective-permute-done.13.rest_5_), channel_id=1, source_target_pairs={{0,2},{1,3},{2,0},{3,1},{4,6},{5,7},{6,4},{7,5}} | collective-permute-start | bytes 6291464 | tf_op jit(solution)/shard_map/ppermute | solution.py:419
  175.1 27.2 %copy-start.4 = (bf16[1024,384]{1,0:T(8,128)(2,1)}, bf16[1024,384]{1,0:T(8,128)(2,1)S(1)}, u32[]{:S(2)}) copy-start(bf16[1024,384]{1,0:T(8,128)(2,1)S(1)} %attention.8.rest_2_) | copy-start | bytes 2359300
  175.1 73.0 %collective-permute-start.10 = (bf16[1024,384]{1,0:T(8,128)(2,1)S(1)}, bf16[1024,384]{1,0:T(8,128)(2,1)S(1)}, u32[]{:S(2)}, u32[]{:S(2)}) collective-permute-start(bf16[1024,384]{1,0:T(8,128)(2,1)S(1)} %attention.8.rest_2_), channel_id=1, source_target_pairs={{0,4},{4,0},{1,5},{5,1},{2,6},{6,2},{3,7},{7,3}} | collective-permute-start | bytes 2359304 | tf_op jit(solution)/shard_map/ppermute | solution.py:414
  175.6 72.5 %collective-permute-start.9 = (bf16[1024,640]{1,0:T(8,128)(2,1)S(1)}, bf16[1024,640]{1,0:T(8,128)(2,1)S(1)}, u32[]{:S(2)}, u32[]{:S(2)}) collective-permute-start(bf16[1024,640]{1,0:T(8,128)(2,1)S(1)} %attention.7.rest_1_), channel_id=1, source_target_pairs={{0,4},{4,0},{1,5},{5,1},{2,6},{6,2},{3,7},{7,3}} | collective-permute-start | bytes 3932168 | tf_op jit(solution)/shard_map/ppermute | solution.py:414
  202.3 48.0 %copy-start.3 = (bf16[1024,512]{1,0:T(8,128)(2,1)}, bf16[1024,512]{1,0:T(8,128)(2,1)S(1)}, u32[]{:S(2)}) copy-start(bf16[1024,512]{1,0:T(8,128)(2,1)S(1)} %attention.9.rest_3_) | copy-start | bytes 3145732
  202.8 71.9 %copy-start.6 = (bf16[256,4096]{1,0:T(8,128)(2,1)}, bf16[256,4096]{1,0:T(8,128)(2,1)S(1)}, u32[]{:S(2)}) copy-start(bf16[256,4096]{1,0:T(8,128)(2,1)S(1)} %collective-permute-done.16.rest_8_) | copy-start | bytes 6291460
  202.8 72.4 %collective-permute-start.14 = (bf16[256,4096]{1,0:T(8,128)(2,1)}, bf16[256,4096]{1,0:T(8,128)(2,1)}, u32[]{:S(2)}, u32[]{:S(2)}) collective-permute-start(bf16[256,4096]{1,0:T(8,128)(2,1)} %collective-permute-done.12.rest_4_), channel_id=1, source_target_pairs={{0,1},{1,0},{2,3},{3,2},{4,5},{5,4},{6,7},{7,6}} | collective-permute-start | bytes 6291464 | tf_op jit(solution)/shard_map/ppermute | solution.py:420
  247.5 27.7 %collective-permute-start.15 = (bf16[256,4096]{1,0:T(8,128)(2,1)}, bf16[256,4096]{1,0:T(8,128)(2,1)}, u32[]{:S(2)}, u32[]{:S(2)}) collective-permute-start(bf16[256,4096]{1,0:T(8,128)(2,1)} %collective-permute-done.13.rest_5_), channel_id=1, source_target_pairs={{0,1},{1,0},{2,3},{3,2},{4,5},{5,4},{6,7},{7,6}} | collective-permute-start | bytes 6291464 | tf_op jit(solution)/shard_map/ppermute | solution.py:420
  247.6 27.7 %collective-permute-start.18 = (bf16[256,4096]{1,0:T(8,128)(2,1)S(1)}, bf16[256,4096]{1,0:T(8,128)(2,1)}, u32[]{:S(2)}, u32[]{:S(2)}) collective-permute-start(bf16[256,4096]{1,0:T(8,128)(2,1)S(1)} %collective-permute-done.16.rest_8_), channel_id=1, source_target_pairs={{0,1},{1,0},{2,3},{3,2},{4,5},{5,4},{6,7},{7,6}} | collective-permute-start | bytes 6291464 | tf_op jit(solution)/shard_map/ppermute | solution.py:427
  248.1 27.2 %collective-permute-start.19 = (bf16[256,4096]{1,0:T(8,128)(2,1)}, bf16[256,4096]{1,0:T(8,128)(2,1)}, u32[]{:S(2)}, u32[]{:S(2)}) collective-permute-start(bf16[256,4096]{1,0:T(8,128)(2,1)} %collective-permute-done.17.rest_9_), channel_id=1, source_target_pairs={{0,1},{1,0},{2,3},{3,2},{4,5},{5,4},{6,7},{7,6}} | collective-permute-start | bytes 6291464 | tf_op jit(solution)/shard_map/ppermute | solution.py:427
  249.6 25.7 %collective-permute-start.11 = (bf16[1024,512]{1,0:T(8,128)(2,1)S(1)}, bf16[1024,512]{1,0:T(8,128)(2,1)}, u32[]{:S(2)}, u32[]{:S(2)}) collective-permute-start(bf16[1024,512]{1,0:T(8,128)(2,1)S(1)} %attention.9.rest_3_), channel_id=1, source_target_pairs={{0,4},{4,0},{1,5},{5,1},{2,6},{6,2},{3,7},{7,3}} | collective-permute-start | bytes 3145736 | tf_op jit(solution)/shard_map/ppermute | solution.py:414
  (6 other events, 57.7 us)
where the time goes:
time: 300 us
  Pallas kernels  216 us (72%)
  waiting for transfers between devices  41 us (14%)
  starting transfers between devices  25.6 us (9%)
  local copies, waits for them, and re-layouts  10.9 us (4%)
  matrix products  5.02 us (2%)
    pallas_call x5, Pallas kernels, attention(): pl.pallas_call(functools.partial(attn_kernel, old=old, first=first, forei...  129 us
    ppermute x2, waiting for transfers between devices, local_step(): w_x = [lax.ppermute(w, 'cp', flip(2)) for w in w_peer]  38.2 us
    pallas_call x1, Pallas kernels, q_proj(): pl.pallas_call(q_kernel, grid=(width // block,), in_specs=[pl.BlockSpec((...  24.8 us
    pallas_call x1, Pallas kernels, other_part(): pl.pallas_call(functools.partial(other_kernel, parts=len(o_parts)), grid_...  24.7 us
    pallas_call x1, Pallas kernels, own_part(): pl.pallas_call(own_kernel, grid=(d // block,), in_specs=[pl.BlockSpec((ro...  24.5 us
    pallas_call x1, Pallas kernels, norm_kv(): pl.pallas_call(norm_kv_kernel, grid=(rows // block,), in_specs=[pl.BlockS...  9.93 us
    ppermute x2, starting transfers between devices, local_step(): w_core = [lax.ppermute(w, 'cp', flip(1)) for w in w_peer]  7.08 us
  transfers between devices with their start and end apart: 20, of which 4 were waited for; matrix products, arithmetic and copies ran while one was open for 5% of the time, Pallas kernels for 64%

commit v1 on v0

--- a/solution.py
+++ b/solution.py
@@ -17,6 +17,8 @@
 BF = jnp.bfloat16
 VMEM_LIMIT = 60 * 2 ** 20
 ATTN_VMEM = 24 * 2 ** 20
+NORM_VMEM = 28 * 2 ** 20
+Q_VMEM = 36 * 2 ** 20
 
 
 def rotate(a, cos, sin):
@@ -25,52 +27,94 @@
     return a * cos + other * sin
 
 
-def norm_kv_kernel(x_ref, g_ref, w_ref, b_ref, cos_ref, sin_ref, h_ref, k_ref, v_ref):
+def norm_kv_kernel(cp_ref, x_ref, g_ref, w_ref, b_ref, table_ref, piece_ref, h_ref, kv_ref, k_ref, v_ref, cos_ref, sin_ref, copy_ref):
+    copy_ref[...] = piece_ref[...]
+    pairs = table_ref.shape[1] // 2
+    lane = lax.broadcasted_iota(jnp.int32, (pairs, HEAD), 1)
+    hit = lax.broadcasted_iota(jnp.int32, (pairs, HEAD), 0) == lane // 2
+    spread = functools.partial(jnp.dot, precision=lax.Precision.HIGHEST, preferred_element_type=F32)
+    stay = lax.broadcasted_iota(jnp.int32, (128, HEAD), 1) >= 2 * pairs
     for r in range(x_ref.shape[0] // 128):
         rs = pl.ds(r * 128, 128)
+        table = table_ref[rs, :]
+        cos = jnp.where(stay, 1.0, spread(table[:, :pairs], hit.astype(F32)))
+        sin = spread(table[:, pairs:], jnp.where(hit, jnp.where(lane % 2 == 0, -1.0, 1.0), 0.0))
+        cos_ref[rs, :] = cos
+        sin_ref[rs, :] = sin
         x = x_ref[rs, :].astype(F32)
         inv = lax.rsqrt(jnp.mean(x * x, axis=-1, keepdims=True) + EPS)
         h = (x * inv * g_ref[...].astype(F32)).astype(BF)
         h_ref[rs, :] = h
         a = jnp.dot(h, w_ref[...], preferred_element_type=F32) + b_ref[...].astype(F32)
-        k_ref[rs, :] = rotate(a[:, :HEAD], cos_ref[rs, :], sin_ref[rs, :]).astype(BF)
-        v_ref[rs, :] = a[:, HEAD:].astype(BF)
-
-
-def norm_kv(x, g, w_qkv, b, cos, sin, block=256):
+        k = rotate(a[:, :HEAD], cos, sin).astype(BF)
+        v = a[:, HEAD:].astype(BF)
+        k_ref[rs, :] = k
+        v_ref[rs, :] = v
+        kv_ref[0, rs, :] = k
+        kv_ref[1, rs, :] = v
+
+
+def norm_kv(cp, x, g, w_qkv, b, table, w_out, piece, block=256):
     rows, d = x.shape
+    steps = rows // block
     last = w_qkv.shape[1] // (2 * HEAD) - 1
-    row = lambda i: (i, 0)
+    row = lambda i, c: (i, 0)
+    part = piece // steps
+    head_rows = pl.BlockSpec((block, HEAD), row)
     return pl.pallas_call(
         norm_kv_kernel,
-        grid=(rows // block,),
-        in_specs=[
-            pl.BlockSpec((block, d), row),
-            pl.BlockSpec((1, d), lambda i: (0, 0)),
-            pl.BlockSpec((d, 2 * HEAD), lambda i: (0, last)),
-            pl.BlockSpec((1, 2 * HEAD), lambda i: (0, last)),
-            pl.BlockSpec((block, HEAD), row),
-            pl.BlockSpec((block, HEAD), row),
+        grid_spec=pltpu.PrefetchScalarGridSpec(
+            num_scalar_prefetch=1,
+            grid=(steps,),
+            in_specs=[
+                pl.BlockSpec((block, d), row),
+                pl.BlockSpec((1, d), lambda i, c: (0, 0)),
+                pl.BlockSpec((d, 2 * HEAD), lambda i, c: (0, last)),
+                pl.BlockSpec((1, 2 * HEAD), lambda i, c: (0, last)),
+                pl.BlockSpec((block, table.shape[1]), row),
+                pl.BlockSpec((part, w_out.shape[1]), lambda i, c: ((c[0] * PIECES + 1) * steps + i, 0)),
+            ],
+            out_specs=[
+                pl.BlockSpec((block, d), row),
+                pl.BlockSpec((2, block, HEAD), lambda i, c: (0, i, 0)),
+                head_rows,
+                head_rows,
+                head_rows,
+                head_rows,
+                pl.BlockSpec((part, w_out.shape[1]), row),
+            ],
+        ),
+        out_shape=[
+            jax.ShapeDtypeStruct((rows, d), BF),
+            jax.ShapeDtypeStruct((2, rows, HEAD), BF),
+            jax.ShapeDtypeStruct((rows, HEAD), BF),
+            jax.ShapeDtypeStruct((rows, HEAD), BF),
+            jax.ShapeDtypeStruct((rows, HEAD), F32),
+            jax.ShapeDtypeStruct((rows, HEAD), F32),
+            jax.ShapeDtypeStruct((piece, w_out.shape[1]), BF),
         ],
-        out_specs=[pl.BlockSpec((block, d), row), pl.BlockSpec((block, HEAD), row), pl.BlockSpec((block, HEAD), row)],
-        out_shape=[jax.ShapeDtypeStruct((rows, d), BF), jax.ShapeDtypeStruct((rows, HEAD), BF), jax.ShapeDtypeStruct((rows, HEAD), BF)],
-        compiler_params=pltpu.CompilerParams(dimension_semantics=("arbitrary",), vmem_limit_bytes=VMEM_LIMIT),
+        compiler_params=pltpu.CompilerParams(dimension_semantics=("arbitrary",), vmem_limit_bytes=NORM_VMEM),
         cost_estimate=pl.CostEstimate(flops=2 * rows * d * 2 * HEAD, bytes_accessed=4 * rows * d, transcendentals=0),
         name="norm_kv",
-    )(x, g, w_qkv, b, cos, sin)
-
-
-def q_kernel(h_ref, w_ref, b_ref, cos_ref, sin_ref, q_ref):
+    )(cp, x, g, w_qkv, b, table, w_out)
+
+
+def q_kernel(h_ref, w_ref, b_ref, cos_ref, sin_ref, q_ref, far_ref):
+    lead = far_ref.shape[1] - w_ref.shape[1]
     for r in range(h_ref.shape[0] // 128):
         rs = pl.ds(r * 128, 128)
         a = jnp.dot(h_ref[rs, :], w_ref[...], preferred_element_type=F32) + b_ref[...].astype(F32)
         for i in range(a.shape[1] // HEAD):
             at = slice(i * HEAD, (i + 1) * HEAD)
-            q_ref[rs, at] = rotate(a[:, at], cos_ref[rs, :], sin_ref[rs, :]).astype(BF)
+            q = rotate(a[:, at], cos_ref[rs, :], sin_ref[rs, :]).astype(BF)
+            q_ref[rs, at] = q
+            if i * HEAD + lead >= 0:
+                far_ref[rs, pl.ds(i * HEAD + lead, HEAD)] = q
 
 
 def q_proj(h, w_qkv, b, cos, sin, width, block=512):
     rows, d = h.shape
+    far = MOVED * HEAD
     return pl.pallas_call(
         q_kernel,
         grid=(width // block,),
@@ -81,9 +125,9 @@
             pl.BlockSpec((rows, HEAD), lambda i: (0, 0)),
             pl.BlockSpec((rows, HEAD), lambda i: (0, 0)),
         ],
-        out_specs=pl.BlockSpec((rows, block), lambda i: (0, i)),
-        out_shape=jax.ShapeDtypeStruct((rows, width), BF),
-        compiler_params=pltpu.CompilerParams(dimension_semantics=("arbitrary",), vmem_limit_bytes=VMEM_LIMIT),
+        out_specs=[pl.BlockSpec((rows, block), lambda i: (0, i)), pl.BlockSpec((rows, far), lambda i: (0, 0))],
+        out_shape=[jax.ShapeDtypeStruct((rows, width), BF), jax.ShapeDtypeStruct((rows, far), BF)],
+        compiler_params=pltpu.CompilerParams(dimension_semantics=("arbitrary",), vmem_limit_bytes=Q_VMEM),
         cost_estimate=pl.CostEstimate(flops=2 * rows * d * width, bytes_accessed=2 * d * width, transcendentals=0),
         name="q_proj",
     )(h, w_qkv, b, cos, sin)
@@ -359,16 +403,6 @@
     )(cp, y, *o_parts, *w_parts)
 
 
-def rope_tables(table):
-    pairs = table.shape[1] // 2
-    pair = jnp.arange(HEAD) // 2
-    hot = (jnp.arange(pairs)[:, None] == pair[None, :]).astype(F32)
-    sign = jnp.where(jnp.arange(HEAD) % 2 == 0, -1.0, 1.0)
-    spread = lambda a, b: jnp.dot(a, b, precision=lax.Precision.HIGHEST, preferred_element_type=F32)
-    stay = (pair >= pairs).astype(F32)
-    return spread(table[:, :pairs], hot) + stay, spread(table[:, pairs:], hot * sign)
-
-
 SIZES = (4, 5, 3, 4)
 PIECES = 2
 
@@ -378,6 +412,7 @@
 
 
 def local_step(x, k_cache, v_cache, rope_table, norm_gain, w_qkv, b_qkv, w_out):
+    rows = x.shape[0]
     n = lax.axis_size("cp")
     cp = lax.axis_index("cp")
     swap = [(0, 1), (1, 0)]
@@ -389,18 +424,17 @@
 
     kv_cache = jnp.concatenate([k_cache[:, 0], v_cache[:, 0]], axis=0)
     old = [kv_cache] + [lax.ppermute(kv_cache, "cp", around(s)) for s in range(1, n)]
-    w_peer = []
-    for i in range(PIECES):
-        mine = lax.dynamic_slice_in_dim(w_out, (cp * PIECES + i) * piece, piece, 0)
-        w_peer.append(lax.ppermute(mine, "tp", swap))
-
-    cos, sin = rope_tables(rope_table)
+    mine = lax.dynamic_slice_in_dim(w_out, cp * PIECES * piece, piece, 0)
+    w_peer = [lax.ppermute(mine, "tp", swap)]
+
     bias = b_qkv[None]
-    h, new_k, new_v = norm_kv(x, norm_gain[None], w_qkv, bias, cos, sin)
-    kv_new = jnp.concatenate([new_k, new_v], axis=0)
+    h, kv_new, new_k, new_v, cos, sin, mine = norm_kv(where, x, norm_gain[None], w_qkv, bias, rope_table, w_out, piece)
+    w_peer.append(lax.ppermute(mine, "tp", swap))
+    kv_new = kv_new.reshape(2 * rows, HEAD)
     new = [kv_new] + [lax.ppermute(kv_new, "cp", around(s)) for s in range(1, n)]
-    queries = q_proj(h, w_qkv, bias, cos, sin, width)
-    q_far = lax.ppermute(queries[:, width - MOVED * HEAD:], "cp", [(3, 0), (2, 1)])
+    queries, q_far = q_proj(h, w_qkv, bias, cos, sin, width)
+    q_far = lax.ppermute(q_far, "cp", [(3, 0), (2, 1)])
+    w_peer[0] = after(w_peer[0], queries)
 
     k_all, vt_all = gather(where, old, new)
     attend = functools.partial(attention, where, k_all=k_all, vt_all=vt_all)
@@ -414,17 +448,28 @@
         o_other.append(lax.ppermute(part, "tp", swap))
         return part
 
+    w_x, w_core, w_far = [None] * PIECES, [None] * PIECES, [None] * PIECES
+
+    def spread(i):
+        w_x[i] = lax.ppermute(w_peer[i], "cp", flip(2))
+        w_core[i] = lax.ppermute(w_peer[i], "cp", flip(1))
+
+    def spread_on(i):
+        w_far[i] = lax.ppermute(w_x[i], "cp", flip(1))
+
+    spread(0)
     part = heads(0)
-    w_peer = [after(w, part) for w in w_peer]
-    w_x = [lax.ppermute(w, "cp", flip(2)) for w in w_peer]
-    w_core = [lax.ppermute(w, "cp", flip(1)) for w in w_peer]
     far = attend(q=after(q_far, part), slots=MOVED, foreign=True)
+    back = lax.ppermute(far, "cp", [(0, 3), (1, 2)])
     part = heads(1, far)
-    back = lax.ppermute(far, "cp", [(0, 3), (1, 2)])
+    w_peer[1] = after(w_peer[1], part)
+    w_x[0] = after(w_x[0], part)
+    spread(1)
+    spread_on(0)
     part = heads(2, part)
     part = heads(3, part, back=back)
-    w_x = [after(w, part) for w in w_x]
-    w_far = [lax.ppermute(w, "cp", flip(1)) for w in w_x]
+    w_x[1] = after(w_x[1], part)
+    spread_on(1)
 
     y = own_part(x, o_own, w_out)
     y = other_part(where, y, o_other, [*w_peer, *w_core, *w_x, *w_far])

time: 300 us -> 293 us (0.977)
  waiting for transfers between devices: 41 us -> 34.4 us
  matrix products: 5.02 us -> 0 us
  Pallas kernels: 216 us -> 212 us
  local copies, waits for them, and re-layouts: 10.9 us -> 14.9 us
  starting transfers between devices: 25.6 us -> 29.3 us
    unnamed x21 -> x31, local copies, waits for them, and re-layouts: 2.46 us -> 11.6 us
    ppermute x7 -> x8, starting transfers between devices: 11.1 us -> 16.6 us  [the longest x2 11.1 us: spread(): w_core[i] = lax.ppermute(w_peer[i], 'cp', flip(1))]
    dot_general x2 -> x0, matrix products: 5.02 us -> none  [rope_tables(): jnp.dot(a, b, precision=lax.Precision.HIGHEST, preferred_element_type=F32)]
    ppermute x7 -> x8, waiting for transfers between devices: 38.2 us -> 34.3 us  [the longest x2 34.3 us: spread(): w_x[i] = lax.ppermute(w_peer[i], 'cp', flip(2))]
  transfers between devices with their start and end apart: 20 -> 20, of which waited for: 4 -> 1; matrix products, arithmetic and copies ran while one was open for 5% -> 2% of each run, Pallas kernels for 64% -> 64%
where the time goes in v1:
time: 293 us
  Pallas kernels  212 us (72%)
  waiting for transfers between devices  34.4 us (12%)
  starting transfers between devices  29.3 us (10%)
  local copies, waits for them, and re-layouts  14.9 us (5%)
    pallas_call x5, Pallas kernels, attention(): pl.pallas_call(functools.partial(attn_kernel, old=old, first=first, forei...  129 us
    ppermute x2, waiting for transfers between devices, spread(): w_x[i] = lax.ppermute(w_peer[i], 'cp', flip(2))  34.3 us
    pallas_call x1, Pallas kernels, other_part(): pl.pallas_call(functools.partial(other_kernel, parts=len(o_parts)), grid_...  24.7 us
    pallas_call x1, Pallas kernels, own_part(): pl.pallas_call(own_kernel, grid=(d // block,), in_specs=[pl.BlockSpec((ro...  24.4 us
    pallas_call x1, Pallas kernels, q_proj(): pl.pallas_call(q_kernel, grid=(width // block,), in_specs=[pl.BlockSpec((...  22.7 us
    unnamed x31, local copies, waits for them, and re-layouts  11.6 us
    ppermute x2, starting transfers between devices, spread(): w_core[i] = lax.ppermute(w_peer[i], 'cp', flip(1))  11.1 us
    pallas_call x1, Pallas kernels, norm_kv(): pl.pallas_call(norm_kv_kernel, grid_spec=pltpu.PrefetchScalarGridSpec(num...  8.79 us
  transfers between devices with their start and end apart: 20, of which 1 were waited for; matrix products, arithmetic and copies ran while one was open for 2% of the time, Pallas kernels for 64%

profile of v1, /device:TPU:0, one launch (start us, length us, event | category | flops | bytes accessed | tf_op | source)
XLA Modules:
  0.0 293.0 jit_solution(10144031788778902242)
XLA Ops:
  1.7 2.8 collective-permute-start.2
  7.8 3.4 %copy-done = bf16[1024,4096]{1,0:T(8,128)(2,1)S(1)} copy-done((bf16[1024,4096]{1,0:T(8,128)(2,1)S(1)}, bf16[1024,4096]{1,0:T(8,128)(2,1)}, u32[]{:S(2)}) %copy-start) | copy-done | bytes 8388632
  11.2 8.8 %norm_kv.1 = (bf16[1024,4096]{1,0:T(8,128)(2,1)S(1)}, bf16[2,1024,128]{2,1,0:T(8,128)(2,1)S(1)}, bf16[1024,128]{1,0:T(8,128)(2,1)}, bf16[1024,128]{1,0:T(8,128)(...) custom-call(s32[1]{0:T(128)} %bitcast.cp_ref, ...), custom_call_target="tpu_custom_call" | custom-call | flops 2147483648 | bytes 16777216 | tf_op jit(solution)/shard_map/norm_kv/pallas_call | solution.py:64
  20.0 1.4 copy-done.1
  21.4 1.6 collective-permute-start.5
  22.9 1.4 collective-permute-start.4
  24.3 22.7 %q_proj.1 = (bf16[1024,2048]{1,0:T(8,128)(2,1)S(1)}, bf16[1024,384]{1,0:T(8,128)(2,1)S(1)}) custom-call(bf16[1024,4096]{1,0:T(8,128)(2,1)S(1)} %get-tuple-element.22.h_ref, bf16[4096,2304]{1,0:T(8,128)(2,1)} %w_ref.3, bf16[1,2304]{1,0:T(2,128)(2,1)S(1)} %broadcast_in_dim.17.b_ref, f32[1024,128]{1,0:T(8,128)S(1)} %get-tuple-element.23.cos_ref, ...), custom_call_target="tpu_custom_call" | custom-call | flops 17179869184 | bytes 16777216 | tf_op jit(solution)/shard_map/q_proj/pallas_call | solution.py:118
  47.9 2.0 copy-done.9
  50.0 1.9 constant_dynamic-slice_fusion
  51.9 1.5 collective-permute-start.12
  53.5 1.5 collective-permute-start.6
  55.5 2.9 gather.1
  58.4 24.9 %attention.5.rest_0_ = bf16[1024,512]{1,0:T(8,128)(2,1)S(1)} custom-call(s32[1]{0:T(128)} %bitcast.cp_ref, bf16[1024,2048]{1,0:T(8,128)(2,1)S(1)} %copy-done.10, bf16[1024,2048]{1,0:T(8,128)(2,1)S(1)} %copy-done.10, bf16[8192,128]{1,0:T(8,128)(2,1)S(1)} %get-tuple-element.27.k_ref, bf16[64,128,128]{2,1,0:T(8,128)(2,1)S(1)} %get-tuple-element.28.vt_ref), custom_call_target="tpu_custom_call" | custom-call | flops 17179869184 | bytes 2097152 | tf_op jit(solution)/shard_map/attention/pallas_call | solution.py:279
  84.6 29.1 %attention.6 = bf16[1024,384]{1,0:T(8,128)(2,1)S(1)} custom-call(s32[1]{0:T(128)} %bitcast.cp_ref, bf16[1024,384]{1,0:T(8,128)(2,1)S(1)} %collective-permute-done.6.q_ref.qn_ref, bf16[1024,384]{1,0:T(8,128)(2,1)S(1)} %collective-permute-done.6.q_ref.qn_ref, bf16[8192,128]{1,0:T(8,128)(2,1)S(1)} %get-tuple-element.27.k_ref, ...), custom_call_target="tpu_custom_call" | custom-call | flops 12884901888 | bytes 1572864 | tf_op jit(solution)/shard_map/attention/pallas_call | solution.py:279
  113.7 1.6 collective-permute-start.7
  115.2 31.0 %attention.7.rest_1_ = bf16[1024,640]{1,0:T(8,128)(2,1)S(1)} custom-call(s32[1]{0:T(128)} %bitcast.cp_ref, bf16[1024,2048]{1,0:T(8,128)(2,1)S(1)} %copy-done.10, bf16[1024,2048]{1,0:T(8,128)(2,1)S(1)} %copy-done.10, bf16[8192,128]{1,0:T(8,128)(2,1)S(1)} %get-tuple-element.27.k_ref, bf16[64,128,128]{2,1,0:T(8,128)(2,1)S(1)} %get-tuple-element.28.vt_ref), custom_call_target="tpu_custom_call" | custom-call | flops 21474836480 | bytes 2621440 | tf_op jit(solution)/shard_map/attention/pallas_call | solution.py:279
  146.3 2.0 collective-permute-start.17
  148.3 18.9 %attention.8.rest_2_ = bf16[1024,384]{1,0:T(8,128)(2,1)S(1)} custom-call(s32[1]{0:T(128)} %bitcast.cp_ref, bf16[1024,2048]{1,0:T(8,128)(2,1)S(1)} %copy-done.10, bf16[1024,2048]{1,0:T(8,128)(2,1)S(1)} %copy-done.10, bf16[8192,128]{1,0:T(8,128)(2,1)S(1)} %get-tuple-element.27.k_ref, bf16[64,128,128]{2,1,0:T(8,128)(2,1)S(1)} %get-tuple-element.28.vt_ref), custom_call_target="tpu_custom_call" | custom-call | flops 12884901888 | bytes 1572864 | tf_op jit(solution)/shard_map/attention/pallas_call | solution.py:279
  169.3 25.1 %attention.9.rest_3_ = bf16[1024,512]{1,0:T(8,128)(2,1)S(1)} custom-call(s32[1]{0:T(128)} %bitcast.cp_ref, bf16[1024,2048]{1,0:T(8,128)(2,1)S(1)} %copy-done.10, bf16[1024,2048]{1,0:T(8,128)(2,1)S(1)} %copy-done.10, bf16[8192,128]{1,0:T(8,128)(2,1)S(1)} %get-tuple-element.27.k_ref, bf16[64,128,128]{2,1,0:T(8,128)(2,1)S(1)} %get-tuple-element.28.vt_ref, ...), custom_call_target="tpu_custom_call" | custom-call | flops 17179869184 | bytes 2097152 | tf_op jit(solution)/shard_map/attention/pallas_call | solution.py:279
  194.5 9.6 %collective-permute-start.14 = (bf16[256,4096]{1,0:T(8,128)(2,1)}, bf16[256,4096]{1,0:T(8,128)(2,1)}, u32[]{:S(2)}, u32[]{:S(2)}) collective-permute-start(bf16[256,4096]{1,0:T(8,128)(2,1)} %collective-permute-done.12.rest_4_), channel_id=1, source_target_pairs={{0,1},{1,0},{2,3},{3,2},{4,5},{5,4},{6,7},{7,6}} | collective-permute-start | bytes 6291464 | tf_op jit(solution)/shard_map/ppermute | solution.py:455
  204.1 34.3 %collective-permute-done.17.rest_9_ = bf16[256,4096]{1,0:T(8,128)(2,1)} collective-permute-done((bf16[256,4096]{1,0:T(8,128)(2,1)}, bf16[256,4096]{1,0:T(8,128)(2,1)}, u32[]{:S(2)}, u32[]{:S(2)}) %collective-permute-start.17) | collective-permute-done | bytes 2097184 | tf_op jit(solution)/shard_map/ppermute | solution.py:454
  238.3 1.5 collective-permute-start.15
  242.9 24.4 %own_part.1.y_ref = f32[1024,4096]{1,0:T(8,128)} custom-call(bf16[1024,4096]{1,0:T(8,128)(2,1)} %x_ref.3, bf16[1024,512]{1,0:T(8,128)(2,1)} %copy-done.4, bf16[1024,640]{1,0:T(8,128)(2,1)} %copy-done.3, bf16[1024,384]{1,0:T(8,128)(2,1)} %copy-done.8, bf16[1024,512]{1,0:T(8,128)(2,1)} %copy-done.5, bf16[2048,4096]{1,0:T(8,128)(2,1)} %rest_4_.1), custom_call_target="tpu_custom_call" | custom-call | flops 17179869184 | bytes 25165824 | tf_op jit(solution)/shard_map/own_part/pallas_call | solution.py:348
  268.4 24.7 %other_part.1 = bf16[1024,4096]{1,0:T(8,128)(2,1)} custom-call(s32[1]{0:T(128)} %bitcast.cp_ref, f32[1024,4096]{1,0:T(8,128)} %own_part.1.y_ref, bf16[1024,512]{1,0:T(8,128)(2,1)} %copy-done.12, bf16[1024,640]{1,0:T(8,128)(2,1)} %copy-done.11, bf16[1024,384]{1,0:T(8,128)(2,1)} %copy-done.14, bf16[1024,512]{1,0:T(8,128)(2,1)} %copy-done.13, ...), custom_call_target="tpu_custom_call" | custom-call | flops 17179869184 | bytes 25165824 | tf_op jit(solution)/shard_map/other_part/pallas_call | solution.py:388
  (61 shorter events, 13.3 us)
Async XLA Ops:
  1.7 22.6 %collective-permute-start.2 = (bf16[2048,128]{1,0:T(8,128)(2,1)S(1)}, bf16[2048,128]{1,0:T(8,128)(2,1)S(1)}, u32[]{:S(2)}, u32[]{:S(2)}) collective-permute-start(bf16[2048,128]{1,0:T(8,128)(2,1)S(1)} %pad_maximum_fusion.refs_0_), channel_id=1, source_target_pairs={{0,3},{1,0},{2,1},{3,2},{4,7},{5,4},{6,5},{7,6}} | collective-permute-start | bytes 1572872 | tf_op jit(solution)/shard_map/ppermute | solution.py:426
  4.5 47.4 %collective-permute-start.1 = (bf16[2048,128]{1,0:T(8,128)(2,1)S(1)}, bf16[2048,128]{1,0:T(8,128)(2,1)S(1)}, u32[]{:S(2)}, u32[]{:S(2)}) collective-permute-start(bf16[2048,128]{1,0:T(8,128)(2,1)S(1)} %pad_maximum_fusion.refs_0_), channel_id=1, source_target_pairs={{0,2},{1,3},{2,0},{3,1},{4,6},{5,7},{6,4},{7,5}} | collective-permute-start | bytes 1572872 | tf_op jit(solution)/shard_map/ppermute | solution.py:426
  5.1 48.4 %collective-permute-start = (bf16[2048,128]{1,0:T(8,128)(2,1)S(1)}, bf16[2048,128]{1,0:T(8,128)(2,1)S(1)}, u32[]{:S(2)}, u32[]{:S(2)}) collective-permute-start(bf16[2048,128]{1,0:T(8,128)(2,1)S(1)} %pad_maximum_fusion.refs_0_), channel_id=1, source_target_pairs={{0,1},{1,2},{2,3},{3,0},{4,5},{5,6},{6,7},{7,4}} | collective-permute-start | bytes 1572872 | tf_op jit(solution)/shard_map/ppermute | solution.py:426
  21.4 33.6 %collective-permute-start.5 = (bf16[2048,128]{1,0:T(8,128)(2,1)S(1)}, bf16[2048,128]{1,0:T(8,128)(2,1)S(1)}, u32[]{:S(2)}, u32[]{:S(2)}) collective-permute-start(bf16[2048,128]{1,0:T(8,128)(2,1)S(1)} %bitcast.6), channel_id=1, source_target_pairs={{0,3},{1,0},{2,1},{3,2},{4,7},{5,4},{6,5},{7,6}} | collective-permute-start | bytes 1572872 | tf_op jit(solution)/shard_map/ppermute | solution.py:434
  22.9 32.6 %collective-permute-start.4 = (bf16[2048,128]{1,0:T(8,128)(2,1)S(1)}, bf16[2048,128]{1,0:T(8,128)(2,1)}, u32[]{:S(2)}, u32[]{:S(2)}) collective-permute-start(bf16[2048,128]{1,0:T(8,128)(2,1)S(1)} %bitcast.7), channel_id=1, source_target_pairs={{0,2},{1,3},{2,0},{3,1},{4,6},{5,7},{6,4},{7,5}} | collective-permute-start | bytes 1572872 | tf_op jit(solution)/shard_map/ppermute | solution.py:434
  24.3 31.2 %collective-permute-start.3 = (bf16[2048,128]{1,0:T(8,128)(2,1)S(1)}, bf16[2048,128]{1,0:T(8,128)(2,1)}, u32[]{:S(2)}, u32[]{:S(2)}) collective-permute-start(bf16[2048,128]{1,0:T(8,128)(2,1)S(1)} %bitcast.8), channel_id=1, source_target_pairs={{0,1},{1,2},{2,3},{3,0},{4,5},{5,6},{6,7},{7,4}} | collective-permute-start | bytes 1572872 | tf_op jit(solution)/shard_map/ppermute | solution.py:434
  51.9 94.3 %collective-permute-start.12 = (bf16[256,4096]{1,0:T(8,128)(2,1)S(1)}, bf16[256,4096]{1,0:T(8,128)(2,1)}, u32[]{:S(2)}, u32[]{:S(2)}) collective-permute-start(bf16[256,4096]{1,0:T(8,128)(2,1)S(1)} %constant_dynamic-slice_fusion), channel_id=1, source_target_pairs={{0,4},{4,0},{1,5},{5,1},{2,6},{6,2},{3,7},{7,3}} | collective-permute-start | bytes 6291464 | tf_op jit(solution)/shard_map/ppermute | solution.py:428
  53.5 31.1 %collective-permute-start.6 = (bf16[1024,384]{1,0:T(8,128)(2,1)S(1)}, bf16[1024,384]{1,0:T(8,128)(2,1)S(1)}, u32[]{:S(2)}, u32[]{:S(2)}) collective-permute-start(bf16[1024,384]{1,0:T(8,128)(2,1)S(1)} %copy-done.7), channel_id=1, source_target_pairs={{3,0},{2,1},{7,4},{6,5}} | collective-permute-start | bytes 2359304 | tf_op jit(solution)/shard_map/ppermute | solution.py:436
  55.0 91.3 %collective-permute-start.13 = (bf16[256,4096]{1,0:T(8,128)(2,1)S(1)}, bf16[256,4096]{1,0:T(8,128)(2,1)}, u32[]{:S(2)}, u32[]{:S(2)}) collective-permute-start(bf16[256,4096]{1,0:T(8,128)(2,1)S(1)} %copy-done.2), channel_id=1, source_target_pairs={{0,4},{4,0},{1,5},{5,1},{2,6},{6,2},{3,7},{7,3}} | collective-permute-start | bytes 6291464 | tf_op jit(solution)/shard_map/ppermute | solution.py:432
  83.3 30.3 %copy-start.4 = (bf16[1024,512]{1,0:T(8,128)(2,1)}, bf16[1024,512]{1,0:T(8,128)(2,1)S(1)}, u32[]{:S(2)}) copy-start(bf16[1024,512]{1,0:T(8,128)(2,1)S(1)} %attention.5.rest_0_) | copy-start | bytes 3145732
  83.3 156.5 %collective-permute-start.8 = (bf16[1024,512]{1,0:T(8,128)(2,1)S(1)}, bf16[1024,512]{1,0:T(8,128)(2,1)S(1)}, u32[]{:S(2)}, u32[]{:S(2)}) collective-permute-start(bf16[1024,512]{1,0:T(8,128)(2,1)S(1)} %attention.5.rest_0_), channel_id=1, source_target_pairs={{0,4},{4,0},{1,5},{5,1},{2,6},{6,2},{3,7},{7,3}} | collective-permute-start | bytes 3145736 | tf_op jit(solution)/shard_map/ppermute | solution.py:448
  113.7 54.4 %collective-permute-start.7 = (bf16[1024,384]{1,0:T(8,128)(2,1)S(1)}, bf16[1024,384]{1,0:T(8,128)(2,1)S(1)}, u32[]{:S(2)}, u32[]{:S(2)}) collective-permute-start(bf16[1024,384]{1,0:T(8,128)(2,1)S(1)} %attention.6), channel_id=1, source_target_pairs={{0,3},{1,2},{4,7},{5,6}} | collective-permute-start | bytes 2359304 | tf_op jit(solution)/shard_map/ppermute | solution.py:463
  146.2 21.8 %copy-start.3 = (bf16[1024,640]{1,0:T(8,128)(2,1)}, bf16[1024,640]{1,0:T(8,128)(2,1)S(1)}, u32[]{:S(2)}) copy-start(bf16[1024,640]{1,0:T(8,128)(2,1)S(1)} %attention.7.rest_1_) | copy-start | bytes 3932164
  146.2 48.2 %collective-permute-start.16 = (bf16[256,4096]{1,0:T(8,128)(2,1)}, bf16[256,4096]{1,0:T(8,128)(2,1)}, u32[]{:S(2)}, u32[]{:S(2)}) collective-permute-start(bf16[256,4096]{1,0:T(8,128)(2,1)} %collective-permute-done.12.rest_4_), channel_id=1, source_target_pairs={{0,2},{1,3},{2,0},{3,1},{4,6},{5,7},{6,4},{7,5}} | collective-permute-start | bytes 6291464 | tf_op jit(solution)/shard_map/ppermute | solution.py:454
  146.3 92.1 %collective-permute-start.17 = (bf16[256,4096]{1,0:T(8,128)(2,1)}, bf16[256,4096]{1,0:T(8,128)(2,1)}, u32[]{:S(2)}, u32[]{:S(2)}) collective-permute-start(bf16[256,4096]{1,0:T(8,128)(2,1)} %collective-permute-done.13.rest_5_), channel_id=1, source_target_pairs={{0,2},{1,3},{2,0},{3,1},{4,6},{5,7},{6,4},{7,5}} | collective-permute-start | bytes 6291464 | tf_op jit(solution)/shard_map/ppermute | solution.py:454
  167.3 27.2 %copy-start.8 = (bf16[1024,384]{1,0:T(8,128)(2,1)}, bf16[1024,384]{1,0:T(8,128)(2,1)S(1)}, u32[]{:S(2)}) copy-start(bf16[1024,384]{1,0:T(8,128)(2,1)S(1)} %attention.8.rest_2_) | copy-start | bytes 2359300
  167.3 72.6 %collective-permute-start.10 = (bf16[1024,384]{1,0:T(8,128)(2,1)S(1)}, bf16[1024,384]{1,0:T(8,128)(2,1)S(1)}, u32[]{:S(2)}, u32[]{:S(2)}) collective-permute-start(bf16[1024,384]{1,0:T(8,128)(2,1)S(1)} %attention.8.rest_2_), channel_id=1, source_target_pairs={{0,4},{4,0},{1,5},{5,1},{2,6},{6,2},{3,7},{7,3}} | collective-permute-start | bytes 2359304 | tf_op jit(solution)/shard_map/ppermute | solution.py:448
  168.1 72.3 %collective-permute-start.9 = (bf16[1024,640]{1,0:T(8,128)(2,1)S(1)}, bf16[1024,640]{1,0:T(8,128)(2,1)S(1)}, u32[]{:S(2)}, u32[]{:S(2)}) collective-permute-start(bf16[1024,640]{1,0:T(8,128)(2,1)S(1)} %attention.7.rest_1_), channel_id=1, source_target_pairs={{0,4},{4,0},{1,5},{5,1},{2,6},{6,2},{3,7},{7,3}} | collective-permute-start | bytes 3932168 | tf_op jit(solution)/shard_map/ppermute | solution.py:448
  194.5 48.5 %copy-start.5 = (bf16[1024,512]{1,0:T(8,128)(2,1)}, bf16[1024,512]{1,0:T(8,128)(2,1)S(1)}, u32[]{:S(2)}) copy-start(bf16[1024,512]{1,0:T(8,128)(2,1)S(1)} %attention.9.rest_3_) | copy-start | bytes 3145732
  194.5 72.9 %collective-permute-start.14 = (bf16[256,4096]{1,0:T(8,128)(2,1)}, bf16[256,4096]{1,0:T(8,128)(2,1)}, u32[]{:S(2)}, u32[]{:S(2)}) collective-permute-start(bf16[256,4096]{1,0:T(8,128)(2,1)} %collective-permute-done.12.rest_4_), channel_id=1, source_target_pairs={{0,1},{1,0},{2,3},{3,2},{4,5},{5,4},{6,7},{7,6}} | collective-permute-start | bytes 6291464 | tf_op jit(solution)/shard_map/ppermute | solution.py:455
  238.3 29.0 %collective-permute-start.15 = (bf16[256,4096]{1,0:T(8,128)(2,1)}, bf16[256,4096]{1,0:T(8,128)(2,1)}, u32[]{:S(2)}, u32[]{:S(2)}) collective-permute-start(bf16[256,4096]{1,0:T(8,128)(2,1)} %collective-permute-done.13.rest_5_), channel_id=1, source_target_pairs={{0,1},{1,0},{2,3},{3,2},{4,5},{5,4},{6,7},{7,6}} | collective-permute-start | bytes 6291464 | tf_op jit(solution)/shard_map/ppermute | solution.py:455
  239.9 27.5 %collective-permute-start.18 = (bf16[256,4096]{1,0:T(8,128)(2,1)}, bf16[256,4096]{1,0:T(8,128)(2,1)}, u32[]{:S(2)}, u32[]{:S(2)}) collective-permute-start(bf16[256,4096]{1,0:T(8,128)(2,1)} %collective-permute-done.16.rest_8_), channel_id=1, source_target_pairs={{0,1},{1,0},{2,3},{3,2},{4,5},{5,4},{6,7},{7,6}} | collective-permute-start | bytes 6291464 | tf_op jit(solution)/shard_map/ppermute | solution.py:458
  239.9 27.5 %collective-permute-start.19 = (bf16[256,4096]{1,0:T(8,128)(2,1)}, bf16[256,4096]{1,0:T(8,128)(2,1)}, u32[]{:S(2)}, u32[]{:S(2)}) collective-permute-start(bf16[256,4096]{1,0:T(8,128)(2,1)} %collective-permute-done.17.rest_9_), channel_id=1, source_target_pairs={{0,1},{1,0},{2,3},{3,2},{4,5},{5,4},{6,7},{7,6}} | collective-permute-start | bytes 6291464 | tf_op jit(solution)/shard_map/ppermute | solution.py:458
  242.2 25.2 %collective-permute-start.11 = (bf16[1024,512]{1,0:T(8,128)(2,1)S(1)}, bf16[1024,512]{1,0:T(8,128)(2,1)S(1)}, u32[]{:S(2)}, u32[]{:S(2)}) collective-permute-start(bf16[1024,512]{1,0:T(8,128)(2,1)S(1)} %attention.9.rest_3_), channel_id=1, source_target_pairs={{0,4},{4,0},{1,5},{5,1},{2,6},{6,2},{3,7},{7,3}} | collective-permute-start | bytes 3145736 | tf_op jit(solution)/shard_map/ppermute | solution.py:448
  (11 other events, 23.8 us)

commit v2 on v1

--- a/solution.py
+++ b/solution.py
@@ -15,10 +15,10 @@
 SCALE2 = HEAD ** -0.5 * math.log2(math.e)
 F32 = jnp.float32
 BF = jnp.bfloat16
-VMEM_LIMIT = 60 * 2 ** 20
 ATTN_VMEM = 24 * 2 ** 20
-NORM_VMEM = 28 * 2 ** 20
+NORM_VMEM = 48 * 2 ** 20
 Q_VMEM = 36 * 2 ** 20
+OUT_VMEM = 28 * 2 ** 20
 
 
 def rotate(a, cos, sin):
@@ -150,7 +150,7 @@
 
 
 def attn_kernel(cp_ref, q_ref, qn_ref, k_ref, vt_ref, *rest, old, first, foreign):
-    back_ref = rest[0] if len(rest) == 9 else None
+    back_refs = rest[:-8]
     o_ref, s_ref, p_ref, acc_ref, mx_ref, m_ref, l_ref, al_ref = rest[-8:]
     slot = pl.program_id(0)
     rows = q_ref.shape[0]
@@ -158,7 +158,7 @@
     chunks = rows // CHUNK
     cp = cp_ref[0]
     if foreign:
-        owner = jnp.where(slot < taken(cp), 3 - cp, -1)
+        owner = jnp.where(first + slot < taken(cp), 3 - cp, -1)
     else:
         owner = jnp.where(first + slot < HEADS - given(cp), cp, -1)
 
@@ -225,8 +225,24 @@
 
     @pl.when((slot == 0) & (owner >= 0))
     def _():
-        stage(qk=(q_ref, 0, full))
-        p_ref[...] = jnp.zeros_like(p_ref)
+        def strip(w, carry):
+            cs = pl.ds(pl.multiple_of(w * STRIP, STRIP), STRIP)
+            top = None
+            for u in range(chunks):
+                ks = pl.ds(u * CHUNK, CHUNK)
+                s = lax.dot_general(k_ref[ks, :], q_ref[cs, :], (((1,), (1,)), ((), ())), preferred_element_type=F32)
+                s_ref[ks, cs] = s
+                top = col_max(s) if top is None else jnp.maximum(top, col_max(s))
+            mx_ref[:, cs] = top
+            return carry
+
+        lax.fori_loop(0, strips, strip, 0)
+
+        def clear(i, carry):
+            p_ref[i] = jnp.zeros_like(p_ref[0])
+            return carry
+
+        lax.fori_loop(0, rows // HEAD, clear, 0)
         acc_ref[...] = jnp.zeros_like(acc_ref)
 
     @pl.when(owner >= 0)
@@ -250,18 +266,18 @@
             cs = pl.ds(w * STRIP, STRIP)
             o_ref[cs, :] = (acc_ref[:, cs] / l_ref[:, cs].sum(axis=0, keepdims=True)).astype(BF).T
 
-    if back_ref is not None:
-        @pl.when(owner < 0)
-        def _():
+    for i, back_ref in enumerate(back_refs):
+        @pl.when((owner < 0) & ((slot == pl.num_programs(0) - 1) == (i == 0)))
+        def _(back_ref=back_ref):
             o_ref[...] = back_ref[...]
 
 
-def attention(cp, q, k_all, vt_all, *, slots, first=0, foreign=False, back=None):
+def attention(cp, q, k_all, vt_all, *, slots, first=0, foreign=False, back=()):
     rows = q.shape[0]
     keys = k_all.shape[0]
     old = keys - 4 * rows
     if foreign:
-        col = lambda s: slots - 1 - s
+        col = lambda s: MOVED - 1 - first - s
     else:
         col = lambda s: s + first
     row_block = lambda index: pl.BlockSpec((rows, HEAD), index)
@@ -272,17 +288,16 @@
         pl.BlockSpec((keys, HEAD), lambda s, c: (0, 0)),
         pl.BlockSpec((keys // HEAD, HEAD, HEAD), lambda s, c: (0, 0, 0)),
     ]
-    if back is not None:
-        skip = slots - MOVED
-        operands.append(back)
-        in_specs.append(row_block(lambda s, c: (0, jnp.maximum(s - skip, 0))))
+    for i, part in enumerate(back):
+        operands.append(part)
+        in_specs.append(row_block((lambda s, c: (0, 0)) if i == 0 else (lambda s, c: (0, jnp.clip(s - (slots - MOVED), 0, MOVED - 2)))))
     return pl.pallas_call(
         functools.partial(attn_kernel, old=old, first=first, foreign=foreign),
         grid_spec=pltpu.PrefetchScalarGridSpec(
             num_scalar_prefetch=1,
             grid=(slots,),
             in_specs=in_specs,
-            out_specs=row_block(lambda s, c: (0, col(s) if foreign else s)),
+            out_specs=row_block(lambda s, c: (0, slots - 1 - s if foreign else s)),
             scratch_shapes=[
                 pltpu.VMEM((rows, rows), F32),
                 pltpu.VMEM((rows // HEAD, rows, HEAD), BF),
@@ -311,7 +326,7 @@
 def gather(cp, old, new):
     n = len(old)
     rows = old[0].shape[0] // 2
-    place = lambda i, c: (i // n) * n + lax.rem(c[0] + n - lax.rem(i, n), n)
+    place = lambda i, c: jnp.where(i < n, c[0] ^ i, n + lax.rem(c[0] + 2 * n - i, n))
     return pl.pallas_call(
         gather_kernel,
         grid_spec=pltpu.PrefetchScalarGridSpec(
@@ -353,7 +368,7 @@
         + [pl.BlockSpec((depth, block), col)],
         out_specs=pl.BlockSpec((rows, block), col),
         out_shape=jax.ShapeDtypeStruct((rows, d), F32),
-        compiler_params=pltpu.CompilerParams(dimension_semantics=("arbitrary",), vmem_limit_bytes=VMEM_LIMIT),
+        compiler_params=pltpu.CompilerParams(dimension_semantics=("arbitrary",), vmem_limit_bytes=OUT_VMEM),
         cost_estimate=pl.CostEstimate(flops=2 * rows * d * depth, bytes_accessed=6 * rows * d, transcendentals=0),
         name="own_part",
     )(x, *o_parts, w)
@@ -397,7 +412,7 @@
             scratch_shapes=[pltpu.VMEM((rows, depth), BF)],
         ),
         out_shape=jax.ShapeDtypeStruct((rows, d), BF),
-        compiler_params=pltpu.CompilerParams(dimension_semantics=("arbitrary",), vmem_limit_bytes=VMEM_LIMIT),
+        compiler_params=pltpu.CompilerParams(dimension_semantics=("arbitrary",), vmem_limit_bytes=OUT_VMEM),
         cost_estimate=pl.CostEstimate(flops=2 * rows * d * depth, bytes_accessed=6 * rows * d, transcendentals=0),
         name="other_part",
     )(cp, y, *o_parts, *w_parts)
@@ -423,13 +438,14 @@
     flip = lambda bits: [(i, i ^ bits) for i in range(n)]
 
     kv_cache = jnp.concatenate([k_cache[:, 0], v_cache[:, 0]], axis=0)
-    old = [kv_cache] + [lax.ppermute(kv_cache, "cp", around(s)) for s in range(1, n)]
+    old = [kv_cache, lax.ppermute(kv_cache, "cp", flip(1)), lax.ppermute(kv_cache, "cp", flip(2))]
     mine = lax.dynamic_slice_in_dim(w_out, cp * PIECES * piece, piece, 0)
     w_peer = [lax.ppermute(mine, "tp", swap)]
 
     bias = b_qkv[None]
     h, kv_new, new_k, new_v, cos, sin, mine = norm_kv(where, x, norm_gain[None], w_qkv, bias, rope_table, w_out, piece)
     w_peer.append(lax.ppermute(mine, "tp", swap))
+    old.append(lax.ppermute(after(old[2], kv_new), "cp", flip(1)))
     kv_new = kv_new.reshape(2 * rows, HEAD)
     new = [kv_new] + [lax.ppermute(kv_new, "cp", around(s)) for s in range(1, n)]
     queries, q_far = q_proj(h, w_qkv, bias, cos, sin, width)
@@ -441,7 +457,7 @@
 
     o_own, o_other = [], []
 
-    def heads(i, *previous, back=None):
+    def heads(i, *previous, back=()):
         q = after(queries, *previous) if previous else queries
         part = attend(q=q, slots=SIZES[i], first=sum(SIZES[:i]), back=back)
         o_own.append(part)
@@ -457,18 +473,21 @@
     def spread_on(i):
         w_far[i] = lax.ppermute(w_x[i], "cp", flip(1))
 
+    def moved(first, slots, *previous):
+        far = attend(q=after(q_far, *previous), slots=slots, first=first, foreign=True)
+        return far, lax.ppermute(far, "cp", [(0, 3), (1, 2)])
+
     spread(0)
     part = heads(0)
-    far = attend(q=after(q_far, part), slots=MOVED, foreign=True)
-    back = lax.ppermute(far, "cp", [(0, 3), (1, 2)])
+    far, back0 = moved(0, 1, part)
+    w_peer[1] = after(w_peer[1], far)
+    spread(1)
     part = heads(1, far)
-    w_peer[1] = after(w_peer[1], part)
-    w_x[0] = after(w_x[0], part)
-    spread(1)
+    far, back1 = moved(1, MOVED - 1, part)
+    part = heads(2, far)
+    part = heads(3, part, back=(back0, back1))
+    w_x = [after(w, part) for w in w_x]
     spread_on(0)
-    part = heads(2, part)
-    part = heads(3, part, back=back)
-    w_x[1] = after(w_x[1], part)
     spread_on(1)
 
     y = own_part(x, o_own, w_out)

time: 293 us -> 301 us (1.027)
  waiting for transfers between devices: 34.4 us -> 44.4 us
  starting transfers between devices: 29.3 us -> 24.8 us
    ppermute x2, starting transfers between devices: 11.1 us -> 0.01 us  [spread(): w_core[i] = lax.ppermute(w_peer[i], 'cp', flip(1))]
    ppermute x2, waiting for transfers between devices: 34.3 us -> 42.9 us  [spread(): w_x[i] = lax.ppermute(w_peer[i], 'cp', flip(2))]
    ppermute x4 -> x5, starting transfers between devices: 5.12 us -> 12.6 us  [the longest x2 9.07 us: moved(): return (far, lax.ppermute(far, 'cp', [(0, 3), (1, 2)]))]
    pallas_call x5 -> x6, Pallas kernels: 129 us -> 133 us  [attention(): pl.pallas_call(functools.partial(attn_kernel, old=old, first=first, forei...]
    unnamed x31 -> x37, local copies, waits for them, and re-layouts: 11.6 us -> 12.2 us
  transfers between devices with their start and end apart: 20 -> 21, of which waited for: 1 -> 3; matrix products, arithmetic and copies ran while one was open for 2% -> 1% of each run, Pallas kernels for 64% -> 64%
where the time goes in v2:
time: 301 us; the launch traced here: 300 us
  Pallas kernels  214 us (71%)
  waiting for transfers between devices  44.4 us (15%)
  starting transfers between devices  24.8 us (8%)
  local copies, waits for them, and re-layouts  15.5 us (5%)
    pallas_call x6, Pallas kernels, attention(): pl.pallas_call(functools.partial(attn_kernel, old=old, first=first, forei...  133 us
    ppermute x2, waiting for transfers between devices, spread(): w_x[i] = lax.ppermute(w_peer[i], 'cp', flip(2))  42.9 us
    pallas_call x1, Pallas kernels, other_part(): pl.pallas_call(functools.partial(other_kernel, parts=len(o_parts)), grid_...  23 us
    pallas_call x1, Pallas kernels, own_part(): pl.pallas_call(own_kernel, grid=(d // block,), in_specs=[pl.BlockSpec((ro...  22.4 us
    pallas_call x1, Pallas kernels, q_proj(): pl.pallas_call(q_kernel, grid=(width // block,), in_specs=[pl.BlockSpec((...  21.3 us
    unnamed x37, local copies, waits for them, and re-layouts  12.2 us
    pallas_call x1, Pallas kernels, norm_kv(): pl.pallas_call(norm_kv_kernel, grid_spec=pltpu.PrefetchScalarGridSpec(num...  10.9 us
    ppermute x2, starting transfers between devices, moved(): return (far, lax.ppermute(far, 'cp', [(0, 3), (1, 2)]))  9.07 us
  transfers between devices with their start and end apart: 21, of which 3 were waited for; matrix products, arithmetic and copies ran while one was open for 1% of the time, Pallas kernels for 64%

profile of v2, /device:TPU:0, one launch (start us, length us, event | category | flops | bytes accessed | tf_op | source)
XLA Modules:
  0.0 300.4 jit_solution(17823409057465644320)
XLA Ops:
  1.7 3.3 %collective-permute-start.1 = (bf16[2048,128]{1,0:T(8,128)(2,1)S(1)}, bf16[2048,128]{1,0:T(8,128)(2,1)S(1)}, u32[]{:S(2)}, u32[]{:S(2)}) collective-permute-start(bf16[2048,128]{1,0:T(8,128)(2,1)S(1)} %pad_maximum_fusion.refs_0_), channel_id=1, source_target_pairs={{0,2},{1,3},{2,0},{3,1},{4,6},{5,7},{6,4},{7,5}} | collective-permute-start | bytes 1572872 | tf_op jit(solution)/shard_map/ppermute | solution.py:441
  7.6 10.9 %norm_kv.1 = (bf16[1024,4096]{1,0:T(8,128)(2,1)}, bf16[2,1024,128]{2,1,0:T(8,128)(2,1)S(1)}, bf16[1024,128]{1,0:T(8,128)(2,1)}, bf16[1024,128]{1,0:T(8,128)(2,1)...) custom-call(s32[1]{0:T(128)} %bitcast.cp_ref, bf16[1024,4096]{1,0:T(8,128)(2,1)} %x_ref.3, ...), custom_call_target="tpu_custom_call" | custom-call | flops 2147483648 | bytes 16777216 | tf_op jit(solution)/shard_map/norm_kv/pallas_call | solution.py:64
  20.0 2.0 collective-permute-start.4
  22.2 3.4 %copy-done = bf16[1024,4096]{1,0:T(8,128)(2,1)S(1)} copy-done((bf16[1024,4096]{1,0:T(8,128)(2,1)S(1)}, bf16[1024,4096]{1,0:T(8,128)(2,1)}, u32[]{:S(2)}) %copy-start) | copy-done | bytes 8388632
  25.6 21.3 %q_proj.1 = (bf16[1024,2048]{1,0:T(8,128)(2,1)S(1)}, bf16[1024,384]{1,0:T(8,128)(2,1)S(1)}) custom-call(bf16[1024,4096]{1,0:T(8,128)(2,1)S(1)} %copy-done, bf16[4096,2304]{1,0:T(8,128)(2,1)} %w_ref.3, bf16[1,2304]{1,0:T(2,128)(2,1)S(1)} %broadcast_in_dim.17.b_ref, f32[1024,128]{1,0:T(8,128)S(1)} %get-tuple-element.25.cos_ref, ...), custom_call_target="tpu_custom_call" | custom-call | flops 17179869184 | bytes 16777216 | tf_op jit(solution)/shard_map/q_proj/pallas_call | solution.py:118
  47.7 2.0 copy-done.13
  49.8 1.9 constant_dynamic-slice_fusion
  51.7 2.0 collective-permute-start.13
  55.2 2.7 gather.1
  57.9 25.5 %attention.6.rest_0_ = bf16[1024,512]{1,0:T(8,128)(2,1)S(1)} custom-call(s32[1]{0:T(128)} %bitcast.cp_ref, bf16[1024,2048]{1,0:T(8,128)(2,1)S(1)} %copy-done.14, bf16[1024,2048]{1,0:T(8,128)(2,1)S(1)} %copy-done.14, bf16[8192,128]{1,0:T(8,128)(2,1)S(1)} %get-tuple-element.30.k_ref, bf16[64,128,128]{2,1,0:T(8,128)(2,1)S(1)} %get-tuple-element.31.vt_ref), custom_call_target="tpu_custom_call" | custom-call | flops 17179869184 | bytes 2097152 | tf_op jit(solution)/shard_map/attention/pallas_call | solution.py:294
  83.4 11.0 %attention.7 = bf16[1024,128]{1,0:T(8,128)(2,1)S(1)} custom-call(s32[1]{0:T(128)} %bitcast.cp_ref, bf16[1024,384]{1,0:T(8,128)(2,1)S(1)} %collective-permute-done.6.q_ref.qn_ref, bf16[1024,384]{1,0:T(8,128)(2,1)S(1)} %collective-permute-done.6.q_ref.qn_ref, bf16[8192,128]{1,0:T(8,128)(2,1)S(1)} %get-tuple-element.30.k_ref, ...), custom_call_target="tpu_custom_call" | custom-call | flops 4294967296 | bytes 524288 | tf_op jit(solution)/shard_map/attention/pallas_call | solution.py:294
  94.4 7.3 %collective-permute-start.7 = (bf16[1024,128]{1,0:T(8,128)(2,1)S(1)}, bf16[1024,128]{1,0:T(8,128)(2,1)S(1)}, u32[]{:S(2)}, u32[]{:S(2)}) collective-permute-start(bf16[1024,128]{1,0:T(8,128)(2,1)S(1)} %attention.7), channel_id=1, source_target_pairs={{0,3},{1,2},{4,7},{5,6}} | collective-permute-start | bytes 786440 | tf_op jit(solution)/shard_map/ppermute | solution.py:478
  101.7 1.6 collective-permute-start.9
  103.3 31.5 %attention.8.rest_1_ = bf16[1024,640]{1,0:T(8,128)(2,1)S(1)} custom-call(s32[1]{0:T(128)} %bitcast.cp_ref, bf16[1024,2048]{1,0:T(8,128)(2,1)S(1)} %copy-done.14, bf16[1024,2048]{1,0:T(8,128)(2,1)S(1)} %copy-done.14, bf16[8192,128]{1,0:T(8,128)(2,1)S(1)} %get-tuple-element.30.k_ref, bf16[64,128,128]{2,1,0:T(8,128)(2,1)S(1)} %get-tuple-element.31.vt_ref), custom_call_target="tpu_custom_call" | custom-call | flops 21474836480 | bytes 2621440 | tf_op jit(solution)/shard_map/attention/pallas_call | solution.py:294
  134.8 20.2 %attention.9 = bf16[1024,256]{1,0:T(8,128)(2,1)S(1)} custom-call(s32[1]{0:T(128)} %bitcast.cp_ref, bf16[1024,384]{1,0:T(8,128)(2,1)S(1)} %collective-permute-done.6.q_ref.qn_ref, bf16[1024,384]{1,0:T(8,128)(2,1)S(1)} %collective-permute-done.6.q_ref.qn_ref, bf16[8192,128]{1,0:T(8,128)(2,1)S(1)} %get-tuple-element.30.k_ref, ...), custom_call_target="tpu_custom_call" | custom-call | flops 8589934592 | bytes 1048576 | tf_op jit(solution)/shard_map/attention/pallas_call | solution.py:294
  155.1 1.8 collective-permute-start.8
  156.9 2.0 collective-permute-start.18
  158.9 19.5 %attention.10.rest_2_ = bf16[1024,384]{1,0:T(8,128)(2,1)S(1)} custom-call(s32[1]{0:T(128)} %bitcast.cp_ref, bf16[1024,2048]{1,0:T(8,128)(2,1)S(1)} %copy-done.14, bf16[1024,2048]{1,0:T(8,128)(2,1)S(1)} %copy-done.14, bf16[8192,128]{1,0:T(8,128)(2,1)S(1)} %get-tuple-element.30.k_ref, bf16[64,128,128]{2,1,0:T(8,128)(2,1)S(1)} %get-tuple-element.31.vt_ref), custom_call_target="tpu_custom_call" | custom-call | flops 12884901888 | bytes 1572864 | tf_op jit(solution)/shard_map/attention/pallas_call | solution.py:294
  179.0 1.5 collective-permute-start.10
  180.5 25.7 %attention.11.rest_3_ = bf16[1024,512]{1,0:T(8,128)(2,1)S(1)} custom-call(s32[1]{0:T(128)} %bitcast.cp_ref, bf16[1024,2048]{1,0:T(8,128)(2,1)S(1)} %copy-done.15, bf16[1024,2048]{1,0:T(8,128)(2,1)S(1)} %copy-done.15, bf16[8192,128]{1,0:T(8,128)(2,1)S(1)} %get-tuple-element.30.k_ref, bf16[64,128,128]{2,1,0:T(8,128)(2,1)S(1)} %get-tuple-element.31.vt_ref, ...), custom_call_target="tpu_custom_call" | custom-call | flops 17179869184 | bytes 2097152 | tf_op jit(solution)/shard_map/attention/pallas_call | solution.py:294
  206.2 7.6 %collective-permute-done.17.rest_8_ = bf16[256,4096]{1,0:T(8,128)(2,1)S(1)} collective-permute-done((bf16[256,4096]{1,0:T(8,128)(2,1)S(1)}, bf16[256,4096]{1,0:T(8,128)(2,1)S(1)}, u32[]{:S(2)}, u32[]{:S(2)}) %collective-permute-start.17) | collective-permute-done | bytes 2097184 | tf_op jit(solution)/shard_map/ppermute | solution.py:470
  213.9 35.3 %collective-permute-done.18.rest_9_ = bf16[256,4096]{1,0:T(8,128)(2,1)S(1)} collective-permute-done((bf16[256,4096]{1,0:T(8,128)(2,1)S(1)}, bf16[256,4096]{1,0:T(8,128)(2,1)S(1)}, u32[]{:S(2)}, u32[]{:S(2)}) %collective-permute-start.18) | collective-permute-done | bytes 2097184 | tf_op jit(solution)/shard_map/ppermute | solution.py:470
  252.3 22.4 %own_part.1.y_ref = f32[1024,4096]{1,0:T(8,128)} custom-call(bf16[1024,4096]{1,0:T(8,128)(2,1)S(1)} %bitcast.7, bf16[1024,512]{1,0:T(8,128)(2,1)S(1)} %copy-done.6, bf16[1024,640]{1,0:T(8,128)(2,1)S(1)} %attention.8.rest_1_, bf16[1024,384]{1,0:T(8,128)(2,1)S(1)} %copy-done.10, bf16[1024,512]{1,0:T(8,128)(2,1)S(1)} %attention.11.rest_3_, ...), custom_call_target="tpu_custom_call" | custom-call | flops 17179869184 | bytes 25165824 | tf_op jit(solution)/shard_map/own_part/pallas_call | solution.py:363
  277.4 23.0 %other_part.1 = bf16[1024,4096]{1,0:T(8,128)(2,1)} custom-call(s32[1]{0:T(128)} %bitcast.cp_ref, f32[1024,4096]{1,0:T(8,128)} %own_part.1.y_ref, bf16[1024,512]{1,0:T(8,128)(2,1)S(1)} %copy-done.4, bf16[1024,640]{1,0:T(8,128)(2,1)S(1)} %collective-permute-done.10.rest_1_, bf16[1024,384]{1,0:T(8,128)(2,1)S(1)} %copy-done.8, ...), custom_call_target="tpu_custom_call" | custom-call | flops 17179869184 | bytes 25165824 | tf_op jit(solution)/shard_map/other_part/pallas_call | solution.py:403
  (71 shorter events, 13.9 us)
Async XLA Ops:
  1.7 20.3 %collective-permute-start.1 = (bf16[2048,128]{1,0:T(8,128)(2,1)S(1)}, bf16[2048,128]{1,0:T(8,128)(2,1)S(1)}, u32[]{:S(2)}, u32[]{:S(2)}) collective-permute-start(bf16[2048,128]{1,0:T(8,128)(2,1)S(1)} %pad_maximum_fusion.refs_0_), channel_id=1, source_target_pairs={{0,2},{1,3},{2,0},{3,1},{4,6},{5,7},{6,4},{7,5}} | collective-permute-start | bytes 1572872 | tf_op jit(solution)/shard_map/ppermute | solution.py:441
  5.0 46.7 %collective-permute-start = (bf16[2048,128]{1,0:T(8,128)(2,1)S(1)}, bf16[2048,128]{1,0:T(8,128)(2,1)S(1)}, u32[]{:S(2)}, u32[]{:S(2)}) collective-permute-start(bf16[2048,128]{1,0:T(8,128)(2,1)S(1)} %pad_maximum_fusion.refs_0_), channel_id=1, source_target_pairs={{0,1},{1,0},{2,3},{3,2},{4,5},{5,4},{6,7},{7,6}} | collective-permute-start | bytes 1572872 | tf_op jit(solution)/shard_map/ppermute | solution.py:441
  19.9 33.9 %collective-permute-start.5 = (bf16[2048,128]{1,0:T(8,128)(2,1)S(1)}, bf16[2048,128]{1,0:T(8,128)(2,1)S(1)}, u32[]{:S(2)}, u32[]{:S(2)}) collective-permute-start(bf16[2048,128]{1,0:T(8,128)(2,1)S(1)} %bitcast.8), channel_id=1, source_target_pairs={{0,3},{1,0},{2,1},{3,2},{4,7},{5,4},{6,5},{7,6}} | collective-permute-start | bytes 1572872 | tf_op jit(solution)/shard_map/ppermute | solution.py:450
  20.0 35.0 %collective-permute-start.4 = (bf16[2048,128]{1,0:T(8,128)(2,1)S(1)}, bf16[2048,128]{1,0:T(8,128)(2,1)S(1)}, u32[]{:S(2)}, u32[]{:S(2)}) collective-permute-start(bf16[2048,128]{1,0:T(8,128)(2,1)S(1)} %bitcast.9), channel_id=1, source_target_pairs={{0,2},{1,3},{2,0},{3,1},{4,6},{5,7},{6,4},{7,5}} | collective-permute-start | bytes 1572872 | tf_op jit(solution)/shard_map/ppermute | solution.py:450
  22.0 33.1 %collective-permute-start.3 = (bf16[2048,128]{1,0:T(8,128)(2,1)S(1)}, bf16[2048,128]{1,0:T(8,128)(2,1)}, u32[]{:S(2)}, u32[]{:S(2)}) collective-permute-start(bf16[2048,128]{1,0:T(8,128)(2,1)S(1)} %bitcast.10), channel_id=1, source_target_pairs={{0,1},{1,2},{2,3},{3,0},{4,5},{5,6},{6,7},{7,4}} | collective-permute-start | bytes 1572872 | tf_op jit(solution)/shard_map/ppermute | solution.py:450
  22.0 33.1 %collective-permute-start.2 = (bf16[2048,128]{1,0:T(8,128)(2,1)S(1)}, bf16[2048,128]{1,0:T(8,128)(2,1)}, u32[]{:S(2)}, u32[]{:S(2)}) collective-permute-start(bf16[2048,128]{1,0:T(8,128)(2,1)S(1)} %collective-permute-done.1.refs_2_), channel_id=1, source_target_pairs={{0,1},{1,0},{2,3},{3,2},{4,5},{5,4},{6,7},{7,6}} | collective-permute-start | bytes 1572872 | tf_op jit(solution)/shard_map/ppermute | solution.py:448
  51.7 105.1 %collective-permute-start.13 = (bf16[256,4096]{1,0:T(8,128)(2,1)S(1)}, bf16[256,4096]{1,0:T(8,128)(2,1)S(1)}, u32[]{:S(2)}, u32[]{:S(2)}) collective-permute-start(bf16[256,4096]{1,0:T(8,128)(2,1)S(1)} %constant_dynamic-slice_fusion), channel_id=1, source_target_pairs={{0,4},{4,0},{1,5},{5,1},{2,6},{6,2},{3,7},{7,3}} | collective-permute-start | bytes 6291464 | tf_op jit(solution)/shard_map/ppermute | solution.py:443
  53.8 29.6 %collective-permute-start.6 = (bf16[1024,384]{1,0:T(8,128)(2,1)S(1)}, bf16[1024,384]{1,0:T(8,128)(2,1)S(1)}, u32[]{:S(2)}, u32[]{:S(2)}) collective-permute-start(bf16[1024,384]{1,0:T(8,128)(2,1)S(1)} %copy-done.12), channel_id=1, source_target_pairs={{3,0},{2,1},{7,4},{6,5}} | collective-permute-start | bytes 2359304 | tf_op jit(solution)/shard_map/ppermute | solution.py:452
  55.1 101.8 %collective-permute-start.14 = (bf16[256,4096]{1,0:T(8,128)(2,1)S(1)}, bf16[256,4096]{1,0:T(8,128)(2,1)S(1)}, u32[]{:S(2)}, u32[]{:S(2)}) collective-permute-start(bf16[256,4096]{1,0:T(8,128)(2,1)S(1)} %copy-done.2), channel_id=1, source_target_pairs={{0,4},{4,0},{1,5},{5,1},{2,6},{6,2},{3,7},{7,3}} | collective-permute-start | bytes 6291464 | tf_op jit(solution)/shard_map/ppermute | solution.py:447
  94.4 84.0 %collective-permute-start.7 = (bf16[1024,128]{1,0:T(8,128)(2,1)S(1)}, bf16[1024,128]{1,0:T(8,128)(2,1)S(1)}, u32[]{:S(2)}, u32[]{:S(2)}) collective-permute-start(bf16[1024,128]{1,0:T(8,128)(2,1)S(1)} %attention.7), channel_id=1, source_target_pairs={{0,3},{1,2},{4,7},{5,6}} | collective-permute-start | bytes 786440 | tf_op jit(solution)/shard_map/ppermute | solution.py:478
  101.7 148.8 %collective-permute-start.9 = (bf16[1024,512]{1,0:T(8,128)(2,1)S(1)}, bf16[1024,512]{1,0:T(8,128)(2,1)S(1)}, u32[]{:S(2)}, u32[]{:S(2)}) collective-permute-start(bf16[1024,512]{1,0:T(8,128)(2,1)S(1)} %attention.6.rest_0_), channel_id=1, source_target_pairs={{0,4},{4,0},{1,5},{5,1},{2,6},{6,2},{3,7},{7,3}} | collective-permute-start | bytes 3145736 | tf_op jit(solution)/shard_map/ppermute | solution.py:464
  155.1 23.9 %collective-permute-start.8 = (bf16[1024,256]{1,0:T(8,128)(2,1)S(1)}, bf16[1024,256]{1,0:T(8,128)(2,1)S(1)}, u32[]{:S(2)}, u32[]{:S(2)}) collective-permute-start(bf16[1024,256]{1,0:T(8,128)(2,1)S(1)} %attention.9), channel_id=1, source_target_pairs={{0,3},{1,2},{4,7},{5,6}} | collective-permute-start | bytes 1572872 | tf_op jit(solution)/shard_map/ppermute | solution.py:478
  156.9 57.0 %collective-permute-start.17 = (bf16[256,4096]{1,0:T(8,128)(2,1)S(1)}, bf16[256,4096]{1,0:T(8,128)(2,1)S(1)}, u32[]{:S(2)}, u32[]{:S(2)}) collective-permute-start(bf16[256,4096]{1,0:T(8,128)(2,1)S(1)} %collective-permute-done.13.rest_4_), channel_id=1, source_target_pairs={{0,2},{1,3},{2,0},{3,1},{4,6},{5,7},{6,4},{7,5}} | collective-permute-start | bytes 6291464 | tf_op jit(solution)/shard_map/ppermute | solution.py:470
  156.9 92.2 %collective-permute-start.18 = (bf16[256,4096]{1,0:T(8,128)(2,1)S(1)}, bf16[256,4096]{1,0:T(8,128)(2,1)S(1)}, u32[]{:S(2)}, u32[]{:S(2)}) collective-permute-start(bf16[256,4096]{1,0:T(8,128)(2,1)S(1)} %collective-permute-done.14.rest_5_), channel_id=1, source_target_pairs={{0,2},{1,3},{2,0},{3,1},{4,6},{5,7},{6,4},{7,5}} | collective-permute-start | bytes 6291464 | tf_op jit(solution)/shard_map/ppermute | solution.py:470
  158.9 92.2 %slice-start = ((s8[8388608]{0:T(1024)(128)(4,1)}), s8[4194304]{0:T(1024)(128)(4,1)S(1)}, s32[]{:S(2)}) async-start(s8[8388608]{0:T(1024)(128)(4,1)} %bitcast.6), calls=%async_computation | async-start | bytes 8388608
  178.4 72.6 %slice-start.1 = ((s8[8388608]{0:T(1024)(128)(4,1)}), s8[4194304]{0:T(1024)(128)(4,1)S(1)}, s32[]{:S(2)}) async-start(s8[8388608]{0:T(1024)(128)(4,1)} %bitcast.6), calls=%async_computation.1 | async-start | bytes 8388608
  178.5 72.6 %copy-start.6 = (bf16[1024,512]{1,0:T(8,128)(2,1)S(1)}, bf16[1024,512]{1,0:T(8,128)(2,1)}, u32[]{:S(2)}) copy-start(bf16[1024,512]{1,0:T(8,128)(2,1)} %copy-done.5) | copy-start | bytes 3145732
  178.5 70.7 %collective-permute-start.11 = (bf16[1024,384]{1,0:T(8,128)(2,1)S(1)}, bf16[1024,384]{1,0:T(8,128)(2,1)S(1)}, u32[]{:S(2)}, u32[]{:S(2)}) collective-permute-start(bf16[1024,384]{1,0:T(8,128)(2,1)S(1)} %attention.10.rest_2_), channel_id=1, source_target_pairs={{0,4},{4,0},{1,5},{5,1},{2,6},{6,2},{3,7},{7,3}} | collective-permute-start | bytes 2359304 | tf_op jit(solution)/shard_map/ppermute | solution.py:464
  179.0 71.6 %collective-permute-start.10 = (bf16[1024,640]{1,0:T(8,128)(2,1)S(1)}, bf16[1024,640]{1,0:T(8,128)(2,1)S(1)}, u32[]{:S(2)}, u32[]{:S(2)}) collective-permute-start(bf16[1024,640]{1,0:T(8,128)(2,1)S(1)} %attention.8.rest_1_), channel_id=1, source_target_pairs={{0,4},{4,0},{1,5},{5,1},{2,6},{6,2},{3,7},{7,3}} | collective-permute-start | bytes 3932168 | tf_op jit(solution)/shard_map/ppermute | solution.py:464
  213.9 62.3 %collective-permute-start.15 = (bf16[256,4096]{1,0:T(8,128)(2,1)S(1)}, bf16[256,4096]{1,0:T(8,128)(2,1)S(1)}, u32[]{:S(2)}, u32[]{:S(2)}) collective-permute-start(bf16[256,4096]{1,0:T(8,128)(2,1)S(1)} %collective-permute-done.13.rest_4_), channel_id=1, source_target_pairs={{0,1},{1,0},{2,3},{3,2},{4,5},{5,4},{6,7},{7,6}} | collective-permute-start | bytes 6291464 | tf_op jit(solution)/shard_map/ppermute | solution.py:471
  249.1 27.0 %collective-permute-start.16 = (bf16[256,4096]{1,0:T(8,128)(2,1)S(1)}, bf16[256,4096]{1,0:T(8,128)(2,1)S(1)}, u32[]{:S(2)}, u32[]{:S(2)}) collective-permute-start(bf16[256,4096]{1,0:T(8,128)(2,1)S(1)} %collective-permute-done.14.rest_5_), channel_id=1, source_target_pairs={{0,1},{1,0},{2,3},{3,2},{4,5},{5,4},{6,7},{7,6}} | collective-permute-start | bytes 6291464 | tf_op jit(solution)/shard_map/ppermute | solution.py:471
  250.0 26.1 %collective-permute-start.19 = (bf16[256,4096]{1,0:T(8,128)(2,1)S(1)}, bf16[256,4096]{1,0:T(8,128)(2,1)S(1)}, u32[]{:S(2)}, u32[]{:S(2)}) collective-permute-start(bf16[256,4096]{1,0:T(8,128)(2,1)S(1)} %collective-permute-done.17.rest_8_), channel_id=1, source_target_pairs={{0,1},{1,0},{2,3},{3,2},{4,5},{5,4},{6,7},{7,6}} | collective-permute-start | bytes 6291464 | tf_op jit(solution)/shard_map/ppermute | solution.py:474
  250.6 25.6 %collective-permute-start.20 = (bf16[256,4096]{1,0:T(8,128)(2,1)S(1)}, bf16[256,4096]{1,0:T(8,128)(2,1)S(1)}, u32[]{:S(2)}, u32[]{:S(2)}) collective-permute-start(bf16[256,4096]{1,0:T(8,128)(2,1)S(1)} %collective-permute-done.18.rest_9_), channel_id=1, source_target_pairs={{0,1},{1,0},{2,3},{3,2},{4,5},{5,4},{6,7},{7,6}} | collective-permute-start | bytes 6291464 | tf_op jit(solution)/shard_map/ppermute | solution.py:474
  250.6 25.5 %collective-permute-start.12 = (bf16[1024,512]{1,0:T(8,128)(2,1)S(1)}, bf16[1024,512]{1,0:T(8,128)(2,1)S(1)}, u32[]{:S(2)}, u32[]{:S(2)}) collective-permute-start(bf16[1024,512]{1,0:T(8,128)(2,1)S(1)} %attention.11.rest_3_), channel_id=1, source_target_pairs={{0,4},{4,0},{1,5},{5,1},{2,6},{6,2},{3,7},{7,3}} | collective-permute-start | bytes 3145736 | tf_op jit(solution)/shard_map/ppermute | solution.py:464
  (15 other events, 144.5 us)

commit v3 on v2

--- a/solution.py
+++ b/solution.py
@@ -16,7 +16,7 @@
 F32 = jnp.float32
 BF = jnp.bfloat16
 ATTN_VMEM = 24 * 2 ** 20
-NORM_VMEM = 48 * 2 ** 20
+NORM_VMEM = 36 * 2 ** 20
 Q_VMEM = 36 * 2 ** 20
 OUT_VMEM = 28 * 2 ** 20
 
@@ -54,12 +54,14 @@
         kv_ref[1, rs, :] = v
 
 
-def norm_kv(cp, x, g, w_qkv, b, table, w_out, piece, block=256):
+def norm_kv(cp, x, g, w_qkv, b, table, w_out, block=256):
     rows, d = x.shape
     steps = rows // block
     last = w_qkv.shape[1] // (2 * HEAD) - 1
     row = lambda i, c: (i, 0)
-    part = piece // steps
+    skip, piece = PIECE_ROWS
+    pieces = piece // skip
+    copied = lambda i: jnp.minimum(i, pieces - 1)
     head_rows = pl.BlockSpec((block, HEAD), row)
     return pl.pallas_call(
         norm_kv_kernel,
@@ -72,7 +74,7 @@
                 pl.BlockSpec((d, 2 * HEAD), lambda i, c: (0, last)),
                 pl.BlockSpec((1, 2 * HEAD), lambda i, c: (0, last)),
                 pl.BlockSpec((block, table.shape[1]), row),
-                pl.BlockSpec((part, w_out.shape[1]), lambda i, c: ((c[0] * PIECES + 1) * steps + i, 0)),
+                pl.BlockSpec((skip, w_out.shape[1]), lambda i, c: (c[0] * (pieces + 1) + 1 + copied(i), 0)),
             ],
             out_specs=[
                 pl.BlockSpec((block, d), row),
@@ -81,7 +83,7 @@
                 head_rows,
                 head_rows,
                 head_rows,
-                pl.BlockSpec((part, w_out.shape[1]), row),
+                pl.BlockSpec((skip, w_out.shape[1]), lambda i, c: (copied(i), 0)),
             ],
         ),
         out_shape=[
@@ -149,18 +151,39 @@
 CHUNK = 256
 
 
-def attn_kernel(cp_ref, q_ref, qn_ref, k_ref, vt_ref, *rest, old, first, foreign):
-    back_refs = rest[:-8]
-    o_ref, s_ref, p_ref, acc_ref, mx_ref, m_ref, l_ref, al_ref = rest[-8:]
+def attn_kernel(cp_ref, *refs, old, slots, first, far, far_first, backs):
+    refs = list(refs)
+    take = lambda n: [refs.pop(0) for _ in range(n)]
+    far_q = take(2 if far else 0)
+    own_q = take(2 if slots else 0)
+    k_ref, vt_ref = take(2)
+    back_refs = take(backs)
+    far_outs = take(1 if far else 0)
+    own_outs = take(1 if slots else 0)
+    s_ref, p_ref, acc_ref, mx_ref, m_ref, l_ref, al_ref = take(7)
     slot = pl.program_id(0)
+    if far and slots:
+        q_ref, qn_ref = take(2)
+        for at, ref, pair in ((slot, q_ref, (far_q[0], own_q[0])), (slot + 1, qn_ref, (far_q[1], own_q[1]))):
+            for is_far, source in ((at < far, pair[0]), (at >= far, pair[1])):
+                @pl.when(is_far)
+                def _(ref=ref, source=source):
+                    ref[...] = source[...]
+    else:
+        q_ref, qn_ref = far_q or own_q
+
     rows = q_ref.shape[0]
     strips = rows // STRIP
     chunks = rows // CHUNK
     cp = cp_ref[0]
-    if foreign:
-        owner = jnp.where(first + slot < taken(cp), 3 - cp, -1)
-    else:
-        owner = jnp.where(first + slot < HEADS - given(cp), cp, -1)
+
+    def owner_of(slot):
+        other = jnp.where(far_first + slot < taken(cp), 3 - cp, -1)
+        mine = jnp.where(first + slot - far < HEADS - given(cp), cp, -1)
+        return jnp.where(slot < far, other, mine)
+
+    owner = owner_of(slot)
+    fresh = (slot == 0) | (owner_of(slot - 1) < 0)
 
     def scores(qr, base, u, w):
         k = k_ref[pl.ds(base + u * CHUNK, CHUNK), :]
@@ -223,26 +246,10 @@
     full = [chunks] * strips
     upper = [w + 1 for w in range(strips)]
 
-    @pl.when((slot == 0) & (owner >= 0))
+    @pl.when(fresh & (owner >= 0))
     def _():
-        def strip(w, carry):
-            cs = pl.ds(pl.multiple_of(w * STRIP, STRIP), STRIP)
-            top = None
-            for u in range(chunks):
-                ks = pl.ds(u * CHUNK, CHUNK)
-                s = lax.dot_general(k_ref[ks, :], q_ref[cs, :], (((1,), (1,)), ((), ())), preferred_element_type=F32)
-                s_ref[ks, cs] = s
-                top = col_max(s) if top is None else jnp.maximum(top, col_max(s))
-            mx_ref[:, cs] = top
-            return carry
-
-        lax.fori_loop(0, strips, strip, 0)
-
-        def clear(i, carry):
-            p_ref[i] = jnp.zeros_like(p_ref[0])
-            return carry
-
-        lax.fori_loop(0, rows // HEAD, clear, 0)
+        stage(qk=(q_ref, 0, full))
+        p_ref[...] = jnp.zeros_like(p_ref)
         acc_ref[...] = jnp.zeros_like(acc_ref)
 
     @pl.when(owner >= 0)
@@ -264,50 +271,57 @@
         stage(pv=(own, upper))
         for w in range(strips):
             cs = pl.ds(w * STRIP, STRIP)
-            o_ref[cs, :] = (acc_ref[:, cs] / l_ref[:, cs].sum(axis=0, keepdims=True)).astype(BF).T
+            o = (acc_ref[:, cs] / l_ref[:, cs].sum(axis=0, keepdims=True)).astype(BF).T
+            for out, mine in [(out, slot < far) for out in far_outs] + [(out, slot >= far) for out in own_outs]:
+                @pl.when(mine)
+                def _(out=out, o=o, cs=cs):
+                    out[cs, :] = o
 
     for i, back_ref in enumerate(back_refs):
         @pl.when((owner < 0) & ((slot == pl.num_programs(0) - 1) == (i == 0)))
         def _(back_ref=back_ref):
-            o_ref[...] = back_ref[...]
-
-
-def attention(cp, q, k_all, vt_all, *, slots, first=0, foreign=False, back=()):
-    rows = q.shape[0]
+            own_outs[0][...] = back_ref[...]
+
+
+def attention(cp, q, q_far, k_all, vt_all, *, slots=0, first=0, far=0, far_first=0, back=()):
+    rows = k_all.shape[0] // 8
     keys = k_all.shape[0]
-    old = keys - 4 * rows
-    if foreign:
-        col = lambda s: MOVED - 1 - first - s
-    else:
-        col = lambda s: s + first
     row_block = lambda index: pl.BlockSpec((rows, HEAD), index)
-    operands = [q, q, k_all, vt_all]
-    in_specs = [
-        row_block(lambda s, c: (0, col(s))),
-        row_block(lambda s, c: (0, col(jnp.minimum(s + 1, slots - 1)))),
+    far_col = lambda s: MOVED - 1 - far_first - jnp.clip(s, 0, far - 1)
+    own_col = lambda s: first + jnp.clip(s - far, 0, slots - 1)
+    operands, in_specs, out_specs, out_shape = [], [], [], []
+    for count, source, col, out_col in (
+        (far, q_far, far_col, lambda s: far - 1 - jnp.clip(s, 0, far - 1)),
+        (slots, q, own_col, lambda s: jnp.clip(s - far, 0, slots - 1)),
+    ):
+        if count:
+            operands += [source, source]
+            in_specs += [row_block(lambda s, c, col=col: (0, col(s))), row_block(lambda s, c, col=col: (0, col(s + 1)))]
+            out_specs.append(row_block(lambda s, c, col=out_col: (0, col(s))))
+            out_shape.append(jax.ShapeDtypeStruct((rows, count * HEAD), BF))
+    operands += [k_all, vt_all, *back]
+    in_specs += [
         pl.BlockSpec((keys, HEAD), lambda s, c: (0, 0)),
         pl.BlockSpec((keys // HEAD, HEAD, HEAD), lambda s, c: (0, 0, 0)),
     ]
-    for i, part in enumerate(back):
-        operands.append(part)
-        in_specs.append(row_block((lambda s, c: (0, 0)) if i == 0 else (lambda s, c: (0, jnp.clip(s - (slots - MOVED), 0, MOVED - 2)))))
+    for i in range(len(back)):
+        in_specs.append(row_block((lambda s, c: (0, 0)) if i == 0 else (lambda s, c: (0, jnp.clip(s - far - (slots - MOVED), 0, MOVED - 2)))))
+    scratch = [
+        pltpu.VMEM((rows, rows), F32),
+        pltpu.VMEM((rows // HEAD, rows, HEAD), BF),
+        pltpu.VMEM((HEAD, rows), F32),
+    ] + [pltpu.VMEM((8, rows), F32)] * 4
+    if far and slots:
+        scratch += [pltpu.VMEM((rows, HEAD), BF)] * 2
+    count = far + slots
     return pl.pallas_call(
-        functools.partial(attn_kernel, old=old, first=first, foreign=foreign),
+        functools.partial(attn_kernel, old=keys // 2, slots=slots, first=first, far=far, far_first=far_first, backs=len(back)),
         grid_spec=pltpu.PrefetchScalarGridSpec(
-            num_scalar_prefetch=1,
-            grid=(slots,),
-            in_specs=in_specs,
-            out_specs=row_block(lambda s, c: (0, slots - 1 - s if foreign else s)),
-            scratch_shapes=[
-                pltpu.VMEM((rows, rows), F32),
-                pltpu.VMEM((rows // HEAD, rows, HEAD), BF),
-                pltpu.VMEM((HEAD, rows), F32),
-            ]
-            + [pltpu.VMEM((8, rows), F32)] * 4,
+            num_scalar_prefetch=1, grid=(count,), in_specs=in_specs, out_specs=out_specs, scratch_shapes=scratch
         ),
-        out_shape=jax.ShapeDtypeStruct((rows, slots * HEAD), BF),
+        out_shape=out_shape,
         compiler_params=pltpu.CompilerParams(dimension_semantics=("arbitrary",), vmem_limit_bytes=ATTN_VMEM),
-        cost_estimate=pl.CostEstimate(flops=4 * rows * slots * HEAD * keys, bytes_accessed=4 * rows * slots * HEAD, transcendentals=0),
+        cost_estimate=pl.CostEstimate(flops=4 * rows * count * HEAD * keys, bytes_accessed=4 * rows * count * HEAD, transcendentals=0),
         name="attention",
     )(cp, *operands)
 
@@ -384,14 +398,15 @@
             o_buf[:, pl.ds(at, o_ref.shape[1])] = o_ref[...]
             at += o_ref.shape[1]
 
-    depth = w_refs[0].shape[0]
-    halves = len(w_refs) // 4
+    pieces = len(w_refs) // 4
+    depth = sum(w_ref.shape[0] for w_ref in w_refs[:pieces])
     for r in range(y_ref.shape[0] // 256):
         rs = pl.ds(r * 256, 256)
         total = None
-        for i, w_ref in enumerate(w_refs):
-            at = pl.multiple_of(((cp_ref[0] ^ (i // halves)) * halves + i % halves) * depth, depth)
-            x = jnp.dot(o_buf[rs, pl.ds(at, depth)], w_ref[...], preferred_element_type=F32)
+        for i in range(4):
+            at = pl.multiple_of((cp_ref[0] ^ i) * depth, depth)
+            w = jnp.concatenate([w_ref[...] for w_ref in w_refs[i * pieces:(i + 1) * pieces]], axis=0)
+            x = jnp.dot(o_buf[rs, pl.ds(at, depth)], w, preferred_element_type=F32)
             total = x if total is None else total + x
         out_ref[rs, :] = (y_ref[rs, :] + total).astype(BF)
 
@@ -419,7 +434,8 @@
 
 
 SIZES = (4, 5, 3, 4)
-PIECES = 2
+PIECE_ROWS = (128, 384)
+PIECES = len(PIECE_ROWS)
 
 
 def after(a, *others):
@@ -432,18 +448,18 @@
     cp = lax.axis_index("cp")
     swap = [(0, 1), (1, 0)]
     width = w_out.shape[0]
-    piece = width // (n * PIECES)
+    quarter = width // n
     where = cp.astype(jnp.int32)[None]
     around = lambda s: [(i, (i + s) % n) for i in range(n)]
     flip = lambda bits: [(i, i ^ bits) for i in range(n)]
 
     kv_cache = jnp.concatenate([k_cache[:, 0], v_cache[:, 0]], axis=0)
     old = [kv_cache, lax.ppermute(kv_cache, "cp", flip(1)), lax.ppermute(kv_cache, "cp", flip(2))]
-    mine = lax.dynamic_slice_in_dim(w_out, cp * PIECES * piece, piece, 0)
+    mine = lax.dynamic_slice_in_dim(w_out, cp * quarter, PIECE_ROWS[0], 0)
     w_peer = [lax.ppermute(mine, "tp", swap)]
 
     bias = b_qkv[None]
-    h, kv_new, new_k, new_v, cos, sin, mine = norm_kv(where, x, norm_gain[None], w_qkv, bias, rope_table, w_out, piece)
+    h, kv_new, new_k, new_v, cos, sin, mine = norm_kv(where, x, norm_gain[None], w_qkv, bias, rope_table, w_out)
     w_peer.append(lax.ppermute(mine, "tp", swap))
     old.append(lax.ppermute(after(old[2], kv_new), "cp", flip(1)))
     kv_new = kv_new.reshape(2 * rows, HEAD)
@@ -456,15 +472,14 @@
     attend = functools.partial(attention, where, k_all=k_all, vt_all=vt_all)
 
     o_own, o_other = [], []
-
-    def heads(i, *previous, back=()):
+    w_x, w_core, w_far = [None] * PIECES, [None] * PIECES, [None] * PIECES
+
+    def heads(i, *previous, far=0, far_first=0, back=()):
         q = after(queries, *previous) if previous else queries
-        part = attend(q=q, slots=SIZES[i], first=sum(SIZES[:i]), back=back)
-        o_own.append(part)
-        o_other.append(lax.ppermute(part, "tp", swap))
-        return part
-
-    w_x, w_core, w_far = [None] * PIECES, [None] * PIECES, [None] * PIECES
+        outs = attend(q, q_far, slots=SIZES[i], first=sum(SIZES[:i]), far=far, far_first=far_first, back=back)
+        o_own.append(outs[-1])
+        o_other.append(lax.ppermute(outs[-1], "tp", swap))
+        return outs
 
     def spread(i):
         w_x[i] = lax.ppermute(w_peer[i], "cp", flip(2))
@@ -473,19 +488,16 @@
     def spread_on(i):
         w_far[i] = lax.ppermute(w_x[i], "cp", flip(1))
 
-    def moved(first, slots, *previous):
-        far = attend(q=after(q_far, *previous), slots=slots, first=first, foreign=True)
-        return far, lax.ppermute(far, "cp", [(0, 3), (1, 2)])
-
     spread(0)
-    part = heads(0)
-    far, back0 = moved(0, 1, part)
+    (part,) = heads(0)
+    (far,) = attend(None, after(q_far, part), far=1)
+    back0 = lax.ppermute(far, "cp", [(0, 3), (1, 2)])
     w_peer[1] = after(w_peer[1], far)
     spread(1)
-    part = heads(1, far)
-    far, back1 = moved(1, MOVED - 1, part)
-    part = heads(2, far)
-    part = heads(3, part, back=(back0, back1))
+    far, part = heads(1, far, far=MOVED - 1, far_first=1)
+    back1 = lax.ppermute(far, "cp", [(0, 3)])
+    (part,) = heads(2, part)
+    (part,) = heads(3, part, back=(back0, back1))
     w_x = [after(w, part) for w in w_x]
     spread_on(0)
     spread_on(1)

time: 301 us -> 328 us (1.090)
  waiting for transfers between devices: 44.4 us -> 70.6 us
  local copies, waits for them, and re-layouts: 15.5 us -> 6.92 us
  starting transfers between devices: 24.8 us -> 33.3 us
    ppermute x6, waiting for transfers between devices: 1.42 us -> 70.5 us  [the longest x4 68.4 us: heads(): o_other.append(lax.ppermute(outs[-1], 'tp', swap))]
    ppermute x2, waiting for transfers between devices: 42.9 us -> 0.01 us  [spread(): w_x[i] = lax.ppermute(w_peer[i], 'cp', flip(2))]
    ppermute x2, starting transfers between devices: 0.01 us -> 9.89 us  [spread(): w_core[i] = lax.ppermute(w_peer[i], 'cp', flip(1))]
    unnamed x37 -> x11, local copies, waits for them, and re-layouts: 12.2 us -> 4.06 us
    pallas_call x6 -> x5, Pallas kernels: 133 us -> 134 us  [attention(): pl.pallas_call(functools.partial(attn_kernel, old=keys // 2, slots=slots,...]
  transfers between devices with their start and end apart: 21 -> 21, of which waited for: 3 -> 4; matrix products, arithmetic and copies ran while one was open for 1% -> 1% of each run, Pallas kernels for 64% -> 59%
where the time goes in v3:
time: 328 us
  Pallas kernels  215 us (66%)
  waiting for transfers between devices  70.6 us (22%)
  starting transfers between devices  33.3 us (10%)
  local copies, waits for them, and re-layouts  6.92 us (2%)
    pallas_call x5, Pallas kernels, attention(): pl.pallas_call(functools.partial(attn_kernel, old=keys // 2, slots=slots,...  134 us
    ppermute x4, waiting for transfers between devices, heads(): o_other.append(lax.ppermute(outs[-1], 'tp', swap))  68.4 us
    pallas_call x1, Pallas kernels, other_part(): pl.pallas_call(functools.partial(other_kernel, parts=len(o_parts)), grid_...  22.8 us
    pallas_call x1, Pallas kernels, q_proj(): pl.pallas_call(q_kernel, grid=(width // block,), in_specs=[pl.BlockSpec((...  22.7 us
    pallas_call x1, Pallas kernels, own_part(): pl.pallas_call(own_kernel, grid=(d // block,), in_specs=[pl.BlockSpec((ro...  22.5 us
    pallas_call x1, Pallas kernels, norm_kv(): pl.pallas_call(norm_kv_kernel, grid_spec=pltpu.PrefetchScalarGridSpec(num...  10.7 us
    ppermute x2, starting transfers between devices, spread(): w_core[i] = lax.ppermute(w_peer[i], 'cp', flip(1))  9.89 us
    ppermute x1, starting transfers between devices, local_step(): back0 = lax.ppermute(far, 'cp', [(0, 3), (1, 2)])  8.05 us
  transfers between devices with their start and end apart: 21, of which 4 were waited for; matrix products, arithmetic and copies ran while one was open for 1% of the time, Pallas kernels for 59%

profile of v3, /device:TPU:0, one launch (start us, length us, event | category | flops | bytes accessed | tf_op | source)
XLA Modules:
  0.0 327.7 jit_solution(2142501489191900876)
XLA Ops:
  1.7 3.3 %collective-permute-start.1 = (bf16[2048,128]{1,0:T(8,128)(2,1)S(1)}, bf16[2048,128]{1,0:T(8,128)(2,1)S(1)}, u32[]{:S(2)}, u32[]{:S(2)}) collective-permute-start(bf16[2048,128]{1,0:T(8,128)(2,1)S(1)} %pad_maximum_fusion.refs_0_), channel_id=1, source_target_pairs={{0,2},{1,3},{2,0},{3,1},{4,6},{5,7},{6,4},{7,5}} | collective-permute-start | bytes 1572872 | tf_op jit(solution)/shard_map/ppermute | solution.py:457
  7.6 10.7 %norm_kv.1 = (bf16[1024,4096]{1,0:T(8,128)(2,1)S(1)}, bf16[2,1024,128]{2,1,0:T(8,128)(2,1)S(1)}, bf16[1024,128]{1,0:T(8,128)(2,1)}, bf16[1024,128]{1,0:T(8,128)(...) custom-call(s32[1]{0:T(128)} %bitcast.cp_ref, bf16[1024,4096]{1,0:T(8,128)(2,1)} %x_ref.3, ...), custom_call_target="tpu_custom_call" | custom-call | flops 2147483648 | bytes 16777216 | tf_op jit(solution)/shard_map/norm_kv/pallas_call | solution.py:66
  18.5 2.0 collective-permute-start.4
  20.5 1.5 collective-permute-start.14
  22.3 22.7 %q_proj.1 = (bf16[1024,2048]{1,0:T(8,128)(2,1)S(1)}, bf16[1024,384]{1,0:T(8,128)(2,1)S(1)}) custom-call(bf16[1024,4096]{1,0:T(8,128)(2,1)S(1)} %get-tuple-element.25.h_ref, bf16[4096,2304]{1,0:T(8,128)(2,1)} %w_ref.3, bf16[1,2304]{1,0:T(2,128)(2,1)S(1)} %broadcast_in_dim.17.b_ref, f32[1024,128]{1,0:T(8,128)S(1)} %get-tuple-element.26.cos_ref, ...), custom_call_target="tpu_custom_call" | custom-call | flops 17179869184 | bytes 16777216 | tf_op jit(solution)/shard_map/q_proj/pallas_call | solution.py:120
  46.0 2.0 copy-done.1
  48.0 1.5 constant_dynamic-slice_fusion
  49.8 1.5 collective-permute-start.6
  51.3 2.6 gather.1
  53.9 25.8 %attention.5.rest_0_ = bf16[1024,512]{1,0:T(8,128)(2,1)S(1)} custom-call(s32[1]{0:T(128)} %bitcast.cp_ref, bf16[1024,2048]{1,0:T(8,128)(2,1)S(1)} %copy-done.2, bf16[1024,2048]{1,0:T(8,128)(2,1)S(1)} %copy-done.2, bf16[8192,128]{1,0:T(8,128)(2,1)S(1)} %get-tuple-element.31.refs_2_.refs_4_, bf16[64,128,128]{2,1,0:T(8,128)(2,1)S(1)} %get-tuple-element.32.refs_3_.refs_5_), custom_call_target="tpu_custom_call" | custom-call | flops 17179869184 | bytes 2097152 | tf_op jit(solution)/shard_map/attention/pallas_call | solution.py:317
  79.7 10.3 %attention.6 = bf16[1024,128]{1,0:T(8,128)(2,1)S(1)} custom-call(s32[1]{0:T(128)} %bitcast.cp_ref, bf16[1024,384]{1,0:T(8,128)(2,1)S(1)} %collective-permute-done.6.refs_0_.refs_1_, bf16[1024,384]{1,0:T(8,128)(2,1)S(1)} %collective-permute-done.6.refs_0_.refs_1_, bf16[8192,128]{1,0:T(8,128)(2,1)S(1)} %get-tuple-element.31.refs_2_.refs_4_, ...), custom_call_target="tpu_custom_call" | custom-call | flops 4294967296 | bytes 524288 | tf_op jit(solution)/shard_map/attention/pallas_call | solution.py:317
  89.9 8.1 %collective-permute-start.7 = (bf16[1024,128]{1,0:T(8,128)(2,1)S(1)}, bf16[1024,128]{1,0:T(8,128)(2,1)S(1)}, u32[]{:S(2)}, u32[]{:S(2)}) collective-permute-start(bf16[1024,128]{1,0:T(8,128)(2,1)S(1)} %attention.6), channel_id=1, source_target_pairs={{0,3},{1,2},{4,7},{5,6}} | collective-permute-start | bytes 786440 | tf_op jit(solution)/shard_map/ppermute | solution.py:494
  98.0 52.0 %attention.7 = (bf16[1024,256]{1,0:T(8,128)(2,1)S(1)}, bf16[1024,640]{1,0:T(8,128)(2,1)S(1)}) custom-call(s32[1]{0:T(128)} %bitcast.cp_ref, bf16[1024,384]{1,0:T(8,128)(2,1)S(1)} %collective-permute-done.6.refs_0_.refs_1_, bf16[1024,384]{1,0:T(8,128)(2,1)S(1)} %collective-permute-done.6.refs_0_.refs_1_, bf16[1024,2048]{1,0:T(8,128)(2,1)S(1)} %copy-done.2, ...), custom_call_target="tpu_custom_call" | custom-call | flops 30064771072 | bytes 3670016 | tf_op jit(solution)/shard_map/attention/pallas_call | solution.py:317
  151.4 19.6 %attention.8.rest_2_ = bf16[1024,384]{1,0:T(8,128)(2,1)S(1)} custom-call(s32[1]{0:T(128)} %bitcast.cp_ref, bf16[1024,2048]{1,0:T(8,128)(2,1)S(1)} %copy-done.2, bf16[1024,2048]{1,0:T(8,128)(2,1)S(1)} %copy-done.2, bf16[8192,128]{1,0:T(8,128)(2,1)S(1)} %get-tuple-element.31.refs_2_.refs_4_, bf16[64,128,128]{2,1,0:T(8,128)(2,1)S(1)} %get-tuple-element.32.refs_3_.refs_5_), custom_call_target="tpu_custom_call" | custom-call | flops 12884901888 | bytes 1572864 | tf_op jit(solution)/shard_map/attention/pallas_call | solution.py:317
  171.8 2.1 collective-permute-done.8.refs_5_
  174.0 26.0 %attention.9.rest_3_ = bf16[1024,512]{1,0:T(8,128)(2,1)S(1)} custom-call(s32[1]{0:T(128)} %bitcast.cp_ref, bf16[1024,2048]{1,0:T(8,128)(2,1)S(1)} %copy-done.2, bf16[1024,2048]{1,0:T(8,128)(2,1)S(1)} %copy-done.2, bf16[8192,128]{1,0:T(8,128)(2,1)S(1)} %get-tuple-element.31.refs_2_.refs_4_, bf16[64,128,128]{2,1,0:T(8,128)(2,1)S(1)} %get-tuple-element.32.refs_3_.refs_5_, ...), custom_call_target="tpu_custom_call" | custom-call | flops 17179869184 | bytes 2097152 | tf_op jit(solution)/shard_map/attention/pallas_call | solution.py:317
  199.9 9.7 %collective-permute-start.16 = (bf16[384,4096]{1,0:T(8,128)(2,1)}, bf16[384,4096]{1,0:T(8,128)(2,1)S(1)}, u32[]{:S(2)}, u32[]{:S(2)}) collective-permute-start(bf16[384,4096]{1,0:T(8,128)(2,1)} %collective-permute-done.14.rest_5_), channel_id=1, source_target_pairs={{0,1},{1,0},{2,3},{3,2},{4,5},{5,4},{6,7},{7,6}} | collective-permute-start | bytes 9437192 | tf_op jit(solution)/shard_map/ppermute | solution.py:486
  209.7 1.7 collective-permute-start.9
  211.9 40.2 %collective-permute-done.11.rest_2_ = bf16[1024,384]{1,0:T(8,128)(2,1)S(1)} collective-permute-done((bf16[1024,384]{1,0:T(8,128)(2,1)S(1)}, bf16[1024,384]{1,0:T(8,128)(2,1)S(1)}, u32[]{:S(2)}, u32[]{:S(2)}) %collective-permute-start.11) | collective-permute-done | bytes 786464 | tf_op jit(solution)/shard_map/ppermute | solution.py:481
  252.1 1.7 collective-permute-start.10
  254.1 22.5 %own_part.1.y_ref = f32[1024,4096]{1,0:T(8,128)} custom-call(bf16[1024,4096]{1,0:T(8,128)(2,1)S(1)} %bitcast.7, bf16[1024,512]{1,0:T(8,128)(2,1)S(1)} %attention.5.rest_0_, bf16[1024,640]{1,0:T(8,128)(2,1)S(1)} %get-tuple-element.36.rest_1_, bf16[1024,384]{1,0:T(8,128)(2,1)S(1)} %attention.8.rest_2_, bf16[1024,512]{1,0:T(8,128)(2,1)S(1)} %attention.9.rest_3_, ...), custom_call_target="tpu_custom_call" | custom-call | flops 17179869184 | bytes 25165824 | tf_op jit(solution)/shard_map/own_part/pallas_call | solution.py:377
  276.6 7.1 %collective-permute-done.10.rest_1_ = bf16[1024,640]{1,0:T(8,128)(2,1)S(1)} collective-permute-done((bf16[1024,640]{1,0:T(8,128)(2,1)S(1)}, bf16[1024,640]{1,0:T(8,128)(2,1)S(1)}, u32[]{:S(2)}, u32[]{:S(2)}) %collective-permute-start.10) | collective-permute-done | bytes 1310752 | tf_op jit(solution)/shard_map/ppermute | solution.py:481
  283.7 21.1 %collective-permute-done.12.rest_3_ = bf16[1024,512]{1,0:T(8,128)(2,1)S(1)} collective-permute-done((bf16[1024,512]{1,0:T(8,128)(2,1)S(1)}, bf16[1024,512]{1,0:T(8,128)(2,1)S(1)}, u32[]{:S(2)}, u32[]{:S(2)}) %collective-permute-start.12) | collective-permute-done | bytes 1048608 | tf_op jit(solution)/shard_map/ppermute | solution.py:481
  304.9 22.8 %other_part.1 = bf16[1024,4096]{1,0:T(8,128)(2,1)} custom-call(s32[1]{0:T(128)} %bitcast.cp_ref, f32[1024,4096]{1,0:T(8,128)} %own_part.1.y_ref, bf16[1024,512]{1,0:T(8,128)(2,1)S(1)} %collective-permute-done.9.rest_0_, bf16[1024,640]{1,0:T(8,128)(2,1)S(1)} %collective-permute-done.10.rest_1_, bf16[1024,384]{1,0:T(8,128)(2,1)S(1)} %collective-permute-done.11.rest_2_, ...), custom_call_target="tpu_custom_call" | custom-call | flops 17179869184 | bytes 25165824 | tf_op jit(solution)/shard_map/other_part/pallas_call | solution.py:418
  (44 shorter events, 8.3 us)
Async XLA Ops:
  1.7 18.8 %collective-permute-start.1 = (bf16[2048,128]{1,0:T(8,128)(2,1)S(1)}, bf16[2048,128]{1,0:T(8,128)(2,1)S(1)}, u32[]{:S(2)}, u32[]{:S(2)}) collective-permute-start(bf16[2048,128]{1,0:T(8,128)(2,1)S(1)} %pad_maximum_fusion.refs_0_), channel_id=1, source_target_pairs={{0,2},{1,3},{2,0},{3,1},{4,6},{5,7},{6,4},{7,5}} | collective-permute-start | bytes 1572872 | tf_op jit(solution)/shard_map/ppermute | solution.py:457
  5.0 17.0 %collective-permute-start = (bf16[2048,128]{1,0:T(8,128)(2,1)S(1)}, bf16[2048,128]{1,0:T(8,128)(2,1)S(1)}, u32[]{:S(2)}, u32[]{:S(2)}) collective-permute-start(bf16[2048,128]{1,0:T(8,128)(2,1)S(1)} %pad_maximum_fusion.refs_0_), channel_id=1, source_target_pairs={{0,1},{1,0},{2,3},{3,2},{4,5},{5,4},{6,7},{7,6}} | collective-permute-start | bytes 1572872 | tf_op jit(solution)/shard_map/ppermute | solution.py:457
  18.3 31.1 %collective-permute-start.5 = (bf16[2048,128]{1,0:T(8,128)(2,1)S(1)}, bf16[2048,128]{1,0:T(8,128)(2,1)S(1)}, u32[]{:S(2)}, u32[]{:S(2)}) collective-permute-start(bf16[2048,128]{1,0:T(8,128)(2,1)S(1)} %bitcast.8), channel_id=1, source_target_pairs={{0,3},{1,0},{2,1},{3,2},{4,7},{5,4},{6,5},{7,6}} | collective-permute-start | bytes 1572872 | tf_op jit(solution)/shard_map/ppermute | solution.py:466
  18.5 31.3 %collective-permute-start.4 = (bf16[2048,128]{1,0:T(8,128)(2,1)S(1)}, bf16[2048,128]{1,0:T(8,128)(2,1)S(1)}, u32[]{:S(2)}, u32[]{:S(2)}) collective-permute-start(bf16[2048,128]{1,0:T(8,128)(2,1)S(1)} %bitcast.9), channel_id=1, source_target_pairs={{0,2},{1,3},{2,0},{3,1},{4,6},{5,7},{6,4},{7,5}} | collective-permute-start | bytes 1572872 | tf_op jit(solution)/shard_map/ppermute | solution.py:466
  20.5 30.8 %collective-permute-start.3 = (bf16[2048,128]{1,0:T(8,128)(2,1)S(1)}, bf16[2048,128]{1,0:T(8,128)(2,1)}, u32[]{:S(2)}, u32[]{:S(2)}) collective-permute-start(bf16[2048,128]{1,0:T(8,128)(2,1)S(1)} %bitcast.10), channel_id=1, source_target_pairs={{0,1},{1,2},{2,3},{3,0},{4,5},{5,6},{6,7},{7,4}} | collective-permute-start | bytes 1572872 | tf_op jit(solution)/shard_map/ppermute | solution.py:466
  20.5 77.6 %collective-permute-start.14 = (bf16[384,4096]{1,0:T(8,128)(2,1)}, bf16[384,4096]{1,0:T(8,128)(2,1)}, u32[]{:S(2)}, u32[]{:S(2)}) collective-permute-start(bf16[384,4096]{1,0:T(8,128)(2,1)} %get-tuple-element.41), channel_id=1, source_target_pairs={{0,4},{4,0},{1,5},{5,1},{2,6},{6,2},{3,7},{7,3}} | collective-permute-start | bytes 9437192 | tf_op jit(solution)/shard_map/ppermute | solution.py:463
  22.0 29.3 %collective-permute-start.2 = (bf16[2048,128]{1,0:T(8,128)(2,1)S(1)}, bf16[2048,128]{1,0:T(8,128)(2,1)}, u32[]{:S(2)}, u32[]{:S(2)}) collective-permute-start(bf16[2048,128]{1,0:T(8,128)(2,1)S(1)} %collective-permute-done.1.refs_2_), channel_id=1, source_target_pairs={{0,1},{1,0},{2,3},{3,2},{4,5},{5,4},{6,7},{7,6}} | collective-permute-start | bytes 1572872 | tf_op jit(solution)/shard_map/ppermute | solution.py:464
  48.0 5.9 %copy-start.2 = (bf16[1024,2048]{1,0:T(8,128)(2,1)S(1)}, bf16[1024,2048]{1,0:T(8,128)(2,1)}, u32[]{:S(2)}) copy-start(bf16[1024,2048]{1,0:T(8,128)(2,1)} %copy-done.1) | copy-start | bytes 12582916
  49.4 121.6 %collective-permute-start.13 = (bf16[128,4096]{1,0:T(8,128)(2,1)S(1)}, bf16[128,4096]{1,0:T(8,128)(2,1)S(1)}, u32[]{:S(2)}, u32[]{:S(2)}) collective-permute-start(bf16[128,4096]{1,0:T(8,128)(2,1)S(1)} %constant_dynamic-slice_fusion), channel_id=1, source_target_pairs={{0,4},{4,0},{1,5},{5,1},{2,6},{6,2},{3,7},{7,3}} | collective-permute-start | bytes 3145736 | tf_op jit(solution)/shard_map/ppermute | solution.py:459
  49.8 29.9 %collective-permute-start.6 = (bf16[1024,384]{1,0:T(8,128)(2,1)}, bf16[1024,384]{1,0:T(8,128)(2,1)S(1)}, u32[]{:S(2)}, u32[]{:S(2)}) collective-permute-start(bf16[1024,384]{1,0:T(8,128)(2,1)} %copy-done), channel_id=1, source_target_pairs={{3,0},{2,1},{7,4},{6,5}} | collective-permute-start | bytes 2359304 | tf_op jit(solution)/shard_map/ppermute | solution.py:468
  89.9 81.9 %collective-permute-start.7 = (bf16[1024,128]{1,0:T(8,128)(2,1)S(1)}, bf16[1024,128]{1,0:T(8,128)(2,1)S(1)}, u32[]{:S(2)}, u32[]{:S(2)}) collective-permute-start(bf16[1024,128]{1,0:T(8,128)(2,1)S(1)} %attention.6), channel_id=1, source_target_pairs={{0,3},{1,2},{4,7},{5,6}} | collective-permute-start | bytes 786440 | tf_op jit(solution)/shard_map/ppermute | solution.py:494
  98.0 111.6 %collective-permute-start.18 = (bf16[384,4096]{1,0:T(8,128)(2,1)}, bf16[384,4096]{1,0:T(8,128)(2,1)S(1)}, u32[]{:S(2)}, u32[]{:S(2)}) collective-permute-start(bf16[384,4096]{1,0:T(8,128)(2,1)} %collective-permute-done.14.rest_5_), channel_id=1, source_target_pairs={{0,2},{1,3},{2,0},{3,1},{4,6},{5,7},{6,4},{7,5}} | collective-permute-start | bytes 9437192 | tf_op jit(solution)/shard_map/ppermute | solution.py:485
  150.1 23.9 %collective-permute-start.8 = (bf16[1024,256]{1,0:T(8,128)(2,1)S(1)}, bf16[1024,256]{1,0:T(8,128)(2,1)S(1)}, u32[]{:S(2)}, u32[]{:S(2)}) collective-permute-start(bf16[1024,256]{1,0:T(8,128)(2,1)S(1)} %get-tuple-element.39), channel_id=1, source_target_pairs={{0,3},{4,7}} | collective-permute-start | bytes 1572872 | tf_op jit(solution)/shard_map/ppermute | solution.py:498
  151.4 102.7 %slice-start = ((s8[8388608]{0:T(1024)(128)(4,1)}), s8[4194304]{0:T(1024)(128)(4,1)S(1)}, s32[]{:S(2)}) async-start(s8[8388608]{0:T(1024)(128)(4,1)} %bitcast.6), calls=%async_computation | async-start | bytes 8388608
  171.0 83.1 %slice-start.1 = ((s8[8388608]{0:T(1024)(128)(4,1)}), s8[4194304]{0:T(1024)(128)(4,1)S(1)}, s32[]{:S(2)}) async-start(s8[8388608]{0:T(1024)(128)(4,1)} %bitcast.6), calls=%async_computation.1 | async-start | bytes 8388608
  171.1 40.6 %collective-permute-start.17 = (bf16[128,4096]{1,0:T(8,128)(2,1)S(1)}, bf16[128,4096]{1,0:T(8,128)(2,1)S(1)}, u32[]{:S(2)}, u32[]{:S(2)}) collective-permute-start(bf16[128,4096]{1,0:T(8,128)(2,1)S(1)} %collective-permute-done.13.rest_4_), channel_id=1, source_target_pairs={{0,2},{1,3},{2,0},{3,1},{4,6},{5,7},{6,4},{7,5}} | collective-permute-start | bytes 3145736 | tf_op jit(solution)/shard_map/ppermute | solution.py:485
  199.9 104.9 %collective-permute-start.16 = (bf16[384,4096]{1,0:T(8,128)(2,1)}, bf16[384,4096]{1,0:T(8,128)(2,1)S(1)}, u32[]{:S(2)}, u32[]{:S(2)}) collective-permute-start(bf16[384,4096]{1,0:T(8,128)(2,1)} %collective-permute-done.14.rest_5_), channel_id=1, source_target_pairs={{0,1},{1,0},{2,3},{3,2},{4,5},{5,4},{6,7},{7,6}} | collective-permute-start | bytes 9437192 | tf_op jit(solution)/shard_map/ppermute | solution.py:486
  209.6 95.2 %collective-permute-start.20 = (bf16[384,4096]{1,0:T(8,128)(2,1)S(1)}, bf16[384,4096]{1,0:T(8,128)(2,1)S(1)}, u32[]{:S(2)}, u32[]{:S(2)}) collective-permute-start(bf16[384,4096]{1,0:T(8,128)(2,1)S(1)} %collective-permute-done.18.rest_9_), channel_id=1, source_target_pairs={{0,1},{1,0},{2,3},{3,2},{4,5},{5,4},{6,7},{7,6}} | collective-permute-start | bytes 9437192 | tf_op jit(solution)/shard_map/ppermute | solution.py:489
  209.7 44.1 %collective-permute-start.9 = (bf16[1024,512]{1,0:T(8,128)(2,1)S(1)}, bf16[1024,512]{1,0:T(8,128)(2,1)S(1)}, u32[]{:S(2)}, u32[]{:S(2)}) collective-permute-start(bf16[1024,512]{1,0:T(8,128)(2,1)S(1)} %attention.5.rest_0_), channel_id=1, source_target_pairs={{0,4},{4,0},{1,5},{5,1},{2,6},{6,2},{3,7},{7,3}} | collective-permute-start | bytes 3145736 | tf_op jit(solution)/shard_map/ppermute | solution.py:481
  211.4 42.7 %collective-permute-start.15 = (bf16[128,4096]{1,0:T(8,128)(2,1)S(1)}, bf16[128,4096]{1,0:T(8,128)(2,1)S(1)}, u32[]{:S(2)}, u32[]{:S(2)}) collective-permute-start(bf16[128,4096]{1,0:T(8,128)(2,1)S(1)} %collective-permute-done.13.rest_4_), channel_id=1, source_target_pairs={{0,1},{1,0},{2,3},{3,2},{4,5},{5,4},{6,7},{7,6}} | collective-permute-start | bytes 3145736 | tf_op jit(solution)/shard_map/ppermute | solution.py:486
  211.6 40.5 %collective-permute-start.11 = (bf16[1024,384]{1,0:T(8,128)(2,1)S(1)}, bf16[1024,384]{1,0:T(8,128)(2,1)S(1)}, u32[]{:S(2)}, u32[]{:S(2)}) collective-permute-start(bf16[1024,384]{1,0:T(8,128)(2,1)S(1)} %attention.8.rest_2_), channel_id=1, source_target_pairs={{0,4},{4,0},{1,5},{5,1},{2,6},{6,2},{3,7},{7,3}} | collective-permute-start | bytes 2359304 | tf_op jit(solution)/shard_map/ppermute | solution.py:481
  252.1 31.6 %collective-permute-start.10 = (bf16[1024,640]{1,0:T(8,128)(2,1)S(1)}, bf16[1024,640]{1,0:T(8,128)(2,1)S(1)}, u32[]{:S(2)}, u32[]{:S(2)}) collective-permute-start(bf16[1024,640]{1,0:T(8,128)(2,1)S(1)} %get-tuple-element.36.rest_1_), channel_id=1, source_target_pairs={{0,4},{4,0},{1,5},{5,1},{2,6},{6,2},{3,7},{7,3}} | collective-permute-start | bytes 3932168 | tf_op jit(solution)/shard_map/ppermute | solution.py:481
  253.8 51.0 %collective-permute-start.12 = (bf16[1024,512]{1,0:T(8,128)(2,1)S(1)}, bf16[1024,512]{1,0:T(8,128)(2,1)S(1)}, u32[]{:S(2)}, u32[]{:S(2)}) collective-permute-start(bf16[1024,512]{1,0:T(8,128)(2,1)S(1)} %attention.9.rest_3_), channel_id=1, source_target_pairs={{0,4},{4,0},{1,5},{5,1},{2,6},{6,2},{3,7},{7,3}} | collective-permute-start | bytes 3145736 | tf_op jit(solution)/shard_map/ppermute | solution.py:481
  254.1 50.7 %collective-permute-start.19 = (bf16[128,4096]{1,0:T(8,128)(2,1)S(1)}, bf16[128,4096]{1,0:T(8,128)(2,1)S(1)}, u32[]{:S(2)}, u32[]{:S(2)}) collective-permute-start(bf16[128,4096]{1,0:T(8,128)(2,1)S(1)} %collective-permute-done.17.rest_8_), channel_id=1, source_target_pairs={{0,1},{1,0},{2,3},{3,2},{4,5},{5,4},{6,7},{7,6}} | collective-permute-start | bytes 3145736 | tf_op jit(solution)/shard_map/ppermute | solution.py:489
  (2 other events, 2.9 us)

commit v4 on v3

--- a/solution.py
+++ b/solution.py
@@ -269,13 +269,20 @@
         stage(full, (pl.multiple_of(own - 2 * rows, rows), full), (q_ref, own, upper), diagonal=True)
         stage(upper, (pl.multiple_of(own - rows, rows), full), (qn_ref, 0, full))
         stage(pv=(own, upper))
+        outs = []
         for w in range(strips):
             cs = pl.ds(w * STRIP, STRIP)
-            o = (acc_ref[:, cs] / l_ref[:, cs].sum(axis=0, keepdims=True)).astype(BF).T
-            for out, mine in [(out, slot < far) for out in far_outs] + [(out, slot >= far) for out in own_outs]:
-                @pl.when(mine)
-                def _(out=out, o=o, cs=cs):
-                    out[cs, :] = o
+            outs.append((acc_ref[:, cs] / l_ref[:, cs].sum(axis=0, keepdims=True)).astype(BF).T)
+
+        def write(out):
+            for w in range(strips):
+                out[pl.ds(w * STRIP, STRIP), :] = outs[w]
+
+        if far and slots:
+            pl.when(slot < far)(functools.partial(write, far_outs[0]))
+            pl.when(slot >= far)(functools.partial(write, own_outs[0]))
+        else:
+            write((far_outs + own_outs)[0])
 
     for i, back_ref in enumerate(back_refs):
         @pl.when((owner < 0) & ((slot == pl.num_programs(0) - 1) == (i == 0)))
@@ -433,7 +440,7 @@
     )(cp, y, *o_parts, *w_parts)
 
 
-SIZES = (4, 5, 3, 4)
+SIZES = (5, 4, 3, 4)
 PIECE_ROWS = (128, 384)
 PIECES = len(PIECE_ROWS)
 

time: 328 us -> 354 us (1.079)
  waiting for transfers between devices: 70.6 us -> 105 us
  starting transfers between devices: 33.3 us -> 28.6 us
  Pallas kernels: 215 us -> 211 us
    ppermute x1, waiting for transfers between devices: 2.14 us -> 29.3 us  [local_step(): back1 = lax.ppermute(far, 'cp', [(0, 3)])]
    ppermute x2, starting transfers between devices: 9.89 us -> 0.07 us  [spread(): w_core[i] = lax.ppermute(w_peer[i], 'cp', flip(1))]
    ppermute x1, waiting for transfers between devices: 0.01 us -> 6.92 us  [local_step(): w_peer = [lax.ppermute(mine, 'tp', swap)]]
    pallas_call x5, Pallas kernels: 134 us -> 130 us  [attention(): pl.pallas_call(functools.partial(attn_kernel, old=keys // 2, slots=slots,...]
  transfers between devices with their start and end apart: 21 -> 21, of which waited for: 4 -> 5; matrix products, arithmetic and copies ran while one was open for 1% -> 1% of each run, Pallas kernels for 59% -> 53%
where the time goes in v4:
time: 354 us
  Pallas kernels  211 us (60%)
  waiting for transfers between devices  105 us (30%)
  starting transfers between devices  28.6 us (8%)
  local copies, waits for them, and re-layouts  6.92 us (2%)
    pallas_call x5, Pallas kernels, attention(): pl.pallas_call(functools.partial(attn_kernel, old=keys // 2, slots=slots,...  130 us
    ppermute x4, waiting for transfers between devices, heads(): o_other.append(lax.ppermute(outs[-1], 'tp', swap))  68.9 us
    ppermute x1, waiting for transfers between devices, local_step(): back1 = lax.ppermute(far, 'cp', [(0, 3)])  29.3 us
    pallas_call x1, Pallas kernels, other_part(): pl.pallas_call(functools.partial(other_kernel, parts=len(o_parts)), grid_...  22.8 us
    pallas_call x1, Pallas kernels, q_proj(): pl.pallas_call(q_kernel, grid=(width // block,), in_specs=[pl.BlockSpec((...  22.7 us
    pallas_call x1, Pallas kernels, own_part(): pl.pallas_call(own_kernel, grid=(d // block,), in_specs=[pl.BlockSpec((ro...  22.5 us
    ppermute x1, starting transfers between devices, local_step(): back0 = lax.ppermute(far, 'cp', [(0, 3), (1, 2)])  11.5 us
    pallas_call x1, Pallas kernels, norm_kv(): pl.pallas_call(norm_kv_kernel, grid_spec=pltpu.PrefetchScalarGridSpec(num...  10.7 us
  transfers between devices with their start and end apart: 21, of which 5 were waited for; matrix products, arithmetic and copies ran while one was open for 1% of the time, Pallas kernels for 53%

profile of v4, /device:TPU:0, one launch (start us, length us, event | category | flops | bytes accessed | tf_op | source)
XLA Modules:
  0.0 353.8 jit_solution(1768708575881855989)
XLA Ops:
  1.7 3.3 collective-permute-start.1
  7.6 10.7 %norm_kv.1 = (bf16[1024,4096]{1,0:T(8,128)(2,1)S(1)}, bf16[2,1024,128]{2,1,0:T(8,128)(2,1)S(1)}, bf16[1024,128]{1,0:T(8,128)(2,1)}, bf16[1024,128]{1,0:T(8,128)(...) custom-call(s32[1]{0:T(128)} %bitcast.cp_ref, bf16[1024,4096]{1,0:T(8,128)(2,1)} %x_ref.3, ...), custom_call_target="tpu_custom_call" | custom-call | flops 2147483648 | bytes 16777216 | tf_op jit(solution)/shard_map/norm_kv/pallas_call | solution.py:66
  18.5 2.0 collective-permute-start.4
  20.5 1.5 collective-permute-start.14
  22.3 22.7 %q_proj.1 = (bf16[1024,2048]{1,0:T(8,128)(2,1)S(1)}, bf16[1024,384]{1,0:T(8,128)(2,1)S(1)}) custom-call(bf16[1024,4096]{1,0:T(8,128)(2,1)S(1)} %get-tuple-element.25.h_ref, bf16[4096,2304]{1,0:T(8,128)(2,1)} %w_ref.3, bf16[1,2304]{1,0:T(2,128)(2,1)S(1)} %broadcast_in_dim.17.b_ref, f32[1024,128]{1,0:T(8,128)S(1)} %get-tuple-element.26.cos_ref, ...), custom_call_target="tpu_custom_call" | custom-call | flops 17179869184 | bytes 16777216 | tf_op jit(solution)/shard_map/q_proj/pallas_call | solution.py:120
  46.0 2.0 copy-done.1
  49.8 1.5 collective-permute-start.6
  51.3 2.6 gather.1
  53.9 31.0 %attention.5.rest_0_ = bf16[1024,640]{1,0:T(8,128)(2,1)S(1)} custom-call(s32[1]{0:T(128)} %bitcast.cp_ref, bf16[1024,2048]{1,0:T(8,128)(2,1)S(1)} %copy-done.2, bf16[1024,2048]{1,0:T(8,128)(2,1)S(1)} %copy-done.2, bf16[8192,128]{1,0:T(8,128)(2,1)S(1)} %get-tuple-element.31.refs_2_.refs_4_, bf16[64,128,128]{2,1,0:T(8,128)(2,1)S(1)} %get-tuple-element.32.refs_3_.refs_5_), custom_call_target="tpu_custom_call" | custom-call | flops 21474836480 | bytes 2621440 | tf_op jit(solution)/shard_map/attention/pallas_call | solution.py:324
  84.9 10.3 %attention.6 = bf16[1024,128]{1,0:T(8,128)(2,1)S(1)} custom-call(s32[1]{0:T(128)} %bitcast.cp_ref, bf16[1024,384]{1,0:T(8,128)(2,1)S(1)} %collective-permute-done.6.refs_0_.refs_1_, bf16[1024,384]{1,0:T(8,128)(2,1)S(1)} %collective-permute-done.6.refs_0_.refs_1_, bf16[8192,128]{1,0:T(8,128)(2,1)S(1)} %get-tuple-element.31.refs_2_.refs_4_, ...), custom_call_target="tpu_custom_call" | custom-call | flops 4294967296 | bytes 524288 | tf_op jit(solution)/shard_map/attention/pallas_call | solution.py:324
  95.1 11.5 %collective-permute-start.7 = (bf16[1024,128]{1,0:T(8,128)(2,1)S(1)}, bf16[1024,128]{1,0:T(8,128)(2,1)S(1)}, u32[]{:S(2)}, u32[]{:S(2)}) collective-permute-start(bf16[1024,128]{1,0:T(8,128)(2,1)S(1)} %attention.6), channel_id=1, source_target_pairs={{0,3},{1,2},{4,7},{5,6}} | collective-permute-start | bytes 786440 | tf_op jit(solution)/shard_map/ppermute | solution.py:501
  106.6 6.9 %collective-permute-done.13.rest_4_ = bf16[128,4096]{1,0:T(8,128)(2,1)S(1)} collective-permute-done((bf16[128,4096]{1,0:T(8,128)(2,1)S(1)}, bf16[128,4096]{1,0:T(8,128)(2,1)S(1)}, u32[]{:S(2)}, u32[]{:S(2)}) %collective-permute-start.13) | collective-permute-done | bytes 1048608 | tf_op jit(solution)/shard_map/ppermute | solution.py:466
  113.6 2.0 collective-permute-start.18
  115.6 44.4 %attention.7 = (bf16[1024,256]{1,0:T(8,128)(2,1)S(1)}, bf16[1024,512]{1,0:T(8,128)(2,1)S(1)}) custom-call(s32[1]{0:T(128)} %bitcast.cp_ref, bf16[1024,384]{1,0:T(8,128)(2,1)S(1)} %collective-permute-done.6.refs_0_.refs_1_, bf16[1024,384]{1,0:T(8,128)(2,1)S(1)} %collective-permute-done.6.refs_0_.refs_1_, bf16[1024,2048]{1,0:T(8,128)(2,1)S(1)} %copy-done.2, ...), custom_call_target="tpu_custom_call" | custom-call | flops 25769803776 | bytes 3145728 | tf_op jit(solution)/shard_map/attention/pallas_call | solution.py:324
  161.3 19.0 %attention.8.rest_2_ = bf16[1024,384]{1,0:T(8,128)(2,1)S(1)} custom-call(s32[1]{0:T(128)} %bitcast.cp_ref, bf16[1024,2048]{1,0:T(8,128)(2,1)S(1)} %copy-done.2, bf16[1024,2048]{1,0:T(8,128)(2,1)S(1)} %copy-done.2, bf16[8192,128]{1,0:T(8,128)(2,1)S(1)} %get-tuple-element.31.refs_2_.refs_4_, bf16[64,128,128]{2,1,0:T(8,128)(2,1)S(1)} %get-tuple-element.32.refs_3_.refs_5_), custom_call_target="tpu_custom_call" | custom-call | flops 12884901888 | bytes 1572864 | tf_op jit(solution)/shard_map/attention/pallas_call | solution.py:324
  180.4 29.3 %collective-permute-done.8.refs_5_ = bf16[1024,256]{1,0:T(8,128)(2,1)S(1)} collective-permute-done((bf16[1024,256]{1,0:T(8,128)(2,1)S(1)}, bf16[1024,256]{1,0:T(8,128)(2,1)S(1)}, u32[]{:S(2)}, u32[]{:S(2)}) %collective-permute-start.8) | collective-permute-done | bytes 524320 | tf_op jit(solution)/shard_map/ppermute | solution.py:505
  209.7 25.2 %attention.9.rest_3_ = bf16[1024,512]{1,0:T(8,128)(2,1)S(1)} custom-call(s32[1]{0:T(128)} %bitcast.cp_ref, bf16[1024,2048]{1,0:T(8,128)(2,1)S(1)} %copy-done.2, bf16[1024,2048]{1,0:T(8,128)(2,1)S(1)} %copy-done.2, bf16[8192,128]{1,0:T(8,128)(2,1)S(1)} %get-tuple-element.31.refs_2_.refs_4_, bf16[64,128,128]{2,1,0:T(8,128)(2,1)S(1)} %get-tuple-element.32.refs_3_.refs_5_, ...), custom_call_target="tpu_custom_call" | custom-call | flops 17179869184 | bytes 2097152 | tf_op jit(solution)/shard_map/attention/pallas_call | solution.py:324
  235.4 1.9 collective-permute-start.10
  237.5 40.5 %collective-permute-done.11.rest_2_ = bf16[1024,384]{1,0:T(8,128)(2,1)S(1)} collective-permute-done((bf16[1024,384]{1,0:T(8,128)(2,1)S(1)}, bf16[1024,384]{1,0:T(8,128)(2,1)S(1)}, u32[]{:S(2)}, u32[]{:S(2)}) %collective-permute-start.11) | collective-permute-done | bytes 786464 | tf_op jit(solution)/shard_map/ppermute | solution.py:488
  278.0 1.7 collective-permute-start.9
  280.1 22.5 %own_part.1.y_ref = f32[1024,4096]{1,0:T(8,128)} custom-call(bf16[1024,4096]{1,0:T(8,128)(2,1)S(1)} %bitcast.7, bf16[1024,640]{1,0:T(8,128)(2,1)S(1)} %attention.5.rest_0_, bf16[1024,512]{1,0:T(8,128)(2,1)S(1)} %get-tuple-element.36.rest_1_, bf16[1024,384]{1,0:T(8,128)(2,1)S(1)} %attention.8.rest_2_, bf16[1024,512]{1,0:T(8,128)(2,1)S(1)} %attention.9.rest_3_, ...), custom_call_target="tpu_custom_call" | custom-call | flops 17179869184 | bytes 25165824 | tf_op jit(solution)/shard_map/own_part/pallas_call | solution.py:384
  302.6 7.0 %collective-permute-done.9.rest_0_ = bf16[1024,640]{1,0:T(8,128)(2,1)S(1)} collective-permute-done((bf16[1024,640]{1,0:T(8,128)(2,1)S(1)}, bf16[1024,640]{1,0:T(8,128)(2,1)S(1)}, u32[]{:S(2)}, u32[]{:S(2)}) %collective-permute-start.9) | collective-permute-done | bytes 1310752 | tf_op jit(solution)/shard_map/ppermute | solution.py:488
  309.7 21.3 %collective-permute-done.12.rest_3_ = bf16[1024,512]{1,0:T(8,128)(2,1)S(1)} collective-permute-done((bf16[1024,512]{1,0:T(8,128)(2,1)S(1)}, bf16[1024,512]{1,0:T(8,128)(2,1)S(1)}, u32[]{:S(2)}, u32[]{:S(2)}) %collective-permute-start.12) | collective-permute-done | bytes 1048608 | tf_op jit(solution)/shard_map/ppermute | solution.py:488
  331.0 22.8 %other_part.1 = bf16[1024,4096]{1,0:T(8,128)(2,1)} custom-call(s32[1]{0:T(128)} %bitcast.cp_ref, f32[1024,4096]{1,0:T(8,128)} %own_part.1.y_ref, bf16[1024,640]{1,0:T(8,128)(2,1)S(1)} %collective-permute-done.9.rest_0_, bf16[1024,512]{1,0:T(8,128)(2,1)S(1)} %collective-permute-done.10.rest_1_, bf16[1024,384]{1,0:T(8,128)(2,1)S(1)} %collective-permute-done.11.rest_2_, ...), custom_call_target="tpu_custom_call" | custom-call | flops 17179869184 | bytes 25165824 | tf_op jit(solution)/shard_map/other_part/pallas_call | solution.py:425
  (44 shorter events, 9.1 us)
Async XLA Ops:
  1.7 18.8 %collective-permute-start.1 = (bf16[2048,128]{1,0:T(8,128)(2,1)S(1)}, bf16[2048,128]{1,0:T(8,128)(2,1)S(1)}, u32[]{:S(2)}, u32[]{:S(2)}) collective-permute-start(bf16[2048,128]{1,0:T(8,128)(2,1)S(1)} %pad_maximum_fusion.refs_0_), channel_id=1, source_target_pairs={{0,2},{1,3},{2,0},{3,1},{4,6},{5,7},{6,4},{7,5}} | collective-permute-start | bytes 1572872 | tf_op jit(solution)/shard_map/ppermute | solution.py:464
  5.0 17.0 %collective-permute-start = (bf16[2048,128]{1,0:T(8,128)(2,1)S(1)}, bf16[2048,128]{1,0:T(8,128)(2,1)S(1)}, u32[]{:S(2)}, u32[]{:S(2)}) collective-permute-start(bf16[2048,128]{1,0:T(8,128)(2,1)S(1)} %pad_maximum_fusion.refs_0_), channel_id=1, source_target_pairs={{0,1},{1,0},{2,3},{3,2},{4,5},{5,4},{6,7},{7,6}} | collective-permute-start | bytes 1572872 | tf_op jit(solution)/shard_map/ppermute | solution.py:464
  18.3 31.1 %collective-permute-start.5 = (bf16[2048,128]{1,0:T(8,128)(2,1)S(1)}, bf16[2048,128]{1,0:T(8,128)(2,1)S(1)}, u32[]{:S(2)}, u32[]{:S(2)}) collective-permute-start(bf16[2048,128]{1,0:T(8,128)(2,1)S(1)} %bitcast.8), channel_id=1, source_target_pairs={{0,3},{1,0},{2,1},{3,2},{4,7},{5,4},{6,5},{7,6}} | collective-permute-start | bytes 1572872 | tf_op jit(solution)/shard_map/ppermute | solution.py:473
  18.5 31.3 %collective-permute-start.4 = (bf16[2048,128]{1,0:T(8,128)(2,1)S(1)}, bf16[2048,128]{1,0:T(8,128)(2,1)S(1)}, u32[]{:S(2)}, u32[]{:S(2)}) collective-permute-start(bf16[2048,128]{1,0:T(8,128)(2,1)S(1)} %bitcast.9), channel_id=1, source_target_pairs={{0,2},{1,3},{2,0},{3,1},{4,6},{5,7},{6,4},{7,5}} | collective-permute-start | bytes 1572872 | tf_op jit(solution)/shard_map/ppermute | solution.py:473
  20.5 30.8 %collective-permute-start.3 = (bf16[2048,128]{1,0:T(8,128)(2,1)S(1)}, bf16[2048,128]{1,0:T(8,128)(2,1)}, u32[]{:S(2)}, u32[]{:S(2)}) collective-permute-start(bf16[2048,128]{1,0:T(8,128)(2,1)S(1)} %bitcast.10), channel_id=1, source_target_pairs={{0,1},{1,2},{2,3},{3,0},{4,5},{5,6},{6,7},{7,4}} | collective-permute-start | bytes 1572872 | tf_op jit(solution)/shard_map/ppermute | solution.py:473
  20.5 93.1 %collective-permute-start.14 = (bf16[384,4096]{1,0:T(8,128)(2,1)}, bf16[384,4096]{1,0:T(8,128)(2,1)}, u32[]{:S(2)}, u32[]{:S(2)}) collective-permute-start(bf16[384,4096]{1,0:T(8,128)(2,1)} %get-tuple-element.41), channel_id=1, source_target_pairs={{0,4},{4,0},{1,5},{5,1},{2,6},{6,2},{3,7},{7,3}} | collective-permute-start | bytes 9437192 | tf_op jit(solution)/shard_map/ppermute | solution.py:470
  22.0 29.3 %collective-permute-start.2 = (bf16[2048,128]{1,0:T(8,128)(2,1)S(1)}, bf16[2048,128]{1,0:T(8,128)(2,1)}, u32[]{:S(2)}, u32[]{:S(2)}) collective-permute-start(bf16[2048,128]{1,0:T(8,128)(2,1)S(1)} %collective-permute-done.1.refs_2_), channel_id=1, source_target_pairs={{0,1},{1,0},{2,3},{3,2},{4,5},{5,4},{6,7},{7,6}} | collective-permute-start | bytes 1572872 | tf_op jit(solution)/shard_map/ppermute | solution.py:471
  48.0 5.9 %copy-start.2 = (bf16[1024,2048]{1,0:T(8,128)(2,1)S(1)}, bf16[1024,2048]{1,0:T(8,128)(2,1)}, u32[]{:S(2)}) copy-start(bf16[1024,2048]{1,0:T(8,128)(2,1)} %copy-done.1) | copy-start | bytes 12582916
  49.4 64.1 %collective-permute-start.13 = (bf16[128,4096]{1,0:T(8,128)(2,1)S(1)}, bf16[128,4096]{1,0:T(8,128)(2,1)S(1)}, u32[]{:S(2)}, u32[]{:S(2)}) collective-permute-start(bf16[128,4096]{1,0:T(8,128)(2,1)S(1)} %constant_dynamic-slice_fusion), channel_id=1, source_target_pairs={{0,4},{4,0},{1,5},{5,1},{2,6},{6,2},{3,7},{7,3}} | collective-permute-start | bytes 3145736 | tf_op jit(solution)/shard_map/ppermute | solution.py:466
  49.8 35.1 %collective-permute-start.6 = (bf16[1024,384]{1,0:T(8,128)(2,1)}, bf16[1024,384]{1,0:T(8,128)(2,1)S(1)}, u32[]{:S(2)}, u32[]{:S(2)}) collective-permute-start(bf16[1024,384]{1,0:T(8,128)(2,1)} %copy-done), channel_id=1, source_target_pairs={{3,0},{2,1},{7,4},{6,5}} | collective-permute-start | bytes 2359304 | tf_op jit(solution)/shard_map/ppermute | solution.py:475
  95.1 85.2 %collective-permute-start.7 = (bf16[1024,128]{1,0:T(8,128)(2,1)S(1)}, bf16[1024,128]{1,0:T(8,128)(2,1)S(1)}, u32[]{:S(2)}, u32[]{:S(2)}) collective-permute-start(bf16[1024,128]{1,0:T(8,128)(2,1)S(1)} %attention.6), channel_id=1, source_target_pairs={{0,3},{1,2},{4,7},{5,6}} | collective-permute-start | bytes 786440 | tf_op jit(solution)/shard_map/ppermute | solution.py:501
  113.6 123.8 %collective-permute-start.17 = (bf16[128,4096]{1,0:T(8,128)(2,1)S(1)}, bf16[128,4096]{1,0:T(8,128)(2,1)S(1)}, u32[]{:S(2)}, u32[]{:S(2)}) collective-permute-start(bf16[128,4096]{1,0:T(8,128)(2,1)S(1)} %collective-permute-done.13.rest_4_), channel_id=1, source_target_pairs={{0,2},{1,3},{2,0},{3,1},{4,6},{5,7},{6,4},{7,5}} | collective-permute-start | bytes 3145736 | tf_op jit(solution)/shard_map/ppermute | solution.py:492
  113.6 121.3 %collective-permute-start.18 = (bf16[384,4096]{1,0:T(8,128)(2,1)}, bf16[384,4096]{1,0:T(8,128)(2,1)S(1)}, u32[]{:S(2)}, u32[]{:S(2)}) collective-permute-start(bf16[384,4096]{1,0:T(8,128)(2,1)} %collective-permute-done.14.rest_5_), channel_id=1, source_target_pairs={{0,2},{1,3},{2,0},{3,1},{4,6},{5,7},{6,4},{7,5}} | collective-permute-start | bytes 9437192 | tf_op jit(solution)/shard_map/ppermute | solution.py:492
  160.0 49.7 %collective-permute-start.8 = (bf16[1024,256]{1,0:T(8,128)(2,1)S(1)}, bf16[1024,256]{1,0:T(8,128)(2,1)S(1)}, u32[]{:S(2)}, u32[]{:S(2)}) collective-permute-start(bf16[1024,256]{1,0:T(8,128)(2,1)S(1)} %get-tuple-element.39), channel_id=1, source_target_pairs={{0,3},{4,7}} | collective-permute-start | bytes 1572872 | tf_op jit(solution)/shard_map/ppermute | solution.py:505
  161.3 118.7 %slice-start = ((s8[8388608]{0:T(1024)(128)(4,1)}), s8[4194304]{0:T(1024)(128)(4,1)S(1)}, s32[]{:S(2)}) async-start(s8[8388608]{0:T(1024)(128)(4,1)} %bitcast.6), calls=%async_computation | async-start | bytes 8388608
  180.3 99.7 %slice-start.1 = ((s8[8388608]{0:T(1024)(128)(4,1)}), s8[4194304]{0:T(1024)(128)(4,1)S(1)}, s32[]{:S(2)}) async-start(s8[8388608]{0:T(1024)(128)(4,1)} %bitcast.6), calls=%async_computation.1 | async-start | bytes 8388608
  234.9 96.1 %collective-permute-start.16 = (bf16[384,4096]{1,0:T(8,128)(2,1)}, bf16[384,4096]{1,0:T(8,128)(2,1)S(1)}, u32[]{:S(2)}, u32[]{:S(2)}) collective-permute-start(bf16[384,4096]{1,0:T(8,128)(2,1)} %collective-permute-done.14.rest_5_), channel_id=1, source_target_pairs={{0,1},{1,0},{2,3},{3,2},{4,5},{5,4},{6,7},{7,6}} | collective-permute-start | bytes 9437192 | tf_op jit(solution)/shard_map/ppermute | solution.py:493
  234.9 96.1 %collective-permute-start.20 = (bf16[384,4096]{1,0:T(8,128)(2,1)S(1)}, bf16[384,4096]{1,0:T(8,128)(2,1)S(1)}, u32[]{:S(2)}, u32[]{:S(2)}) collective-permute-start(bf16[384,4096]{1,0:T(8,128)(2,1)S(1)} %collective-permute-done.18.rest_9_), channel_id=1, source_target_pairs={{0,1},{1,0},{2,3},{3,2},{4,5},{5,4},{6,7},{7,6}} | collective-permute-start | bytes 9437192 | tf_op jit(solution)/shard_map/ppermute | solution.py:496
  235.4 44.4 %collective-permute-start.15 = (bf16[128,4096]{1,0:T(8,128)(2,1)S(1)}, bf16[128,4096]{1,0:T(8,128)(2,1)S(1)}, u32[]{:S(2)}, u32[]{:S(2)}) collective-permute-start(bf16[128,4096]{1,0:T(8,128)(2,1)S(1)} %collective-permute-done.13.rest_4_), channel_id=1, source_target_pairs={{0,1},{1,0},{2,3},{3,2},{4,5},{5,4},{6,7},{7,6}} | collective-permute-start | bytes 3145736 | tf_op jit(solution)/shard_map/ppermute | solution.py:493
  235.4 44.6 %collective-permute-start.10 = (bf16[1024,512]{1,0:T(8,128)(2,1)S(1)}, bf16[1024,512]{1,0:T(8,128)(2,1)S(1)}, u32[]{:S(2)}, u32[]{:S(2)}) collective-permute-start(bf16[1024,512]{1,0:T(8,128)(2,1)S(1)} %get-tuple-element.36.rest_1_), channel_id=1, source_target_pairs={{0,4},{4,0},{1,5},{5,1},{2,6},{6,2},{3,7},{7,3}} | collective-permute-start | bytes 3145736 | tf_op jit(solution)/shard_map/ppermute | solution.py:488
  237.4 40.6 %collective-permute-start.11 = (bf16[1024,384]{1,0:T(8,128)(2,1)S(1)}, bf16[1024,384]{1,0:T(8,128)(2,1)S(1)}, u32[]{:S(2)}, u32[]{:S(2)}) collective-permute-start(bf16[1024,384]{1,0:T(8,128)(2,1)S(1)} %attention.8.rest_2_), channel_id=1, source_target_pairs={{0,4},{4,0},{1,5},{5,1},{2,6},{6,2},{3,7},{7,3}} | collective-permute-start | bytes 2359304 | tf_op jit(solution)/shard_map/ppermute | solution.py:488
  278.0 31.6 %collective-permute-start.9 = (bf16[1024,640]{1,0:T(8,128)(2,1)S(1)}, bf16[1024,640]{1,0:T(8,128)(2,1)S(1)}, u32[]{:S(2)}, u32[]{:S(2)}) collective-permute-start(bf16[1024,640]{1,0:T(8,128)(2,1)S(1)} %attention.5.rest_0_), channel_id=1, source_target_pairs={{0,4},{4,0},{1,5},{5,1},{2,6},{6,2},{3,7},{7,3}} | collective-permute-start | bytes 3932168 | tf_op jit(solution)/shard_map/ppermute | solution.py:488
  279.8 51.2 %collective-permute-start.12 = (bf16[1024,512]{1,0:T(8,128)(2,1)S(1)}, bf16[1024,512]{1,0:T(8,128)(2,1)S(1)}, u32[]{:S(2)}, u32[]{:S(2)}) collective-permute-start(bf16[1024,512]{1,0:T(8,128)(2,1)S(1)} %attention.9.rest_3_), channel_id=1, source_target_pairs={{0,4},{4,0},{1,5},{5,1},{2,6},{6,2},{3,7},{7,3}} | collective-permute-start | bytes 3145736 | tf_op jit(solution)/shard_map/ppermute | solution.py:488
  280.0 50.9 %collective-permute-start.19 = (bf16[128,4096]{1,0:T(8,128)(2,1)S(1)}, bf16[128,4096]{1,0:T(8,128)(2,1)S(1)}, u32[]{:S(2)}, u32[]{:S(2)}) collective-permute-start(bf16[128,4096]{1,0:T(8,128)(2,1)S(1)} %collective-permute-done.17.rest_8_), channel_id=1, source_target_pairs={{0,1},{1,0},{2,3},{3,2},{4,5},{5,4},{6,7},{7,6}} | collective-permute-start | bytes 3145736 | tf_op jit(solution)/shard_map/ppermute | solution.py:496
  (2 other events, 2.9 us)

commit v5 on v4

--- a/solution.py
+++ b/solution.py
@@ -19,6 +19,7 @@
 NORM_VMEM = 36 * 2 ** 20
 Q_VMEM = 36 * 2 ** 20
 OUT_VMEM = 28 * 2 ** 20
+OTHER_VMEM = 58 * 2 ** 20
 
 
 def rotate(a, cos, sin):
@@ -60,8 +61,8 @@
     last = w_qkv.shape[1] // (2 * HEAD) - 1
     row = lambda i, c: (i, 0)
     skip, piece = PIECE_ROWS
-    pieces = piece // skip
-    copied = lambda i: jnp.minimum(i, pieces - 1)
+    part = piece // steps
+    quarter = skip + piece
     head_rows = pl.BlockSpec((block, HEAD), row)
     return pl.pallas_call(
         norm_kv_kernel,
@@ -74,7 +75,7 @@
                 pl.BlockSpec((d, 2 * HEAD), lambda i, c: (0, last)),
                 pl.BlockSpec((1, 2 * HEAD), lambda i, c: (0, last)),
                 pl.BlockSpec((block, table.shape[1]), row),
-                pl.BlockSpec((skip, w_out.shape[1]), lambda i, c: (c[0] * (pieces + 1) + 1 + copied(i), 0)),
+                pl.BlockSpec((pl.Element(part), pl.Element(w_out.shape[1])), lambda i, c: (pl.multiple_of(c[0] * quarter + skip + i * part, 16), 0)),
             ],
             out_specs=[
                 pl.BlockSpec((block, d), row),
@@ -83,7 +84,7 @@
                 head_rows,
                 head_rows,
                 head_rows,
-                pl.BlockSpec((skip, w_out.shape[1]), lambda i, c: (copied(i), 0)),
+                pl.BlockSpec((part, w_out.shape[1]), row),
             ],
         ),
         out_shape=[
@@ -248,8 +249,18 @@
 
     @pl.when(fresh & (owner >= 0))
     def _():
-        stage(qk=(q_ref, 0, full))
-        p_ref[...] = jnp.zeros_like(p_ref)
+        def strip(w, carry):
+            cs = pl.ds(pl.multiple_of(w * STRIP, STRIP), STRIP)
+            top = None
+            for u in range(chunks):
+                ks = pl.ds(u * CHUNK, CHUNK)
+                s = lax.dot_general(k_ref[ks, :], q_ref[cs, :], (((1,), (1,)), ((), ())), preferred_element_type=F32)
+                s_ref[ks, cs] = s
+                top = col_max(s) if top is None else jnp.maximum(top, col_max(s))
+            mx_ref[:, cs] = top
+            return carry
+
+        lax.fori_loop(0, strips, strip, 0)
         acc_ref[...] = jnp.zeros_like(acc_ref)
 
     @pl.when(owner >= 0)
@@ -257,15 +268,15 @@
         own = pl.multiple_of(old + rows * owner, rows)
         m_ref[...] = jnp.full_like(m_ref, NEG)
         l_ref[...] = jnp.zeros_like(l_ref)
-        al_ref[...] = jnp.zeros_like(al_ref)
+        stage(full, None, (q_ref, rows, full))
 
         def body(j, carry):
-            before = pl.multiple_of(jnp.maximum(j - 1, 0) * rows, rows)
+            before = pl.multiple_of((j - 1) * rows, rows)
             after = pl.multiple_of((j + 1) * rows, rows)
             stage(full, (before, full), (q_ref, after, full))
             return carry
 
-        lax.fori_loop(0, own // rows - 1, body, 0)
+        lax.fori_loop(1, own // rows - 1, body, 0)
         stage(full, (pl.multiple_of(own - 2 * rows, rows), full), (q_ref, own, upper), diagonal=True)
         stage(upper, (pl.multiple_of(own - rows, rows), full), (qn_ref, 0, full))
         stage(pv=(own, upper))
@@ -434,14 +445,14 @@
             scratch_shapes=[pltpu.VMEM((rows, depth), BF)],
         ),
         out_shape=jax.ShapeDtypeStruct((rows, d), BF),
-        compiler_params=pltpu.CompilerParams(dimension_semantics=("arbitrary",), vmem_limit_bytes=OUT_VMEM),
+        compiler_params=pltpu.CompilerParams(dimension_semantics=("arbitrary",), vmem_limit_bytes=OTHER_VMEM),
         cost_estimate=pl.CostEstimate(flops=2 * rows * d * depth, bytes_accessed=6 * rows * d, transcendentals=0),
         name="other_part",
     )(cp, y, *o_parts, *w_parts)
 
 
 SIZES = (5, 4, 3, 4)
-PIECE_ROWS = (128, 384)
+PIECE_ROWS = (192, 320)
 PIECES = len(PIECE_ROWS)
 
 

time: 354 us -> 313 us (0.88)
  waiting for transfers between devices: 105 us -> 58.8 us
  local copies, waits for them, and re-layouts: 6.92 us -> 12.1 us
  Pallas kernels: 211 us -> 206 us
  starting transfers between devices: 28.6 us -> 33.5 us
    ppermute x4, waiting for transfers between devices: 68.9 us -> 20.1 us  [heads(): o_other.append(lax.ppermute(outs[-1], 'tp', swap))]
    ppermute x2, waiting for transfers between devices: 0.01 us -> 38.7 us  [spread(): w_x[i] = lax.ppermute(w_peer[i], 'cp', flip(2))]
    ppermute x1, waiting for transfers between devices: 29.3 us -> 0.01 us  [local_step(): back1 = lax.ppermute(far, 'cp', [(0, 3)])]
    ppermute x1, waiting for transfers between devices: 6.92 us -> 0.01 us  [local_step(): w_peer = [lax.ppermute(mine, 'tp', swap)]]
    ppermute x2, starting transfers between devices: 2.03 us -> 8.6 us  [spread(): w_x[i] = lax.ppermute(w_peer[i], 'cp', flip(2))]
    unnamed x11 -> x37, local copies, waits for them, and re-layouts: 4.06 us -> 8.99 us
    pallas_call x5, Pallas kernels: 130 us -> 125 us  [attention(): pl.pallas_call(functools.partial(attn_kernel, old=keys // 2, slots=slots,...]
  transfers between devices with their start and end apart: 21 -> 21, of which waited for: 5 -> 3; matrix products, arithmetic and copies ran while one was open for 1% -> 1% of each run, Pallas kernels for 53% -> 58%
where the time goes in v5:
time: 313 us
  Pallas kernels  206 us (66%)
  waiting for transfers between devices  58.8 us (19%)
  starting transfers between devices  33.5 us (11%)
  local copies, waits for them, and re-layouts  12.1 us (4%)
    pallas_call x5, Pallas kernels, attention(): pl.pallas_call(functools.partial(attn_kernel, old=keys // 2, slots=slots,...  125 us
    ppermute x2, waiting for transfers between devices, spread(): w_x[i] = lax.ppermute(w_peer[i], 'cp', flip(2))  38.7 us
    pallas_call x1, Pallas kernels, other_part(): pl.pallas_call(functools.partial(other_kernel, parts=len(o_parts)), grid_...  24.9 us
    pallas_call x1, Pallas kernels, own_part(): pl.pallas_call(own_kernel, grid=(d // block,), in_specs=[pl.BlockSpec((ro...  22.4 us
    pallas_call x1, Pallas kernels, q_proj(): pl.pallas_call(q_kernel, grid=(width // block,), in_specs=[pl.BlockSpec((...  21.3 us
    ppermute x4, waiting for transfers between devices, heads(): o_other.append(lax.ppermute(outs[-1], 'tp', swap))  20.1 us
    ppermute x1, starting transfers between devices, local_step(): back0 = lax.ppermute(far, 'cp', [(0, 3), (1, 2)])  10.8 us
    pallas_call x1, Pallas kernels, norm_kv(): pl.pallas_call(norm_kv_kernel, grid_spec=pltpu.PrefetchScalarGridSpec(num...  9.64 us
  transfers between devices with their start and end apart: 21, of which 3 were waited for; matrix products, arithmetic and copies ran while one was open for 1% of the time, Pallas kernels for 58%

profile of v5, /device:TPU:0, one launch (start us, length us, event | category | flops | bytes accessed | tf_op | source)
XLA Modules:
  0.0 312.7 jit_solution(9634433394675685580)
XLA Ops:
  1.7 3.3 %collective-permute-start.1 = (bf16[2048,128]{1,0:T(8,128)(2,1)S(1)}, bf16[2048,128]{1,0:T(8,128)(2,1)S(1)}, u32[]{:S(2)}, u32[]{:S(2)}) collective-permute-start(bf16[2048,128]{1,0:T(8,128)(2,1)S(1)} %pad_maximum_fusion.refs_0_), channel_id=1, source_target_pairs={{0,2},{1,3},{2,0},{3,1},{4,6},{5,7},{6,4},{7,5}} | collective-permute-start | bytes 1572872 | tf_op jit(solution)/shard_map/ppermute | solution.py:475
  7.6 9.6 %norm_kv.1 = (bf16[1024,4096]{1,0:T(8,128)(2,1)S(1)}, bf16[2,1024,128]{2,1,0:T(8,128)(2,1)S(1)}, bf16[1024,128]{1,0:T(8,128)(2,1)}, bf16[1024,128]{1,0:T(8,128)(...) custom-call(s32[1]{0:T(128)} %bitcast.cp_ref, bf16[1024,4096]{1,0:T(8,128)(2,1)} %x_ref.3, ...), custom_call_target="tpu_custom_call" | custom-call | flops 2147483648 | bytes 16777216 | tf_op jit(solution)/shard_map/norm_kv/pallas_call | solution.py:67
  17.2 1.5 copy-done
  18.8 2.0 collective-permute-start.4
  21.0 21.3 %q_proj.1 = (bf16[1024,2048]{1,0:T(8,128)(2,1)S(1)}, bf16[1024,384]{1,0:T(8,128)(2,1)S(1)}) custom-call(bf16[1024,4096]{1,0:T(8,128)(2,1)S(1)} %get-tuple-element.25.h_ref, bf16[4096,2304]{1,0:T(8,128)(2,1)} %w_ref.3, bf16[1,2304]{1,0:T(2,128)(2,1)S(1)} %broadcast_in_dim.17.b_ref, f32[1024,128]{1,0:T(8,128)S(1)} %get-tuple-element.26.cos_ref, ...), custom_call_target="tpu_custom_call" | custom-call | flops 17179869184 | bytes 16777216 | tf_op jit(solution)/shard_map/q_proj/pallas_call | solution.py:121
  43.2 2.0 copy-done.3
  45.2 1.7 constant_dynamic-slice_fusion
  46.9 2.0 collective-permute-start.13
  49.0 1.5 collective-permute-start.6
  50.8 2.6 gather.1
  53.4 29.8 %attention.5.rest_0_ = bf16[1024,640]{1,0:T(8,128)(2,1)S(1)} custom-call(s32[1]{0:T(128)} %bitcast.cp_ref, bf16[1024,2048]{1,0:T(8,128)(2,1)S(1)} %copy-done.4, bf16[1024,2048]{1,0:T(8,128)(2,1)S(1)} %copy-done.4, bf16[8192,128]{1,0:T(8,128)(2,1)S(1)} %get-tuple-element.31.refs_2_.refs_4_, bf16[64,128,128]{2,1,0:T(8,128)(2,1)S(1)} %get-tuple-element.32.refs_3_.refs_5_), custom_call_target="tpu_custom_call" | custom-call | flops 21474836480 | bytes 2621440 | tf_op jit(solution)/shard_map/attention/pallas_call | solution.py:335
  83.2 10.1 %attention.6 = bf16[1024,128]{1,0:T(8,128)(2,1)S(1)} custom-call(s32[1]{0:T(128)} %bitcast.cp_ref, bf16[1024,384]{1,0:T(8,128)(2,1)S(1)} %collective-permute-done.6.refs_0_.refs_1_, bf16[1024,384]{1,0:T(8,128)(2,1)S(1)} %collective-permute-done.6.refs_0_.refs_1_, bf16[8192,128]{1,0:T(8,128)(2,1)S(1)} %get-tuple-element.31.refs_2_.refs_4_, ...), custom_call_target="tpu_custom_call" | custom-call | flops 4294967296 | bytes 524288 | tf_op jit(solution)/shard_map/attention/pallas_call | solution.py:335
  93.4 10.8 %collective-permute-start.7 = (bf16[1024,128]{1,0:T(8,128)(2,1)S(1)}, bf16[1024,128]{1,0:T(8,128)(2,1)S(1)}, u32[]{:S(2)}, u32[]{:S(2)}) collective-permute-start(bf16[1024,128]{1,0:T(8,128)(2,1)S(1)} %attention.6), channel_id=1, source_target_pairs={{0,3},{1,2},{4,7},{5,6}} | collective-permute-start | bytes 786440 | tf_op jit(solution)/shard_map/ppermute | solution.py:512
  104.1 42.7 %attention.7 = (bf16[1024,256]{1,0:T(8,128)(2,1)S(1)}, bf16[1024,512]{1,0:T(8,128)(2,1)S(1)}) custom-call(s32[1]{0:T(128)} %bitcast.cp_ref, bf16[1024,384]{1,0:T(8,128)(2,1)S(1)} %collective-permute-done.6.refs_0_.refs_1_, bf16[1024,384]{1,0:T(8,128)(2,1)S(1)} %collective-permute-done.6.refs_0_.refs_1_, bf16[1024,2048]{1,0:T(8,128)(2,1)S(1)} %copy-done.4, ...), custom_call_target="tpu_custom_call" | custom-call | flops 25769803776 | bytes 3145728 | tf_op jit(solution)/shard_map/attention/pallas_call | solution.py:335
  146.9 1.7 collective-permute-start.10
  150.0 18.5 %attention.8.rest_2_ = bf16[1024,384]{1,0:T(8,128)(2,1)S(1)} custom-call(s32[1]{0:T(128)} %bitcast.cp_ref, bf16[1024,2048]{1,0:T(8,128)(2,1)S(1)} %copy-done.4, bf16[1024,2048]{1,0:T(8,128)(2,1)S(1)} %copy-done.4, bf16[8192,128]{1,0:T(8,128)(2,1)S(1)} %get-tuple-element.31.refs_2_.refs_4_, bf16[64,128,128]{2,1,0:T(8,128)(2,1)S(1)} %get-tuple-element.32.refs_3_.refs_5_), custom_call_target="tpu_custom_call" | custom-call | flops 12884901888 | bytes 1572864 | tf_op jit(solution)/shard_map/attention/pallas_call | solution.py:335
  168.8 8.6 %collective-permute-start.17 = (bf16[192,4096]{1,0:T(8,128)(2,1)S(1)}, bf16[192,4096]{1,0:T(8,128)(2,1)S(1)}, u32[]{:S(2)}, u32[]{:S(2)}) collective-permute-start(bf16[192,4096]{1,0:T(8,128)(2,1)S(1)} %collective-permute-done.13.rest_4_), channel_id=1, source_target_pairs={{0,2},{1,3},{2,0},{3,1},{4,6},{5,7},{6,4},{7,5}} | collective-permute-start | bytes 4718600 | tf_op jit(solution)/shard_map/ppermute | solution.py:503
  177.4 24.3 %attention.9.rest_3_ = bf16[1024,512]{1,0:T(8,128)(2,1)S(1)} custom-call(s32[1]{0:T(128)} %bitcast.cp_ref, bf16[1024,2048]{1,0:T(8,128)(2,1)S(1)} %copy-done.4, bf16[1024,2048]{1,0:T(8,128)(2,1)S(1)} %copy-done.4, bf16[8192,128]{1,0:T(8,128)(2,1)S(1)} %get-tuple-element.31.refs_2_.refs_4_, bf16[64,128,128]{2,1,0:T(8,128)(2,1)S(1)} %get-tuple-element.32.refs_3_.refs_5_, ...), custom_call_target="tpu_custom_call" | custom-call | flops 17179869184 | bytes 2097152 | tf_op jit(solution)/shard_map/attention/pallas_call | solution.py:335
  201.9 16.5 %collective-permute-done.18.rest_9_ = bf16[320,4096]{1,0:T(8,128)(2,1)S(1)} collective-permute-done((bf16[320,4096]{1,0:T(8,128)(2,1)S(1)}, bf16[320,4096]{1,0:T(8,128)(2,1)S(1)}, u32[]{:S(2)}, u32[]{:S(2)}) %collective-permute-start.18) | collective-permute-done | bytes 2621472 | tf_op jit(solution)/shard_map/ppermute | solution.py:503
  218.4 22.2 %collective-permute-done.17.rest_8_ = bf16[192,4096]{1,0:T(8,128)(2,1)S(1)} collective-permute-done((bf16[192,4096]{1,0:T(8,128)(2,1)S(1)}, bf16[192,4096]{1,0:T(8,128)(2,1)S(1)}, u32[]{:S(2)}, u32[]{:S(2)}) %collective-permute-start.17) | collective-permute-done | bytes 1572896 | tf_op jit(solution)/shard_map/ppermute | solution.py:503
  240.9 20.1 %collective-permute-done.11.rest_2_ = bf16[1024,384]{1,0:T(8,128)(2,1)S(1)} collective-permute-done((bf16[1024,384]{1,0:T(8,128)(2,1)S(1)}, bf16[1024,384]{1,0:T(8,128)(2,1)S(1)}, u32[]{:S(2)}, u32[]{:S(2)}) %collective-permute-start.11) | collective-permute-done | bytes 786464 | tf_op jit(solution)/shard_map/ppermute | solution.py:499
  261.9 22.4 %own_part.1.y_ref = f32[1024,4096]{1,0:T(8,128)} custom-call(bf16[1024,4096]{1,0:T(8,128)(2,1)S(1)} %bitcast.7, bf16[1024,640]{1,0:T(8,128)(2,1)S(1)} %attention.5.rest_0_, bf16[1024,512]{1,0:T(8,128)(2,1)S(1)} %get-tuple-element.36.rest_1_, bf16[1024,384]{1,0:T(8,128)(2,1)S(1)} %attention.8.rest_2_, bf16[1024,512]{1,0:T(8,128)(2,1)S(1)} %attention.9.rest_3_, ...), custom_call_target="tpu_custom_call" | custom-call | flops 17179869184 | bytes 25165824 | tf_op jit(solution)/shard_map/own_part/pallas_call | solution.py:395
  286.3 1.5 copy-done.7
  287.8 24.9 %other_part.1 = bf16[1024,4096]{1,0:T(8,128)(2,1)} custom-call(s32[1]{0:T(128)} %bitcast.cp_ref, f32[1024,4096]{1,0:T(8,128)} %own_part.1.y_ref, bf16[1024,640]{1,0:T(8,128)(2,1)} %copy-done.12, bf16[1024,512]{1,0:T(8,128)(2,1)} %copy-done.13, bf16[1024,384]{1,0:T(8,128)(2,1)} %copy-done.15, bf16[1024,512]{1,0:T(8,128)(2,1)} %copy-done.14, ...), custom_call_target="tpu_custom_call" | custom-call | flops 17179869184 | bytes 25165824 | tf_op jit(solution)/shard_map/other_part/pallas_call | solution.py:436
  (70 shorter events, 10.2 us)
Async XLA Ops:
  1.7 19.1 %collective-permute-start.1 = (bf16[2048,128]{1,0:T(8,128)(2,1)S(1)}, bf16[2048,128]{1,0:T(8,128)(2,1)S(1)}, u32[]{:S(2)}, u32[]{:S(2)}) collective-permute-start(bf16[2048,128]{1,0:T(8,128)(2,1)S(1)} %pad_maximum_fusion.refs_0_), channel_id=1, source_target_pairs={{0,2},{1,3},{2,0},{3,1},{4,6},{5,7},{6,4},{7,5}} | collective-permute-start | bytes 1572872 | tf_op jit(solution)/shard_map/ppermute | solution.py:475
  5.0 41.9 %collective-permute-start = (bf16[2048,128]{1,0:T(8,128)(2,1)S(1)}, bf16[2048,128]{1,0:T(8,128)(2,1)S(1)}, u32[]{:S(2)}, u32[]{:S(2)}) collective-permute-start(bf16[2048,128]{1,0:T(8,128)(2,1)S(1)} %pad_maximum_fusion.refs_0_), channel_id=1, source_target_pairs={{0,1},{1,0},{2,3},{3,2},{4,5},{5,4},{6,7},{7,6}} | collective-permute-start | bytes 1572872 | tf_op jit(solution)/shard_map/ppermute | solution.py:475
  18.7 30.3 %collective-permute-start.5 = (bf16[2048,128]{1,0:T(8,128)(2,1)S(1)}, bf16[2048,128]{1,0:T(8,128)(2,1)S(1)}, u32[]{:S(2)}, u32[]{:S(2)}) collective-permute-start(bf16[2048,128]{1,0:T(8,128)(2,1)S(1)} %bitcast.8), channel_id=1, source_target_pairs={{0,3},{1,0},{2,1},{3,2},{4,7},{5,4},{6,5},{7,6}} | collective-permute-start | bytes 1572872 | tf_op jit(solution)/shard_map/ppermute | solution.py:484
  18.8 31.6 %collective-permute-start.4 = (bf16[2048,128]{1,0:T(8,128)(2,1)S(1)}, bf16[2048,128]{1,0:T(8,128)(2,1)S(1)}, u32[]{:S(2)}, u32[]{:S(2)}) collective-permute-start(bf16[2048,128]{1,0:T(8,128)(2,1)S(1)} %bitcast.9), channel_id=1, source_target_pairs={{0,2},{1,3},{2,0},{3,1},{4,6},{5,7},{6,4},{7,5}} | collective-permute-start | bytes 1572872 | tf_op jit(solution)/shard_map/ppermute | solution.py:484
  20.8 29.9 %collective-permute-start.3 = (bf16[2048,128]{1,0:T(8,128)(2,1)S(1)}, bf16[2048,128]{1,0:T(8,128)(2,1)}, u32[]{:S(2)}, u32[]{:S(2)}) collective-permute-start(bf16[2048,128]{1,0:T(8,128)(2,1)S(1)} %bitcast.10), channel_id=1, source_target_pairs={{0,1},{1,2},{2,3},{3,0},{4,5},{5,6},{6,7},{7,4}} | collective-permute-start | bytes 1572872 | tf_op jit(solution)/shard_map/ppermute | solution.py:484
  20.8 29.9 %collective-permute-start.2 = (bf16[2048,128]{1,0:T(8,128)(2,1)S(1)}, bf16[2048,128]{1,0:T(8,128)(2,1)}, u32[]{:S(2)}, u32[]{:S(2)}) collective-permute-start(bf16[2048,128]{1,0:T(8,128)(2,1)S(1)} %collective-permute-done.1.refs_2_), channel_id=1, source_target_pairs={{0,1},{1,0},{2,3},{3,2},{4,5},{5,4},{6,7},{7,6}} | collective-permute-start | bytes 1572872 | tf_op jit(solution)/shard_map/ppermute | solution.py:482
  46.9 121.5 %collective-permute-start.13 = (bf16[192,4096]{1,0:T(8,128)(2,1)S(1)}, bf16[192,4096]{1,0:T(8,128)(2,1)S(1)}, u32[]{:S(2)}, u32[]{:S(2)}) collective-permute-start(bf16[192,4096]{1,0:T(8,128)(2,1)S(1)} %constant_dynamic-slice_fusion), channel_id=1, source_target_pairs={{0,4},{4,0},{1,5},{5,1},{2,6},{6,2},{3,7},{7,3}} | collective-permute-start | bytes 4718600 | tf_op jit(solution)/shard_map/ppermute | solution.py:477
  49.0 34.3 %collective-permute-start.6 = (bf16[1024,384]{1,0:T(8,128)(2,1)}, bf16[1024,384]{1,0:T(8,128)(2,1)S(1)}, u32[]{:S(2)}, u32[]{:S(2)}) collective-permute-start(bf16[1024,384]{1,0:T(8,128)(2,1)} %copy-done.2), channel_id=1, source_target_pairs={{3,0},{2,1},{7,4},{6,5}} | collective-permute-start | bytes 2359304 | tf_op jit(solution)/shard_map/ppermute | solution.py:486
  50.5 99.5 %collective-permute-start.14 = (bf16[320,4096]{1,0:T(8,128)(2,1)S(1)}, bf16[320,4096]{1,0:T(8,128)(2,1)S(1)}, u32[]{:S(2)}, u32[]{:S(2)}) collective-permute-start(bf16[320,4096]{1,0:T(8,128)(2,1)S(1)} %copy-done.1), channel_id=1, source_target_pairs={{0,4},{4,0},{1,5},{5,1},{2,6},{6,2},{3,7},{7,3}} | collective-permute-start | bytes 7864328 | tf_op jit(solution)/shard_map/ppermute | solution.py:481
  93.4 75.5 %collective-permute-start.7 = (bf16[1024,128]{1,0:T(8,128)(2,1)S(1)}, bf16[1024,128]{1,0:T(8,128)(2,1)S(1)}, u32[]{:S(2)}, u32[]{:S(2)}) collective-permute-start(bf16[1024,128]{1,0:T(8,128)(2,1)S(1)} %attention.6), channel_id=1, source_target_pairs={{0,3},{1,2},{4,7},{5,6}} | collective-permute-start | bytes 786440 | tf_op jit(solution)/shard_map/ppermute | solution.py:512
  146.9 114.5 %collective-permute-start.10 = (bf16[1024,512]{1,0:T(8,128)(2,1)S(1)}, bf16[1024,512]{1,0:T(8,128)(2,1)S(1)}, u32[]{:S(2)}, u32[]{:S(2)}) collective-permute-start(bf16[1024,512]{1,0:T(8,128)(2,1)S(1)} %get-tuple-element.36.rest_1_), channel_id=1, source_target_pairs={{0,4},{4,0},{1,5},{5,1},{2,6},{6,2},{3,7},{7,3}} | collective-permute-start | bytes 3145736 | tf_op jit(solution)/shard_map/ppermute | solution.py:499
  148.6 28.8 %collective-permute-start.8 = (bf16[1024,256]{1,0:T(8,128)(2,1)S(1)}, bf16[1024,256]{1,0:T(8,128)(2,1)S(1)}, u32[]{:S(2)}, u32[]{:S(2)}) collective-permute-start(bf16[1024,256]{1,0:T(8,128)(2,1)S(1)} %get-tuple-element.39), channel_id=1, source_target_pairs={{0,3},{4,7}} | collective-permute-start | bytes 1572872 | tf_op jit(solution)/shard_map/ppermute | solution.py:516
  149.9 68.4 %collective-permute-start.18 = (bf16[320,4096]{1,0:T(8,128)(2,1)S(1)}, bf16[320,4096]{1,0:T(8,128)(2,1)S(1)}, u32[]{:S(2)}, u32[]{:S(2)}) collective-permute-start(bf16[320,4096]{1,0:T(8,128)(2,1)S(1)} %collective-permute-done.14.rest_5_), channel_id=1, source_target_pairs={{0,2},{1,3},{2,0},{3,1},{4,6},{5,7},{6,4},{7,5}} | collective-permute-start | bytes 7864328 | tf_op jit(solution)/shard_map/ppermute | solution.py:503
  150.0 111.9 %slice-start = ((s8[8388608]{0:T(1024)(128)(4,1)}), s8[4194304]{0:T(1024)(128)(4,1)S(1)}, s32[]{:S(2)}) async-start(s8[8388608]{0:T(1024)(128)(4,1)} %bitcast.6), calls=%async_computation | async-start | bytes 8388608
  168.4 93.5 %slice-start.1 = ((s8[8388608]{0:T(1024)(128)(4,1)}), s8[4194304]{0:T(1024)(128)(4,1)S(1)}, s32[]{:S(2)}) async-start(s8[8388608]{0:T(1024)(128)(4,1)} %bitcast.6), calls=%async_computation.1 | async-start | bytes 8388608
  168.5 92.9 %copy-start.8 = (bf16[192,4096]{1,0:T(8,128)(2,1)}, bf16[192,4096]{1,0:T(8,128)(2,1)S(1)}, u32[]{:S(2)}) copy-start(bf16[192,4096]{1,0:T(8,128)(2,1)S(1)} %collective-permute-done.13.rest_4_) | copy-start | bytes 4718596
  168.5 92.9 %collective-permute-start.9 = (bf16[1024,640]{1,0:T(8,128)(2,1)S(1)}, bf16[1024,640]{1,0:T(8,128)(2,1)S(1)}, u32[]{:S(2)}, u32[]{:S(2)}) collective-permute-start(bf16[1024,640]{1,0:T(8,128)(2,1)S(1)} %attention.5.rest_0_), channel_id=1, source_target_pairs={{0,4},{4,0},{1,5},{5,1},{2,6},{6,2},{3,7},{7,3}} | collective-permute-start | bytes 3932168 | tf_op jit(solution)/shard_map/ppermute | solution.py:499
  168.8 71.8 %collective-permute-start.17 = (bf16[192,4096]{1,0:T(8,128)(2,1)S(1)}, bf16[192,4096]{1,0:T(8,128)(2,1)S(1)}, u32[]{:S(2)}, u32[]{:S(2)}) collective-permute-start(bf16[192,4096]{1,0:T(8,128)(2,1)S(1)} %collective-permute-done.13.rest_4_), channel_id=1, source_target_pairs={{0,2},{1,3},{2,0},{3,1},{4,6},{5,7},{6,4},{7,5}} | collective-permute-start | bytes 4718600 | tf_op jit(solution)/shard_map/ppermute | solution.py:503
  201.7 82.7 %collective-permute-start.16 = (bf16[320,4096]{1,0:T(8,128)(2,1)S(1)}, bf16[320,4096]{1,0:T(8,128)(2,1)S(1)}, u32[]{:S(2)}, u32[]{:S(2)}) collective-permute-start(bf16[320,4096]{1,0:T(8,128)(2,1)S(1)} %collective-permute-done.14.rest_5_), channel_id=1, source_target_pairs={{0,1},{1,0},{2,3},{3,2},{4,5},{5,4},{6,7},{7,6}} | collective-permute-start | bytes 7864328 | tf_op jit(solution)/shard_map/ppermute | solution.py:504
  218.4 69.5 %collective-permute-start.20 = (bf16[320,4096]{1,0:T(8,128)(2,1)S(1)}, bf16[320,4096]{1,0:T(8,128)(2,1)}, u32[]{:S(2)}, u32[]{:S(2)}) collective-permute-start(bf16[320,4096]{1,0:T(8,128)(2,1)S(1)} %collective-permute-done.18.rest_9_), channel_id=1, source_target_pairs={{0,1},{1,0},{2,3},{3,2},{4,5},{5,4},{6,7},{7,6}} | collective-permute-start | bytes 7864328 | tf_op jit(solution)/shard_map/ppermute | solution.py:507
  240.6 20.4 %collective-permute-start.11 = (bf16[1024,384]{1,0:T(8,128)(2,1)S(1)}, bf16[1024,384]{1,0:T(8,128)(2,1)S(1)}, u32[]{:S(2)}, u32[]{:S(2)}) collective-permute-start(bf16[1024,384]{1,0:T(8,128)(2,1)S(1)} %attention.8.rest_2_), channel_id=1, source_target_pairs={{0,4},{4,0},{1,5},{5,1},{2,6},{6,2},{3,7},{7,3}} | collective-permute-start | bytes 2359304 | tf_op jit(solution)/shard_map/ppermute | solution.py:499
  261.0 23.3 %collective-permute-start.12 = (bf16[1024,512]{1,0:T(8,128)(2,1)S(1)}, bf16[1024,512]{1,0:T(8,128)(2,1)S(1)}, u32[]{:S(2)}, u32[]{:S(2)}) collective-permute-start(bf16[1024,512]{1,0:T(8,128)(2,1)S(1)} %attention.9.rest_3_), channel_id=1, source_target_pairs={{0,4},{4,0},{1,5},{5,1},{2,6},{6,2},{3,7},{7,3}} | collective-permute-start | bytes 3145736 | tf_op jit(solution)/shard_map/ppermute | solution.py:499
  261.4 23.0 %collective-permute-start.15 = (bf16[192,4096]{1,0:T(8,128)(2,1)S(1)}, bf16[192,4096]{1,0:T(8,128)(2,1)S(1)}, u32[]{:S(2)}, u32[]{:S(2)}) collective-permute-start(bf16[192,4096]{1,0:T(8,128)(2,1)S(1)} %collective-permute-done.13.rest_4_), channel_id=1, source_target_pairs={{0,1},{1,0},{2,3},{3,2},{4,5},{5,4},{6,7},{7,6}} | collective-permute-start | bytes 4718600 | tf_op jit(solution)/shard_map/ppermute | solution.py:504
  261.4 23.0 %collective-permute-start.19 = (bf16[192,4096]{1,0:T(8,128)(2,1)S(1)}, bf16[192,4096]{1,0:T(8,128)(2,1)S(1)}, u32[]{:S(2)}, u32[]{:S(2)}) collective-permute-start(bf16[192,4096]{1,0:T(8,128)(2,1)S(1)} %collective-permute-done.17.rest_8_), channel_id=1, source_target_pairs={{0,1},{1,0},{2,3},{3,2},{4,5},{5,4},{6,7},{7,6}} | collective-permute-start | bytes 4718600 | tf_op jit(solution)/shard_map/ppermute | solution.py:507
  (15 other events, 252.8 us)

commit v6 on v5

--- a/solution.py
+++ b/solution.py
@@ -19,7 +19,7 @@
 NORM_VMEM = 36 * 2 ** 20
 Q_VMEM = 36 * 2 ** 20
 OUT_VMEM = 28 * 2 ** 20
-OTHER_VMEM = 58 * 2 ** 20
+OTHER_VMEM = 48 * 2 ** 20
 
 
 def rotate(a, cos, sin):
@@ -296,7 +296,7 @@
             write((far_outs + own_outs)[0])
 
     for i, back_ref in enumerate(back_refs):
-        @pl.when((owner < 0) & ((slot == pl.num_programs(0) - 1) == (i == 0)))
+        @pl.when((owner < 0) & ((slot >= pl.num_programs(0) - 2) == (i == 0)))
         def _(back_ref=back_ref):
             own_outs[0][...] = back_ref[...]
 
@@ -323,7 +323,7 @@
         pl.BlockSpec((keys // HEAD, HEAD, HEAD), lambda s, c: (0, 0, 0)),
     ]
     for i in range(len(back)):
-        in_specs.append(row_block((lambda s, c: (0, 0)) if i == 0 else (lambda s, c: (0, jnp.clip(s - far - (slots - MOVED), 0, MOVED - 2)))))
+        in_specs.append(row_block((lambda s, c: (0, jnp.clip(s - far - (slots - 2), 0, 1))) if i == 0 else (lambda s, c: (0, 0))))
     scratch = [
         pltpu.VMEM((rows, rows), F32),
         pltpu.VMEM((rows // HEAD, rows, HEAD), BF),
@@ -451,7 +451,7 @@
     )(cp, y, *o_parts, *w_parts)
 
 
-SIZES = (5, 4, 3, 4)
+SIZES = (6, 4, 2, 4)
 PIECE_ROWS = (192, 320)
 PIECES = len(PIECE_ROWS)
 
@@ -508,11 +508,11 @@
 
     spread(0)
     (part,) = heads(0)
-    (far,) = attend(None, after(q_far, part), far=1)
+    (far,) = attend(None, after(q_far, part), far=2)
     back0 = lax.ppermute(far, "cp", [(0, 3), (1, 2)])
     w_peer[1] = after(w_peer[1], far)
     spread(1)
-    far, part = heads(1, far, far=MOVED - 1, far_first=1)
+    far, part = heads(1, far, far=1, far_first=2)
     back1 = lax.ppermute(far, "cp", [(0, 3)])
     (part,) = heads(2, part)
     (part,) = heads(3, part, back=(back0, back1))

time: 313 us -> 322 us (1.029); the launches traced: 313 us -> 318 us
  starting transfers between devices: 33.5 us -> 39.3 us
    ppermute x2, waiting for transfers between devices: 38.7 us -> 0.55 us  [spread(): w_x[i] = lax.ppermute(w_peer[i], 'cp', flip(2))]
    ppermute x1, waiting for transfers between devices: 0.01 us -> 25.5 us  [local_step(): w_peer.append(lax.ppermute(mine, 'tp', swap))]
    ppermute x2, starting transfers between devices: 0.17 us -> 9.61 us  [spread(): w_core[i] = lax.ppermute(w_peer[i], 'cp', flip(1))]
    ppermute x4, waiting for transfers between devices: 20.1 us -> 28.5 us  [heads(): o_other.append(lax.ppermute(outs[-1], 'tp', swap))]
    ppermute x2, starting transfers between devices: 8.6 us -> 2.18 us  [spread(): w_x[i] = lax.ppermute(w_peer[i], 'cp', flip(2))]
    ppermute x1, starting transfers between devices: 10.8 us -> 5.21 us  [local_step(): back0 = lax.ppermute(far, 'cp', [(0, 3), (1, 2)])]
    ppermute x4, starting transfers between devices: 2.73 us -> 7.68 us  [heads(): o_other.append(lax.ppermute(outs[-1], 'tp', swap))]
    ppermute x1, waiting for transfers between devices: 0.01 us -> 4.1 us  [local_step(): back1 = lax.ppermute(far, 'cp', [(0, 3)])]
  transfers between devices with their start and end apart: 21 -> 21, of which waited for: 3 -> 5; matrix products, arithmetic and copies ran while one was open for 1% -> 1% of each run, Pallas kernels for 58% -> 58%
where the time goes in v6:
time: 322 us; the launch traced here: 318 us
  Pallas kernels  208 us (65%)
  waiting for transfers between devices  58.7 us (18%)
  starting transfers between devices  39.3 us (12%)
  local copies, waits for them, and re-layouts  11.1 us (3%)
    pallas_call x5, Pallas kernels, attention(): pl.pallas_call(functools.partial(attn_kernel, old=keys // 2, slots=slots,...  128 us
    ppermute x4, waiting for transfers between devices, heads(): o_other.append(lax.ppermute(outs[-1], 'tp', swap))  28.5 us
    ppermute x1, waiting for transfers between devices, local_step(): w_peer.append(lax.ppermute(mine, 'tp', swap))  25.5 us
    pallas_call x1, Pallas kernels, q_proj(): pl.pallas_call(q_kernel, grid=(width // block,), in_specs=[pl.BlockSpec((...  22.7 us
    pallas_call x1, Pallas kernels, other_part(): pl.pallas_call(functools.partial(other_kernel, parts=len(o_parts)), grid_...  22.7 us
    pallas_call x1, Pallas kernels, own_part(): pl.pallas_call(own_kernel, grid=(d // block,), in_specs=[pl.BlockSpec((ro...  22.3 us
    pallas_call x1, Pallas kernels, norm_kv(): pl.pallas_call(norm_kv_kernel, grid_spec=pltpu.PrefetchScalarGridSpec(num...  9.64 us
    ppermute x2, starting transfers between devices, spread(): w_core[i] = lax.ppermute(w_peer[i], 'cp', flip(1))  9.61 us
  transfers between devices with their start and end apart: 21, of which 5 were waited for; matrix products, arithmetic and copies ran while one was open for 1% of the time, Pallas kernels for 58%

profile of v6, /device:TPU:0, one launch (start us, length us, event | category | flops | bytes accessed | tf_op | source)
XLA Modules:
  0.0 318.5 jit_solution(12788910445468748107)
XLA Ops:
  1.7 3.3 %collective-permute-start.1 = (bf16[2048,128]{1,0:T(8,128)(2,1)S(1)}, bf16[2048,128]{1,0:T(8,128)(2,1)S(1)}, u32[]{:S(2)}, u32[]{:S(2)}) collective-permute-start(bf16[2048,128]{1,0:T(8,128)(2,1)S(1)} %pad_maximum_fusion.refs_0_), channel_id=1, source_target_pairs={{0,2},{1,3},{2,0},{3,1},{4,6},{5,7},{6,4},{7,5}} | collective-permute-start | bytes 1572872 | tf_op jit(solution)/shard_map/ppermute | solution.py:475
  7.6 9.6 %norm_kv.1 = (bf16[1024,4096]{1,0:T(8,128)(2,1)S(1)}, bf16[2,1024,128]{2,1,0:T(8,128)(2,1)S(1)}, bf16[1024,128]{1,0:T(8,128)(2,1)}, bf16[1024,128]{1,0:T(8,128)(...) custom-call(s32[1]{0:T(128)} %bitcast.cp_ref, bf16[1024,4096]{1,0:T(8,128)(2,1)} %x_ref.3, ...), custom_call_target="tpu_custom_call" | custom-call | flops 2147483648 | bytes 16777216 | tf_op jit(solution)/shard_map/norm_kv/pallas_call | solution.py:67
  18.9 2.0 collective-permute-start.4
  21.0 22.7 %q_proj.1 = (bf16[1024,2048]{1,0:T(8,128)(2,1)S(1)}, bf16[1024,384]{1,0:T(8,128)(2,1)S(1)}) custom-call(bf16[1024,4096]{1,0:T(8,128)(2,1)S(1)} %get-tuple-element.25.h_ref, bf16[4096,2304]{1,0:T(8,128)(2,1)} %w_ref.3, bf16[1,2304]{1,0:T(2,128)(2,1)S(1)} %broadcast_in_dim.17.b_ref, f32[1024,128]{1,0:T(8,128)S(1)} %get-tuple-element.26.cos_ref, ...), custom_call_target="tpu_custom_call" | custom-call | flops 17179869184 | bytes 16777216 | tf_op jit(solution)/shard_map/q_proj/pallas_call | solution.py:121
  44.6 2.0 copy-done.3
  48.4 2.0 collective-permute-start.13
  52.2 2.6 gather.1
  54.8 36.2 %attention.5.rest_0_ = bf16[1024,768]{1,0:T(8,128)(2,1)S(1)} custom-call(s32[1]{0:T(128)} %bitcast.cp_ref, bf16[1024,2048]{1,0:T(8,128)(2,1)S(1)} %copy-done.4, bf16[1024,2048]{1,0:T(8,128)(2,1)S(1)} %copy-done.4, bf16[8192,128]{1,0:T(8,128)(2,1)S(1)} %get-tuple-element.31.refs_2_.refs_4_, bf16[64,128,128]{2,1,0:T(8,128)(2,1)S(1)} %get-tuple-element.32.refs_3_.refs_5_), custom_call_target="tpu_custom_call" | custom-call | flops 25769803776 | bytes 3145728 | tf_op jit(solution)/shard_map/attention/pallas_call | solution.py:335
  91.1 19.6 %attention.6 = bf16[1024,256]{1,0:T(8,128)(2,1)S(1)} custom-call(s32[1]{0:T(128)} %bitcast.cp_ref, bf16[1024,384]{1,0:T(8,128)(2,1)S(1)} %collective-permute-done.6.refs_0_.refs_1_, bf16[1024,384]{1,0:T(8,128)(2,1)S(1)} %collective-permute-done.6.refs_0_.refs_1_, bf16[8192,128]{1,0:T(8,128)(2,1)S(1)} %get-tuple-element.31.refs_2_.refs_4_, ...), custom_call_target="tpu_custom_call" | custom-call | flops 8589934592 | bytes 1048576 | tf_op jit(solution)/shard_map/attention/pallas_call | solution.py:335
  110.6 5.2 %collective-permute-start.7 = (bf16[1024,256]{1,0:T(8,128)(2,1)S(1)}, bf16[1024,256]{1,0:T(8,128)(2,1)S(1)}, u32[]{:S(2)}, u32[]{:S(2)}) collective-permute-start(bf16[1024,256]{1,0:T(8,128)(2,1)S(1)} %attention.6), channel_id=1, source_target_pairs={{0,3},{1,2},{4,7},{5,6}} | collective-permute-start | bytes 1572872 | tf_op jit(solution)/shard_map/ppermute | solution.py:512
  115.8 25.5 %collective-permute-done.14.rest_5_ = bf16[320,4096]{1,0:T(8,128)(2,1)} collective-permute-done((bf16[320,4096]{1,0:T(8,128)(2,1)S(1)}, bf16[320,4096]{1,0:T(8,128)(2,1)}, u32[]{:S(2)}, u32[]{:S(2)}) %collective-permute-start.14) | collective-permute-done | bytes 2621472 | tf_op jit(solution)/shard_map/ppermute | solution.py:481
  143.0 34.2 %attention.7 = (bf16[1024,128]{1,0:T(8,128)(2,1)S(1)}, bf16[1024,512]{1,0:T(8,128)(2,1)S(1)}) custom-call(s32[1]{0:T(128)} %bitcast.cp_ref, bf16[1024,384]{1,0:T(8,128)(2,1)S(1)} %collective-permute-done.6.refs_0_.refs_1_, bf16[1024,384]{1,0:T(8,128)(2,1)S(1)} %collective-permute-done.6.refs_0_.refs_1_, bf16[1024,2048]{1,0:T(8,128)(2,1)S(1)} %copy-done.4, ...), custom_call_target="tpu_custom_call" | custom-call | flops 21474836480 | bytes 2621440 | tf_op jit(solution)/shard_map/attention/pallas_call | solution.py:335
  178.7 5.1 %collective-permute-start.8 = (bf16[1024,128]{1,0:T(8,128)(2,1)S(1)}, bf16[1024,128]{1,0:T(8,128)(2,1)S(1)}, u32[]{:S(2)}, u32[]{:S(2)}) collective-permute-start(bf16[1024,128]{1,0:T(8,128)(2,1)S(1)} %get-tuple-element.39), channel_id=1, source_target_pairs={{0,3},{4,7}} | collective-permute-start | bytes 786440 | tf_op jit(solution)/shard_map/ppermute | solution.py:516
  183.8 12.9 %attention.8.rest_2_ = bf16[1024,256]{1,0:T(8,128)(2,1)S(1)} custom-call(s32[1]{0:T(128)} %bitcast.cp_ref, bf16[1024,2048]{1,0:T(8,128)(2,1)S(1)} %copy-done.4, bf16[1024,2048]{1,0:T(8,128)(2,1)S(1)} %copy-done.4, bf16[8192,128]{1,0:T(8,128)(2,1)S(1)} %get-tuple-element.31.refs_2_.refs_4_, bf16[64,128,128]{2,1,0:T(8,128)(2,1)S(1)} %get-tuple-element.32.refs_3_.refs_5_), custom_call_target="tpu_custom_call" | custom-call | flops 8589934592 | bytes 1048576 | tf_op jit(solution)/shard_map/attention/pallas_call | solution.py:335
  197.3 4.1 %collective-permute-done.8.refs_5_ = bf16[1024,128]{1,0:T(8,128)(2,1)S(1)} collective-permute-done((bf16[1024,128]{1,0:T(8,128)(2,1)S(1)}, bf16[1024,128]{1,0:T(8,128)(2,1)S(1)}, u32[]{:S(2)}, u32[]{:S(2)}) %collective-permute-start.8) | collective-permute-done | bytes 262176 | tf_op jit(solution)/shard_map/ppermute | solution.py:516
  201.4 24.8 %attention.9.rest_3_ = bf16[1024,512]{1,0:T(8,128)(2,1)S(1)} custom-call(s32[1]{0:T(128)} %bitcast.cp_ref, bf16[1024,2048]{1,0:T(8,128)(2,1)S(1)} %copy-done.4, bf16[1024,2048]{1,0:T(8,128)(2,1)S(1)} %copy-done.4, bf16[8192,128]{1,0:T(8,128)(2,1)S(1)} %get-tuple-element.31.refs_2_.refs_4_, bf16[64,128,128]{2,1,0:T(8,128)(2,1)S(1)} %get-tuple-element.32.refs_3_.refs_5_, ...), custom_call_target="tpu_custom_call" | custom-call | flops 17179869184 | bytes 2097152 | tf_op jit(solution)/shard_map/attention/pallas_call | solution.py:335
  227.7 4.9 %collective-permute-start.16 = (bf16[320,4096]{1,0:T(8,128)(2,1)}, bf16[320,4096]{1,0:T(8,128)(2,1)S(1)}, u32[]{:S(2)}, u32[]{:S(2)}) collective-permute-start(bf16[320,4096]{1,0:T(8,128)(2,1)} %collective-permute-done.14.rest_5_), channel_id=1, source_target_pairs={{0,1},{1,0},{2,3},{3,2},{4,5},{5,4},{6,7},{7,6}} | collective-permute-start | bytes 7864328 | tf_op jit(solution)/shard_map/ppermute | solution.py:504
  233.2 2.3 collective-permute-start.11
  235.5 23.0 %collective-permute-done.11.rest_2_ = bf16[1024,256]{1,0:T(8,128)(2,1)S(1)} collective-permute-done((bf16[1024,256]{1,0:T(8,128)(2,1)S(1)}, bf16[1024,256]{1,0:T(8,128)(2,1)S(1)}, u32[]{:S(2)}, u32[]{:S(2)}) %collective-permute-start.11) | collective-permute-done | bytes 524320 | tf_op jit(solution)/shard_map/ppermute | solution.py:499
  258.5 2.3 collective-permute-start.9
  260.8 4.7 %collective-permute-start.15 = (bf16[192,4096]{1,0:T(8,128)(2,1)S(1)}, bf16[192,4096]{1,0:T(8,128)(2,1)S(1)}, u32[]{:S(2)}, u32[]{:S(2)}) collective-permute-start(bf16[192,4096]{1,0:T(8,128)(2,1)S(1)} %collective-permute-done.13.rest_4_), channel_id=1, source_target_pairs={{0,1},{1,0},{2,3},{3,2},{4,5},{5,4},{6,7},{7,6}} | collective-permute-start | bytes 4718600 | tf_op jit(solution)/shard_map/ppermute | solution.py:504
  265.5 22.3 %own_part.1.y_ref = f32[1024,4096]{1,0:T(8,128)} custom-call(bf16[1024,4096]{1,0:T(8,128)(2,1)S(1)} %bitcast.7, bf16[1024,768]{1,0:T(8,128)(2,1)S(1)} %attention.5.rest_0_, bf16[1024,512]{1,0:T(8,128)(2,1)S(1)} %get-tuple-element.36.rest_1_, bf16[1024,256]{1,0:T(8,128)(2,1)S(1)} %attention.8.rest_2_, bf16[1024,512]{1,0:T(8,128)(2,1)S(1)} %attention.9.rest_3_, ...), custom_call_target="tpu_custom_call" | custom-call | flops 17179869184 | bytes 25165824 | tf_op jit(solution)/shard_map/own_part/pallas_call | solution.py:395
  287.8 5.5 %collective-permute-done.9.rest_0_ = bf16[1024,768]{1,0:T(8,128)(2,1)S(1)} collective-permute-done((bf16[1024,768]{1,0:T(8,128)(2,1)S(1)}, bf16[1024,768]{1,0:T(8,128)(2,1)S(1)}, u32[]{:S(2)}, u32[]{:S(2)}) %collective-permute-start.9) | collective-permute-done | bytes 1572896 | tf_op jit(solution)/shard_map/ppermute | solution.py:499
  295.8 22.7 %other_part.1 = bf16[1024,4096]{1,0:T(8,128)(2,1)} custom-call(s32[1]{0:T(128)} %bitcast.cp_ref, f32[1024,4096]{1,0:T(8,128)} %own_part.1.y_ref, bf16[1024,768]{1,0:T(8,128)(2,1)S(1)} %collective-permute-done.9.rest_0_, bf16[1024,512]{1,0:T(8,128)(2,1)S(1)} %collective-permute-done.10.rest_1_, bf16[1024,256]{1,0:T(8,128)(2,1)S(1)} %collective-permute-done.11.rest_2_, ...), custom_call_target="tpu_custom_call" | custom-call | flops 17179869184 | bytes 25165824 | tf_op jit(solution)/shard_map/other_part/pallas_call | solution.py:436
  (58 shorter events, 18.1 us)
Async XLA Ops:
  1.7 19.2 %collective-permute-start.1 = (bf16[2048,128]{1,0:T(8,128)(2,1)S(1)}, bf16[2048,128]{1,0:T(8,128)(2,1)S(1)}, u32[]{:S(2)}, u32[]{:S(2)}) collective-permute-start(bf16[2048,128]{1,0:T(8,128)(2,1)S(1)} %pad_maximum_fusion.refs_0_), channel_id=1, source_target_pairs={{0,2},{1,3},{2,0},{3,1},{4,6},{5,7},{6,4},{7,5}} | collective-permute-start | bytes 1572872 | tf_op jit(solution)/shard_map/ppermute | solution.py:475
  5.0 43.3 %collective-permute-start = (bf16[2048,128]{1,0:T(8,128)(2,1)S(1)}, bf16[2048,128]{1,0:T(8,128)(2,1)S(1)}, u32[]{:S(2)}, u32[]{:S(2)}) collective-permute-start(bf16[2048,128]{1,0:T(8,128)(2,1)S(1)} %pad_maximum_fusion.refs_0_), channel_id=1, source_target_pairs={{0,1},{1,0},{2,3},{3,2},{4,5},{5,4},{6,7},{7,6}} | collective-permute-start | bytes 1572872 | tf_op jit(solution)/shard_map/ppermute | solution.py:475
  18.7 31.7 %collective-permute-start.5 = (bf16[2048,128]{1,0:T(8,128)(2,1)S(1)}, bf16[2048,128]{1,0:T(8,128)(2,1)S(1)}, u32[]{:S(2)}, u32[]{:S(2)}) collective-permute-start(bf16[2048,128]{1,0:T(8,128)(2,1)S(1)} %bitcast.8), channel_id=1, source_target_pairs={{0,3},{1,0},{2,1},{3,2},{4,7},{5,4},{6,5},{7,6}} | collective-permute-start | bytes 1572872 | tf_op jit(solution)/shard_map/ppermute | solution.py:484
  18.9 33.0 %collective-permute-start.4 = (bf16[2048,128]{1,0:T(8,128)(2,1)S(1)}, bf16[2048,128]{1,0:T(8,128)(2,1)S(1)}, u32[]{:S(2)}, u32[]{:S(2)}) collective-permute-start(bf16[2048,128]{1,0:T(8,128)(2,1)S(1)} %bitcast.9), channel_id=1, source_target_pairs={{0,2},{1,3},{2,0},{3,1},{4,6},{5,7},{6,4},{7,5}} | collective-permute-start | bytes 1572872 | tf_op jit(solution)/shard_map/ppermute | solution.py:484
  20.9 31.3 %collective-permute-start.3 = (bf16[2048,128]{1,0:T(8,128)(2,1)S(1)}, bf16[2048,128]{1,0:T(8,128)(2,1)}, u32[]{:S(2)}, u32[]{:S(2)}) collective-permute-start(bf16[2048,128]{1,0:T(8,128)(2,1)S(1)} %bitcast.10), channel_id=1, source_target_pairs={{0,1},{1,2},{2,3},{3,0},{4,5},{5,6},{6,7},{7,4}} | collective-permute-start | bytes 1572872 | tf_op jit(solution)/shard_map/ppermute | solution.py:484
  20.9 31.3 %collective-permute-start.2 = (bf16[2048,128]{1,0:T(8,128)(2,1)S(1)}, bf16[2048,128]{1,0:T(8,128)(2,1)}, u32[]{:S(2)}, u32[]{:S(2)}) collective-permute-start(bf16[2048,128]{1,0:T(8,128)(2,1)S(1)} %collective-permute-done.1.refs_2_), channel_id=1, source_target_pairs={{0,1},{1,0},{2,3},{3,2},{4,5},{5,4},{6,7},{7,6}} | collective-permute-start | bytes 1572872 | tf_op jit(solution)/shard_map/ppermute | solution.py:482
  48.4 148.4 %collective-permute-start.13 = (bf16[192,4096]{1,0:T(8,128)(2,1)S(1)}, bf16[192,4096]{1,0:T(8,128)(2,1)S(1)}, u32[]{:S(2)}, u32[]{:S(2)}) collective-permute-start(bf16[192,4096]{1,0:T(8,128)(2,1)S(1)} %constant_dynamic-slice_fusion), channel_id=1, source_target_pairs={{0,4},{4,0},{1,5},{5,1},{2,6},{6,2},{3,7},{7,3}} | collective-permute-start | bytes 4718600 | tf_op jit(solution)/shard_map/ppermute | solution.py:477
  50.4 40.6 %collective-permute-start.6 = (bf16[1024,384]{1,0:T(8,128)(2,1)}, bf16[1024,384]{1,0:T(8,128)(2,1)S(1)}, u32[]{:S(2)}, u32[]{:S(2)}) collective-permute-start(bf16[1024,384]{1,0:T(8,128)(2,1)} %copy-done.2), channel_id=1, source_target_pairs={{3,0},{2,1},{7,4},{6,5}} | collective-permute-start | bytes 2359304 | tf_op jit(solution)/shard_map/ppermute | solution.py:486
  51.9 89.4 %collective-permute-start.14 = (bf16[320,4096]{1,0:T(8,128)(2,1)S(1)}, bf16[320,4096]{1,0:T(8,128)(2,1)}, u32[]{:S(2)}, u32[]{:S(2)}) collective-permute-start(bf16[320,4096]{1,0:T(8,128)(2,1)S(1)} %copy-done.1), channel_id=1, source_target_pairs={{0,4},{4,0},{1,5},{5,1},{2,6},{6,2},{3,7},{7,3}} | collective-permute-start | bytes 7864328 | tf_op jit(solution)/shard_map/ppermute | solution.py:481
  110.6 90.8 %collective-permute-start.7 = (bf16[1024,256]{1,0:T(8,128)(2,1)S(1)}, bf16[1024,256]{1,0:T(8,128)(2,1)S(1)}, u32[]{:S(2)}, u32[]{:S(2)}) collective-permute-start(bf16[1024,256]{1,0:T(8,128)(2,1)S(1)} %attention.6), channel_id=1, source_target_pairs={{0,3},{1,2},{4,7},{5,6}} | collective-permute-start | bytes 1572872 | tf_op jit(solution)/shard_map/ppermute | solution.py:512
  141.3 91.3 %collective-permute-start.18 = (bf16[320,4096]{1,0:T(8,128)(2,1)}, bf16[320,4096]{1,0:T(8,128)(2,1)S(1)}, u32[]{:S(2)}, u32[]{:S(2)}) collective-permute-start(bf16[320,4096]{1,0:T(8,128)(2,1)} %collective-permute-done.14.rest_5_), channel_id=1, source_target_pairs={{0,2},{1,3},{2,0},{3,1},{4,6},{5,7},{6,4},{7,5}} | collective-permute-start | bytes 7864328 | tf_op jit(solution)/shard_map/ppermute | solution.py:503
  177.1 83.6 %collective-permute-start.10 = (bf16[1024,512]{1,0:T(8,128)(2,1)S(1)}, bf16[1024,512]{1,0:T(8,128)(2,1)S(1)}, u32[]{:S(2)}, u32[]{:S(2)}) collective-permute-start(bf16[1024,512]{1,0:T(8,128)(2,1)S(1)} %get-tuple-element.36.rest_1_), channel_id=1, source_target_pairs={{0,4},{4,0},{1,5},{5,1},{2,6},{6,2},{3,7},{7,3}} | collective-permute-start | bytes 3145736 | tf_op jit(solution)/shard_map/ppermute | solution.py:499
  178.7 22.7 %collective-permute-start.8 = (bf16[1024,128]{1,0:T(8,128)(2,1)S(1)}, bf16[1024,128]{1,0:T(8,128)(2,1)S(1)}, u32[]{:S(2)}, u32[]{:S(2)}) collective-permute-start(bf16[1024,128]{1,0:T(8,128)(2,1)S(1)} %get-tuple-element.39), channel_id=1, source_target_pairs={{0,3},{4,7}} | collective-permute-start | bytes 786440 | tf_op jit(solution)/shard_map/ppermute | solution.py:516
  183.8 81.7 %slice-start = ((s8[8388608]{0:T(1024)(128)(4,1)}), s8[4194304]{0:T(1024)(128)(4,1)S(1)}, s32[]{:S(2)}) async-start(s8[8388608]{0:T(1024)(128)(4,1)} %bitcast.6), calls=%async_computation | async-start | bytes 8388608
  196.7 68.8 %slice-start.1 = ((s8[8388608]{0:T(1024)(128)(4,1)}), s8[4194304]{0:T(1024)(128)(4,1)S(1)}, s32[]{:S(2)}) async-start(s8[8388608]{0:T(1024)(128)(4,1)} %bitcast.6), calls=%async_computation.1 | async-start | bytes 8388608
  196.7 36.4 %collective-permute-start.17 = (bf16[192,4096]{1,0:T(8,128)(2,1)S(1)}, bf16[192,4096]{1,0:T(8,128)(2,1)S(1)}, u32[]{:S(2)}, u32[]{:S(2)}) collective-permute-start(bf16[192,4096]{1,0:T(8,128)(2,1)S(1)} %collective-permute-done.13.rest_4_), channel_id=1, source_target_pairs={{0,2},{1,3},{2,0},{3,1},{4,6},{5,7},{6,4},{7,5}} | collective-permute-start | bytes 4718600 | tf_op jit(solution)/shard_map/ppermute | solution.py:503
  226.2 39.3 %collective-permute-start.12 = (bf16[1024,512]{1,0:T(8,128)(2,1)S(1)}, bf16[1024,512]{1,0:T(8,128)(2,1)S(1)}, u32[]{:S(2)}, u32[]{:S(2)}) collective-permute-start(bf16[1024,512]{1,0:T(8,128)(2,1)S(1)} %attention.9.rest_3_), channel_id=1, source_target_pairs={{0,4},{4,0},{1,5},{5,1},{2,6},{6,2},{3,7},{7,3}} | collective-permute-start | bytes 3145736 | tf_op jit(solution)/shard_map/ppermute | solution.py:499
  227.7 65.6 %collective-permute-start.16 = (bf16[320,4096]{1,0:T(8,128)(2,1)}, bf16[320,4096]{1,0:T(8,128)(2,1)S(1)}, u32[]{:S(2)}, u32[]{:S(2)}) collective-permute-start(bf16[320,4096]{1,0:T(8,128)(2,1)} %collective-permute-done.14.rest_5_), channel_id=1, source_target_pairs={{0,1},{1,0},{2,3},{3,2},{4,5},{5,4},{6,7},{7,6}} | collective-permute-start | bytes 7864328 | tf_op jit(solution)/shard_map/ppermute | solution.py:504
  232.6 55.2 %copy-start.5 = (bf16[320,4096]{1,0:T(8,128)(2,1)}, bf16[320,4096]{1,0:T(8,128)(2,1)S(1)}, u32[]{:S(2)}) copy-start(bf16[320,4096]{1,0:T(8,128)(2,1)S(1)} %collective-permute-done.18.rest_9_) | copy-start | bytes 7864324
  232.6 60.7 %collective-permute-start.20 = (bf16[320,4096]{1,0:T(8,128)(2,1)S(1)}, bf16[320,4096]{1,0:T(8,128)(2,1)}, u32[]{:S(2)}, u32[]{:S(2)}) collective-permute-start(bf16[320,4096]{1,0:T(8,128)(2,1)S(1)} %collective-permute-done.18.rest_9_), channel_id=1, source_target_pairs={{0,1},{1,0},{2,3},{3,2},{4,5},{5,4},{6,7},{7,6}} | collective-permute-start | bytes 7864328 | tf_op jit(solution)/shard_map/ppermute | solution.py:507
  233.2 25.3 %collective-permute-start.11 = (bf16[1024,256]{1,0:T(8,128)(2,1)S(1)}, bf16[1024,256]{1,0:T(8,128)(2,1)S(1)}, u32[]{:S(2)}, u32[]{:S(2)}) collective-permute-start(bf16[1024,256]{1,0:T(8,128)(2,1)S(1)} %attention.8.rest_2_), channel_id=1, source_target_pairs={{0,4},{4,0},{1,5},{5,1},{2,6},{6,2},{3,7},{7,3}} | collective-permute-start | bytes 1572872 | tf_op jit(solution)/shard_map/ppermute | solution.py:499
  258.5 34.8 %collective-permute-start.9 = (bf16[1024,768]{1,0:T(8,128)(2,1)S(1)}, bf16[1024,768]{1,0:T(8,128)(2,1)S(1)}, u32[]{:S(2)}, u32[]{:S(2)}) collective-permute-start(bf16[1024,768]{1,0:T(8,128)(2,1)S(1)} %attention.5.rest_0_), channel_id=1, source_target_pairs={{0,4},{4,0},{1,5},{5,1},{2,6},{6,2},{3,7},{7,3}} | collective-permute-start | bytes 4718600 | tf_op jit(solution)/shard_map/ppermute | solution.py:499
  260.8 32.5 %collective-permute-start.15 = (bf16[192,4096]{1,0:T(8,128)(2,1)S(1)}, bf16[192,4096]{1,0:T(8,128)(2,1)S(1)}, u32[]{:S(2)}, u32[]{:S(2)}) collective-permute-start(bf16[192,4096]{1,0:T(8,128)(2,1)S(1)} %collective-permute-done.13.rest_4_), channel_id=1, source_target_pairs={{0,1},{1,0},{2,3},{3,2},{4,5},{5,4},{6,7},{7,6}} | collective-permute-start | bytes 4718600 | tf_op jit(solution)/shard_map/ppermute | solution.py:504
  265.5 27.8 %collective-permute-start.19 = (bf16[192,4096]{1,0:T(8,128)(2,1)S(1)}, bf16[192,4096]{1,0:T(8,128)(2,1)S(1)}, u32[]{:S(2)}, u32[]{:S(2)}) collective-permute-start(bf16[192,4096]{1,0:T(8,128)(2,1)S(1)} %collective-permute-done.17.rest_8_), channel_id=1, source_target_pairs={{0,1},{1,0},{2,3},{3,2},{4,5},{5,4},{6,7},{7,6}} | collective-permute-start | bytes 4718600 | tf_op jit(solution)/shard_map/ppermute | solution.py:507
  (9 other events, 76.0 us)
